TPU v7x, 32 devices: a whole 2x2x4 slice. The times are simulated.
32 devices in a mesh: dp: 8 (over z, core), tensor: 4 (over y, x).
Axes of the slice: x: 2, y: 2, z: 4, core: 2. Of those that a mesh axis runs over, the one named last changes fastest.
Arguments:
- image_in: bfloat16 [8, 896, 1536], P('dp', None, 'tensor'), may hold values from -6 to 6
- text_in: bfloat16 [8, 154, 1536], P('dp', None, 'tensor'), may hold values from -6 to 6
- cond_in: bfloat16 [8, 1536], P(None, 'dp'), may hold values from -6 to 6
- mod_weight: bfloat16 [1, 2, 1536, 6, 1536], P(None, None, 'dp', None, 'tensor'), may hold values from -0.21875 to 0.21875
- mod_bias: bfloat16 [1, 2, 6, 1536], P(None, None, None, 'tensor'), may hold values from -3 to 3
- qkv_weight: bfloat16 [1, 2, 1536, 3, 1536], P(None, None, None, None, 'tensor'), may hold values from -0.15625 to 0.15625
- qkv_bias: bfloat16 [1, 2, 3, 1536], P(None, None, None, 'tensor'), may hold values from -2 to 2
- out_weight: bfloat16 [1, 2, 1536, 1536], P(None, None, None, 'tensor'), may hold values from -0.875 to 0.875
- out_bias: bfloat16 [1, 2, 1536], P(None, None, 'tensor'), may hold values from -2 to 2
- up_weight: bfloat16 [1, 2, 1536, 6144], P(None, None, None, 'tensor'), may hold values from -0.15625 to 0.15625
- up_bias: bfloat16 [1, 2, 6144], P(None, None, 'tensor'), may hold values from -3 to 3
- down_weight: bfloat16 [1, 2, 1536, 6144], P(None, None, None, 'tensor'), may hold values from -0.078125 to 0.078125
- down_bias: bfloat16 [1, 2, 1536], P(None, None, 'tensor'), may hold values from -2 to 2
- image_cot: bfloat16 [8, 896, 1536], P('dp', None, 'tensor'), may hold values from -6 to 6
- text_cot: bfloat16 [8, 154, 1536], P('dp', None, 'tensor'), may hold values from -6 to 6
Outputs:
- image_out: float32 [8, 896, 1536], P('dp', None, 'tensor')
- text_out: float32 [8, 154, 1536], P('dp', None, 'tensor')
- image_grad: float32 [8, 896, 1536], P('dp', None, 'tensor')
- text_grad: float32 [8, 154, 1536], P('dp', None, 'tensor')
- cond_grad: float32 [8, 1536], P(None, 'dp')
- mod_wgrad: float32 [1, 2, 1536, 6, 1536], P(None, None, 'dp', None, 'tensor')
- mod_bgrad: float32 [1, 2, 6, 1536], P(None, None, None, 'tensor')
- qkv_wgrad: float32 [1, 2, 1536, 3, 1536], P(None, None, 'dp', None, 'tensor')
- qkv_bgrad: float32 [1, 2, 3, 1536], P(None, None, None, 'tensor')
- out_wgrad: float32 [1, 2, 1536, 1536], P(None, None, 'dp', 'tensor')
- out_bgrad: float32 [1, 2, 1536], P(None, None, 'tensor')
- up_wgrad: float32 [1, 2, 1536, 6144], P(None, None, 'dp', 'tensor')
- up_bgrad: float32 [1, 2, 6144], P(None, None, 'tensor')
- down_wgrad: float32 [1, 2, 1536, 6144], P(None, None, 'dp', 'tensor')
- down_bgrad: float32 [1, 2, 1536], P(None, None, 'tensor')
All inputs are finite; a program needn't handle non-finite values.
Results may differ from a plain program's by a relative error of at most 0.023.
The roundings to bfloat16 on the way count: a program that leaves them out, or rounds other values in their place, can miss the bound.
Values may be sent and summed in bfloat16 or wider, within the bound.
A program may use at most 320 MiB of HBM per device.

v0:
```python
import jax
import jax.numpy as jnp
from jax import lax
from jax.sharding import PartitionSpec as P

HEAD_DIM = 64


eps_norm = 1e-06


def gelu_tanh(values):
    return jax.nn.gelu(values, approximate=True)


def share_of(whole_row, offset, share_width):
    return lax.dynamic_slice_in_dim(whole_row, offset, share_width, whole_row.ndim - 1)


def norm_forward(shards, shifts, scales):
    saved_norm = []
    gathered = (
        lax.all_gather(shards[0].astype(jnp.bfloat16), "tensor", axis=2, tiled=True).astype(
            jnp.float32
        ),
        lax.all_gather(shards[1].astype(jnp.bfloat16), "tensor", axis=2, tiled=True).astype(
            jnp.float32
        ),
    )
    moddeds = []
    for stream in range(2):
        row_mean = jnp.mean(gathered[stream], axis=-1, keepdims=True)
        centred = gathered[stream] - row_mean
        inv_std = lax.rsqrt(jnp.mean(centred * centred, axis=-1, keepdims=True) + eps_norm)
        normed = centred * inv_std
        moddeds.append(
            (normed * (1.0 + scales[stream][:, None, :]) + shifts[stream][:, None, :]).astype(
                jnp.bfloat16
            )
        )
        saved_norm.append((normed, inv_std))
    return (moddeds, saved_norm)


def norm_backward(partials, saved_norm, scales, offset, share_width):
    results = []
    totals = (
        lax.psum(partials[0].astype(jnp.bfloat16), "tensor").astype(jnp.float32),
        lax.psum(partials[1].astype(jnp.bfloat16), "tensor").astype(jnp.float32),
    )
    for stream in range(2):
        normed, inv_std = saved_norm[stream]
        grad_normed = totals[stream] * (1.0 + scales[stream][:, None, :])
        mean_grad = jnp.mean(grad_normed, axis=-1, keepdims=True)
        mean_cross = jnp.mean(grad_normed * normed, axis=-1, keepdims=True)
        local_total = share_of(totals[stream], offset, share_width)
        local_normed = share_of(normed, offset, share_width)
        local_grad = share_of(grad_normed, offset, share_width)
        results.append(
            (
                inv_std * (local_grad - mean_grad - local_normed * mean_cross),
                jnp.sum(local_total, axis=1),
                jnp.sum(local_total * local_normed, axis=1),
            )
        )
    return results


def reduce_branches(partials):
    return (
        lax.psum_scatter(
            partials[0].astype(jnp.bfloat16), "tensor", scatter_dimension=2, tiled=True
        ).astype(jnp.float32),
        lax.psum_scatter(
            partials[1].astype(jnp.bfloat16), "tensor", scatter_dimension=2, tiled=True
        ).astype(jnp.float32),
    )


def gather_grads(branch_grads):
    return (
        lax.all_gather(branch_grads[0], "tensor", axis=2, tiled=True),
        lax.all_gather(branch_grads[1], "tensor", axis=2, tiled=True),
    )


def attend(joint_qkv, heads_here, score_scale):
    seq_count, tokens = (joint_qkv.shape[0], joint_qkv.shape[1])
    separated = joint_qkv.reshape(seq_count, tokens, 3, heads_here, HEAD_DIM)
    scores = (
        jnp.einsum(
            "sqhd,skhd->shqk",
            separated[:, :, 0],
            separated[:, :, 1],
            preferred_element_type=jnp.float32,
        )
        * score_scale
    )
    highest_score = jnp.max(scores, axis=-1, keepdims=True)
    raised = jnp.exp(scores - highest_score)
    denominator = jnp.sum(raised, axis=-1, keepdims=True)
    weights = (raised / denominator).astype(jnp.bfloat16)
    mixed_heads = jnp.einsum(
        "shqk,skhd->sqhd", weights, separated[:, :, 2], preferred_element_type=jnp.float32
    )
    return (
        mixed_heads.astype(jnp.bfloat16).reshape(seq_count, tokens, heads_here * HEAD_DIM),
        highest_score + jnp.log(denominator),
    )


def attend_back(joint_qkv, log_total, head_grads, heads_here, score_scale):
    seq_count, tokens = (joint_qkv.shape[0], joint_qkv.shape[1])
    separated = joint_qkv.reshape(seq_count, tokens, 3, heads_here, HEAD_DIM)
    queries, keys_all, values = (separated[:, :, 0], separated[:, :, 1], separated[:, :, 2])
    outgrad = head_grads.reshape(seq_count, tokens, heads_here, HEAD_DIM)
    scores = (
        jnp.einsum("sqhd,skhd->shqk", queries, keys_all, preferred_element_type=jnp.float32)
        * score_scale
    )
    weights = jnp.exp(scores - log_total)
    weight_grad = jnp.einsum("sqhd,skhd->shqk", outgrad, values, preferred_element_type=jnp.float32)
    row_dot = jnp.sum(weights * weight_grad, axis=-1, keepdims=True)
    score_grad = (weights * (weight_grad - row_dot)).astype(jnp.bfloat16)
    query_grad = (
        jnp.einsum("shqk,skhd->sqhd", score_grad, keys_all, preferred_element_type=jnp.float32)
        * score_scale
    )
    key_grad = (
        jnp.einsum("shqk,sqhd->skhd", score_grad, queries, preferred_element_type=jnp.float32)
        * score_scale
    )
    value_grad = jnp.einsum(
        "shqk,sqhd->skhd", weights.astype(jnp.bfloat16), outgrad, preferred_element_type=jnp.float32
    )
    stacked = jnp.stack([query_grad, key_grad, value_grad], axis=2)
    return stacked.reshape(seq_count, tokens, 3, heads_here * HEAD_DIM).astype(jnp.bfloat16)


def body(
    image_in,
    text_in,
    cond_in,
    mod_weight,
    mod_bias,
    qkv_weight,
    qkv_bias,
    out_weight,
    out_bias,
    up_weight,
    up_bias,
    down_weight,
    down_bias,
    image_cot,
    text_cot,
):
    share_width = image_in.shape[2]
    offset = lax.axis_index("tensor") * share_width
    heads_here = qkv_weight.shape[4] // HEAD_DIM
    score_scale = HEAD_DIM ** (-0.5)
    image_rows = image_in.shape[1]
    layer_count = qkv_weight.shape[0]
    cond_float = cond_in.astype(jnp.float32)
    cond_act = jax.nn.silu(cond_float).astype(jnp.bfloat16)
    mod_terms = jnp.einsum(
        "sc,lxcjd->slxjd", cond_act, mod_weight, preferred_element_type=jnp.float32
    )
    modulation = lax.psum_scatter(
        mod_terms, "dp", scatter_dimension=0, tiled=True
    ) + mod_bias.astype(jnp.float32)
    mod_view = lax.all_gather(modulation, "tensor", axis=4, tiled=True)
    residual = [image_in.astype(jnp.float32), text_in.astype(jnp.float32)]
    layer_at = 0
    moddeds, first_norm = norm_forward(
        residual,
        [mod_view[:, layer_at, stream, 0] for stream in range(2)],
        [mod_view[:, layer_at, stream, 1] for stream in range(2)],
    )
    projected = [
        (
            jnp.einsum(
                "snd,dje->snje",
                moddeds[stream],
                qkv_weight[layer_at, stream],
                preferred_element_type=jnp.float32,
            )
            + qkv_bias[layer_at, stream]
        ).astype(jnp.bfloat16)
        for stream in range(2)
    ]
    joint_qkv = jnp.concatenate(projected, axis=1)
    attended, log_total = attend(joint_qkv, heads_here, score_scale)
    pieces = [attended[:, :image_rows], attended[:, image_rows:]]
    summed = reduce_branches(
        [
            jnp.einsum(
                "puj,oj->puo",
                pieces[stream],
                out_weight[layer_at, stream],
                preferred_element_type=jnp.float32,
            )
            for stream in range(2)
        ]
    )
    first_branch = [summed[stream] + out_bias[layer_at, stream] for stream in range(2)]
    residual = [
        residual[stream] + modulation[:, layer_at, stream, 2][:, None, :] * first_branch[stream]
        for stream in range(2)
    ]
    second_mod, second_norm = norm_forward(
        residual,
        [mod_view[:, layer_at, stream, 3] for stream in range(2)],
        [mod_view[:, layer_at, stream, 4] for stream in range(2)],
    )
    hidden = [
        jnp.einsum(
            "snd,df->snf",
            second_mod[stream],
            up_weight[layer_at, stream],
            preferred_element_type=jnp.float32,
        )
        + up_bias[layer_at, stream]
        for stream in range(2)
    ]
    activated = [gelu_tanh(hidden[stream]).astype(jnp.bfloat16) for stream in range(2)]
    summed = reduce_branches(
        [
            jnp.einsum(
                "snf,df->snd",
                activated[stream],
                down_weight[layer_at, stream],
                preferred_element_type=jnp.float32,
            )
            for stream in range(2)
        ]
    )
    second_branch = [summed[stream] + down_bias[layer_at, stream] for stream in range(2)]
    residual = [
        residual[stream] + modulation[:, layer_at, stream, 5][:, None, :] * second_branch[stream]
        for stream in range(2)
    ]
    forward_saved = [
        (
            moddeds,
            first_norm,
            joint_qkv,
            attended,
            log_total,
            first_branch,
            second_mod,
            second_norm,
            hidden,
            activated,
            second_branch,
        )
    ]
    gradients = [image_cot.astype(jnp.float32), text_cot.astype(jnp.float32)]
    mod_parts = [None] * layer_count
    weight_parts = [None] * layer_count
    bias_parts = [None] * layer_count
    for layer_at in reversed(range(layer_count)):
        (
            moddeds,
            first_norm,
            joint_qkv,
            attended,
            log_total,
            first_branch,
            second_mod,
            second_norm,
            hidden,
            activated,
            second_branch,
        ) = forward_saved[layer_at]
        second_gate = [
            jnp.sum(second_branch[stream] * gradients[stream], axis=1) for stream in range(2)
        ]
        branch_grads = [
            (modulation[:, layer_at, stream, 5][:, None, :] * gradients[stream]).astype(
                jnp.bfloat16
            )
            for stream in range(2)
        ]
        down_bias_grad = [
            jnp.sum(branch_grads[stream].astype(jnp.float32), axis=(0, 1)) for stream in range(2)
        ]
        whole_grads = gather_grads(branch_grads)
        down_grad = [
            jnp.einsum(
                "snd,snf->df",
                whole_grads[stream],
                activated[stream],
                preferred_element_type=jnp.float32,
            )
            for stream in range(2)
        ]
        act_grad = [
            jnp.einsum(
                "snd,df->snf",
                whole_grads[stream],
                down_weight[layer_at, stream],
                preferred_element_type=jnp.float32,
            )
            for stream in range(2)
        ]
        hidden_grad = [
            jax.vjp(gelu_tanh, hidden[stream])[1](act_grad[stream])[0].astype(jnp.bfloat16)
            for stream in range(2)
        ]
        up_bias_grad = [
            jnp.sum(hidden_grad[stream].astype(jnp.float32), axis=(0, 1)) for stream in range(2)
        ]
        up_grad = [
            jnp.einsum(
                "snd,snf->df",
                second_mod[stream],
                hidden_grad[stream],
                preferred_element_type=jnp.float32,
            )
            for stream in range(2)
        ]
        norm_partials = [
            jnp.einsum(
                "snf,df->snd",
                hidden_grad[stream],
                up_weight[layer_at, stream],
                preferred_element_type=jnp.float32,
            )
            for stream in range(2)
        ]
        second_back = norm_backward(
            norm_partials,
            second_norm,
            [mod_view[:, layer_at, stream, 4] for stream in range(2)],
            offset,
            share_width,
        )
        gradients = [gradients[stream] + second_back[stream][0] for stream in range(2)]
        first_gate = [
            jnp.sum(first_branch[stream] * gradients[stream], axis=1) for stream in range(2)
        ]
        branch_grads = [
            (modulation[:, layer_at, stream, 2][:, None, :] * gradients[stream]).astype(
                jnp.bfloat16
            )
            for stream in range(2)
        ]
        out_bias_grad = [
            jnp.sum(branch_grads[stream].astype(jnp.float32), axis=(0, 1)) for stream in range(2)
        ]
        whole_grads = gather_grads(branch_grads)
        pieces = [attended[:, :image_rows], attended[:, image_rows:]]
        out_grad = [
            jnp.einsum(
                "kux,kut->xt",
                whole_grads[stream],
                pieces[stream],
                preferred_element_type=jnp.float32,
            )
            for stream in range(2)
        ]
        head_grads = jnp.concatenate(
            [
                jnp.einsum(
                    "hom,mr->hor",
                    whole_grads[stream],
                    out_weight[layer_at, stream],
                    preferred_element_type=jnp.float32,
                )
                for stream in range(2)
            ],
            axis=1,
        ).astype(jnp.bfloat16)
        joint_grad = attend_back(joint_qkv, log_total, head_grads, heads_here, score_scale)
        stream_grads = [joint_grad[:, :image_rows], joint_grad[:, image_rows:]]
        qkv_bias_grad = [
            jnp.sum(stream_grads[stream].astype(jnp.float32), axis=(0, 1)) for stream in range(2)
        ]
        qkv_grad = [
            jnp.einsum(
                "snd,snje->dje",
                moddeds[stream],
                stream_grads[stream],
                preferred_element_type=jnp.float32,
            )
            for stream in range(2)
        ]
        norm_partials = [
            jnp.einsum(
                "snje,dje->snd",
                stream_grads[stream],
                qkv_weight[layer_at, stream],
                preferred_element_type=jnp.float32,
            )
            for stream in range(2)
        ]
        first_back = norm_backward(
            norm_partials,
            first_norm,
            [mod_view[:, layer_at, stream, 1] for stream in range(2)],
            offset,
            share_width,
        )
        gradients = [gradients[stream] + first_back[stream][0] for stream in range(2)]
        mod_parts[layer_at] = jnp.stack(
            [
                jnp.stack(
                    [
                        first_back[stream][1],
                        first_back[stream][2],
                        first_gate[stream],
                        second_back[stream][1],
                        second_back[stream][2],
                        second_gate[stream],
                    ],
                    axis=1,
                )
                for stream in range(2)
            ],
            axis=1,
        )
        bias_parts[layer_at] = (
            jnp.stack(qkv_bias_grad, axis=0),
            jnp.stack(out_bias_grad, axis=0),
            jnp.stack(up_bias_grad, axis=0),
            jnp.stack(down_bias_grad, axis=0),
        )
        weight_parts[layer_at] = (
            jnp.stack(qkv_grad, axis=0),
            jnp.stack(out_grad, axis=0),
            jnp.stack(up_grad, axis=0),
            jnp.stack(down_grad, axis=0),
        )
    reduced = (
        lax.psum_scatter(
            jnp.stack([weight_parts[0][0]], axis=0).astype(jnp.bfloat16),
            "dp",
            scatter_dimension=2,
            tiled=True,
        ).astype(jnp.float32),
        lax.psum_scatter(
            jnp.stack([weight_parts[0][1]], axis=0).astype(jnp.bfloat16),
            "dp",
            scatter_dimension=2,
            tiled=True,
        ).astype(jnp.float32),
        lax.psum_scatter(
            jnp.stack([weight_parts[0][2]], axis=0).astype(jnp.bfloat16),
            "dp",
            scatter_dimension=2,
            tiled=True,
        ).astype(jnp.float32),
        lax.psum_scatter(
            jnp.stack([weight_parts[0][3]], axis=0).astype(jnp.bfloat16),
            "dp",
            scatter_dimension=2,
            tiled=True,
        ).astype(jnp.float32),
    )
    bias_totals = lax.psum(
        (
            jnp.stack([bias_parts[0][0]], axis=0),
            jnp.stack([bias_parts[0][1]], axis=0),
            jnp.stack([bias_parts[0][2]], axis=0),
            jnp.stack([bias_parts[0][3]], axis=0),
        ),
        "dp",
    )
    mod_grad = jnp.stack(mod_parts, axis=1).astype(jnp.bfloat16)
    all_mod = lax.all_gather(mod_grad, "dp", axis=0, tiled=True)
    mod_wgrad = jnp.einsum("sc,slxjd->lxcjd", cond_act, all_mod, preferred_element_type=jnp.float32)
    mod_bgrad = jnp.sum(all_mod.astype(jnp.float32), axis=0)
    act_partial = jnp.einsum(
        "slxjd,lxcjd->sc", all_mod, mod_weight, preferred_element_type=jnp.float32
    )
    act_total = lax.psum(act_partial, "tensor")
    cond_grad = jax.vjp(jax.nn.silu, cond_float)[1](act_total)[0]
    return (
        residual[0],
        residual[1],
        gradients[0],
        gradients[1],
        cond_grad,
        mod_wgrad,
        mod_bgrad,
        reduced[0],
        bias_totals[0],
        reduced[1],
        bias_totals[1],
        reduced[2],
        bias_totals[2],
        reduced[3],
        bias_totals[3],
    )


def solution(mesh):
    return jax.shard_map(
        body,
        mesh=mesh,
        in_specs=(
            P("dp", None, "tensor"),
            P("dp", None, "tensor"),
            P(None, "dp"),
            P(None, None, "dp", None, "tensor"),
            P(None, None, None, "tensor"),
            P(None, None, None, None, "tensor"),
            P(None, None, None, "tensor"),
            P(None, None, None, "tensor"),
            P(None, None, "tensor"),
            P(None, None, None, "tensor"),
            P(None, None, "tensor"),
            P(None, None, None, "tensor"),
            P(None, None, "tensor"),
            P("dp", None, "tensor"),
            P("dp", None, "tensor"),
        ),
        out_specs=(
            P("dp", None, "tensor"),
            P("dp", None, "tensor"),
            P("dp", None, "tensor"),
            P("dp", None, "tensor"),
            P(None, "dp"),
            P(None, None, "dp", None, "tensor"),
            P(None, None, None, "tensor"),
            P(None, None, "dp", None, "tensor"),
            P(None, None, None, "tensor"),
            P(None, None, "dp", "tensor"),
            P(None, None, "tensor"),
            P(None, None, "dp", "tensor"),
            P(None, None, "tensor"),
            P(None, None, "dp", "tensor"),
            P(None, None, "tensor"),
        ),
        check_vma=False,
    )
```

profile of v0, /device:TPU:0, one launch (start us, length us, event | category | flops | bytes accessed | tf_op | source)
XLA Modules:
  0.0 1017.5 jit_solution(17720880857674907446)
XLA Ops:
  14.0 13.0 %all_gather.32 = bf16[1,154,1536]{2,1,0:T(8,128)(2,1)S(1)} all-gather(bf16[1,154,384]{2,1,0:T(8,128)(2,1)} %param.16), channel_id=1, replica_groups=mesh['dp'=8,'tensor'=4] {'tensor'}, dimensions={2}, use_global_device_ids=true | all-gather | bytes 591360 | tf_op jit(solution)/shard_map/all_gather | solution.py:26
  27.4 39.8 %all-reduce.8.cloned.1.call-done = f32[8,1,2,6,384]{4,2,3,1,0:T(2,128)} async-done(((f32[8,1,2,6,384]{4,2,3,1,0:T(2,128)}), f32[8,1,2,6,384]{4,2,3,1,0:T(2,128)}) %all-reduce.8.cloned.1.call-update) | async-done | bytes 147472
  68.6 8.5 all_gather.31
  86.6 6.3 add_convert_fusion.2
  92.9 12.1 %fusion.227 = (f32[6,1050]{1,0:T(8,128)S(1)}, f32[6,1050,1050]{1,2,0:T(8,128)}) fusion(bf16[1,154,3,6,64]{1,4,3,2,0:T(8,128)(2,1)S(1)} %bitcast.318, bf16[1,896,3,6,64]{1,4,3,2,0:T(8,128)(2,1)S(1)} %bitcast.311), kind=kOutput, calls=%fused_computation.315 | convolution fusion | flops 863169280 | bytes 31793616 | tf_op jit(solution)/shard_map/sqhd,skhd->shqk/dot_general | solution.py:91
  105.1 11.8 %fusion = f32[6,1050]{1,0:T(8,128)S(1)} fusion(f32[6,1050,1050]{1,2,0:T(8,128)} %get-tuple-element.141, f32[6,1050]{1,0:T(8,128)S(1)} %get-tuple-element.140), kind=kLoop, calls=%fused_computation.6 | loop fusion | flops 13223700 | bytes 26510400 | tf_op jit(solution)/shard_map/reduce_sum | solution.py:101
  116.9 12.0 %fusion.78 = bf16[6,64,1050]{2,1,0:T(8,128)(2,1)S(1)} fusion(f32[6,1050,1050]{1,2,0:T(8,128)} %get-tuple-element.141, f32[6,1050]{1,0:T(8,128)S(1)} %fusion, f32[6,1050]{1,0:T(8,128)S(1)} %get-tuple-element.140, bf16[1,896,3,6,64]{1,4,3,2,0:T(8,128)(2,1)S(1)} %bitcast.312, bf16[1,154,3,6,64]{1,4,3,2,0:T(8,128)(2,1)S(1)} %bitcast.319), kind=kOutput, calls=%fused_computation.100 | convolution fusion | flops 868580992 | bytes 29736000 | tf_op jit(solution)/shard_map/shqk,skhd->sqhd/dot_general | solution.py:103
  133.1 14.1 %copy.97 = bf16[1,896,1536]{1,0,2:T(2,128)(2,1)} copy(bf16[1,896,1536]{2,1,0:T(8,128)(2,1)} %fusion.73) | data formatting | bytes 5505024
  147.2 4.5 copy.127
  160.1 33.0 %reduce-scatter.25.cloned.1.call-done = bf16[384,896]{1,0:T(8,128)(2,1)} async-done(((bf16[1536,896]{1,0:T(8,128)(2,1)}), bf16[384,896]{1,0:T(8,128)(2,1)}) %reduce-scatter.25.cloned.1.call-update) | async-done | bytes 688144
  196.0 4.6 copy.98
  204.4 12.5 %all_gather.37 = bf16[1,154,1536]{2,1,0:T(8,128)(2,1)} all-gather(bf16[1,154,384]{2,1,0:T(8,128)(2,1)S(1)} %get-tuple-element.105), channel_id=1, replica_groups=mesh['dp'=8,'tensor'=4] {'tensor'}, dimensions={2}, use_global_device_ids=true | all-gather | bytes 591360 | tf_op jit(solution)/shard_map/all_gather | solution.py:83
  218.6 5.0 reduce-scatter.29.cloned.1.call-done
  226.9 13.8 %all_gather.34 = bf16[1,154,1536]{2,1,0:T(8,128)(2,1)S(1)} all-gather(bf16[1,154,384]{2,1,0:T(8,128)(2,1)S(1)} %fusion.186), channel_id=1, replica_groups=mesh['dp'=8,'tensor'=4] {'tensor'}, dimensions={2}, use_global_device_ids=true | all-gather | bytes 591360 | tf_op jit(solution)/shard_map/all_gather | solution.py:26
  244.6 5.0 convert_reduce_fusion.8
  252.9 14.7 %all-gather.8.cloned.1.call-done = bf16[1,896,1536]{2,1,0:T(8,128)(2,1)} async-done(((bf16[1,896,384]{2,1,0:T(8,128)(2,1)}), bf16[1,896,1536]{2,1,0:T(8,128)(2,1)}) %all-gather.8.cloned.1.call-update) | async-done | bytes 2752528 | tf_op jit(solution)/shard_map/all_gather | solution.py:23
  272.6 8.9 fusion.39
  281.5 28.9 %all-gather.10.cloned.1.call-done = bf16[1,896,1536]{2,1,0:T(8,128)(2,1)} async-done(((bf16[1,896,384]{2,1,0:T(8,128)(2,1)}), bf16[1,896,1536]{2,1,0:T(8,128)(2,1)}) %all-gather.10.cloned.1.call-update) | async-done | bytes 2752528 | tf_op jit(solution)/shard_map/all_gather | solution.py:82
  310.4 11.4 %convert_reduce_fusion.2 = (f32[1536]{0:T(1024)}, bf16[896,1536]{1,0:T(8,128)(2,1)S(1)}) fusion(f32[896,1536]{1,0:T(8,128)} %fusion.39, f32[1536]{0:T(1024)} %get-tuple-element.89, bf16[1,2,1536,1536]{3,2,1,0:T(8,128)(2,1)} %param.26, bf16[1,896,1536]{2,1,0:T(8,128)(2,1)} %all-gather.10.cloned.1.call-done), kind=kOutput, calls=%fused_computation.42 | convolution fusion | flops 4259510784 | bytes 15742976 | tf_op jit(solution)/shard_map/snd,df->snf/dot_general | solution.py:298
  323.4 8.2 fusion.67
  331.8 88.3 %all-reduce.12.cloned.1.call-done = (bf16[1,896,1536]{2,1,0:T(8,128)(2,1)}, bf16[1,154,1536]{2,1,0:T(8,128)(2,1)}) async-done(((bf16[1,896,1536]{2,1,0:T(8,128)(2,1)}, bf16[1,154,1536]{2,1,0:T(8,128)(2,1)}), (bf16[1,896,1536]{2,1,0:T(8,128)(2,1)}, bf16[1,154,1536]{2,1,0:T(8,128)(2,1)})) %all-reduce.12.cloned.1.call-update) | async-done | bytes 3225616 | tf_op jit(solution)/shard_map/psum | solution.py:48
  420.2 5.1 convert_element_type.339
  427.3 4.0 multiply_reduce_fusion.3
  440.0 4.4 fusion.111
  449.9 10.5 %fusion.64 = bf16[1,896,1536]{2,1,0:T(8,128)(2,1)} fusion(bf16[1,2,1536,1536]{3,2,1,0:T(8,128)(2,1)} %param.26, f32[896,1536]{1,0:T(8,128)} %fusion.39, f32[1536]{0:T(1024)S(1)} %copy-done.83), kind=kOutput, calls=%fused_computation.92 | convolution fusion | flops 4242997248 | bytes 12982272 | tf_op jit(solution)/shard_map/snf,df->snd/dot_general | solution.py:228
  460.4 14.1 %copy.99 = bf16[1,896,1536]{1,0,2:T(2,128)(2,1)} copy(bf16[1,896,1536]{2,1,0:T(8,128)(2,1)} %fusion.64) | data formatting | bytes 5505024
  474.5 4.6 copy.126
  481.4 12.6 %all_gather.38 = bf16[1,154,1536]{2,1,0:T(8,128)(2,1)S(1)} all-gather(bf16[1,154,384]{2,1,0:T(8,128)(2,1)S(1)} %get-tuple-element.126), channel_id=1, replica_groups=mesh['dp'=8,'tensor'=4] {'tensor'}, dimensions={2}, use_global_device_ids=true | all-gather | bytes 591360 | tf_op jit(solution)/shard_map/all_gather | solution.py:83
  499.6 22.8 %multiply_reduce_fusion = (f32[6,1050]{1,0:T(8,128)}, f32[6,1050,1050]{1,2,0:T(8,128)}) fusion(f32[6,1050,1050]{1,2,0:T(8,128)} %get-tuple-element.141, f32[6,1050]{1,0:T(8,128)S(1)} %copy-done.21, bf16[1,896,3,6,64]{1,4,3,2,0:T(8,128)(2,1)S(1)} %bitcast.315, bf16[1,154,3,6,64]{1,4,3,2,0:T(8,128)(2,1)S(1)} %bitcast.320, ...), kind=kOutput, calls=%fused_computation.2 | convolution fusion | flops 869784256 | bytes 56196000 | tf_op jit(solution)/shard_map/sqhd,skhd->shqk/dot_general | solution.py:122
  522.4 25.2 %multiply_convert_fusion = bf16[6,1050,1050]{1,2,0:T(8,128)(2,1)} fusion(f32[6,1050,1050]{1,2,0:T(8,128)} %get-tuple-element.143, f32[6,1050,1050]{1,2,0:T(8,128)} %get-tuple-element.141, f32[6,1050]{1,0:T(8,128)} %get-tuple-element.142, f32[6,1050]{1,0:T(8,128)} %log_add_fusion), kind=kLoop, calls=%fused_computation.1 | loop fusion | flops 26460000 | bytes 66200400 | tf_op jit(solution)/shard_map/convert_element_type | solution.py:124
  547.6 12.6 %fusion.81 = bf16[6,64,1050]{2,1,0:T(8,128)(2,1)} fusion(f32[6,1050,1050]{1,2,0:T(8,128)} %get-tuple-element.141, f32[6,1050]{1,0:T(8,128)} %log_add_fusion, bf16[154,6,64]{0,2,1:T(8,128)(2,1)} %convolution_convert_fusion.10, bf16[896,6,64]{0,2,1:T(8,128)(2,1)S(1)} %fusion.132), kind=kOutput, calls=%fused_computation.105 | convolution fusion | flops 861966016 | bytes 28098000 | tf_op jit(solution)/shard_map/shqk,sqhd->skhd/dot_general | solution.py:133
  562.4 8.7 fusion.79
  573.3 10.7 %fusion.80 = bf16[6,64,1050]{2,1,0:T(8,128)(2,1)} fusion(bf16[6,1050,1050]{1,2,0:T(8,128)(2,1)} %multiply_convert_fusion, bf16[1,896,3,6,64]{1,4,3,2,0:T(8,128)(2,1)} %bitcast.314, bf16[1,154,3,6,64]{1,4,3,2,0:T(8,128)(2,1)S(1)} %bitcast.322), kind=kOutput, calls=%fused_computation.103 | convolution fusion | flops 849139200 | bytes 16455600 | tf_op jit(solution)/shard_map/shqk,sqhd->skhd/dot_general | solution.py:130
  589.6 5.0 fusion.117
  594.6 5.3 fusion.70
  607.0 5.1 fusion.11
  612.1 10.0 fusion.13
  622.1 8.3 pad_maximum_fusion.1
  635.8 7.5 fusion.12
  643.4 8.5 pad_maximum_fusion
  654.3 6.9 fusion.62
  671.0 4.8 copy.100
  677.7 27.3 %all-reduce.1 = (f32[1,2,3,384]{3,1,2,0:T(2,128)}, f32[1,2,384]{2,1,0:T(2,128)}, f32[1,2,1536]{2,1,0:T(2,128)}, f32[1,2,384]{2,1,0:T(2,128)}) all-reduce(f32[1,2,3,384]{3,1,2,0:T(2,128)S(1)} %maximum_bitcast_fusion.1, f32[1,2,384]{2,1,0:T(2,128)S(1)} %maximum_bitcast_fusion.2, ...), channel_id=1, replica_groups=mesh['dp'=8,'tensor'=4] {'dp'}, use_global_device_ids=true, to_apply=%region_45.46 | all-reduce | flops 6912 | bytes 55296 | tf_op jit(solution)/shard_map/psum | solution.py:460
  719.2 14.0 %all-gather = bf16[8,2,6,384]{3,1,2,0:T(2,128)(2,1)S(1)} all-gather(bf16[1,2,6,384]{3,1,2,0:T(2,128)(2,1)S(1)} %copy.81), channel_id=2, replica_groups=mesh['dp'=8,'tensor'=4] {'dp'}, dimensions={0}, use_global_device_ids=true | all-gather | bytes 82944 | tf_op jit(solution)/shard_map/all_gather | solution.py:470
  733.8 9.4 psum.67
  748.8 80.3 %reduce-scatter.23.cloned.1.call-done = bf16[1,2,192,1536]{3,2,1,0:T(8,128)(2,1)} async-done(((bf16[1,2,1536,1536]{3,2,1,0:T(8,128)(2,1)}), bf16[1,2,192,1536]{3,2,1,0:T(8,128)(2,1)}) %reduce-scatter.23.cloned.1.call-update) | async-done | bytes 1179664 | tf_op jit(solution)/shard_map/reduce_scatter | solution.py:453
  832.0 97.1 %reduce-scatter.21.cloned.1.call-done = bf16[1,2,192,1536]{3,2,1,0:T(8,128)(2,1)} async-done(((bf16[1,2,1536,1536]{3,2,1,0:T(8,128)(2,1)}), bf16[1,2,192,1536]{3,2,1,0:T(8,128)(2,1)}) %reduce-scatter.21.cloned.1.call-update) | async-done | bytes 1179664 | tf_op jit(solution)/shard_map/reduce_scatter | solution.py:447
  932.1 74.9 %reduce-scatter.17.cloned.1.call-done = bf16[1,2,192,3,384]{4,2,3,1,0:T(8,128)(2,1)} async-done(((bf16[1,2,1536,3,384]{4,2,3,1,0:T(8,128)(2,1)}), bf16[1,2,192,3,384]{4,2,3,1,0:T(8,128)(2,1)}) %reduce-scatter.17.cloned.1.call-update) | async-done | bytes 884752 | tf_op jit(solution)/shard_map/reduce_scatter | solution.py:435
  (366 shorter events, 143.9 us)
Async XLA Ops:
  8.0 59.2 %copy-start.71 = (bf16[1,2,6,384]{3,1,2,0:T(2,128)(2,1)S(1)}, bf16[1,2,6,384]{3,1,2,0:T(2,128)(2,1)}, u32[]{:S(2)}) copy-start(bf16[1,2,6,384]{3,1,2,0:T(2,128)(2,1)} %param.19) | copy-start | bytes 27652
  8.0 59.2 %all-reduce.8.cloned.1.call-start = ((), (), s32[]{:S(2)}) async-start(), calls=%async_computation.20 | async-start | bytes 294912
  11.3 70.3 %all-gather.6.cloned.1.call-start = ((), (), s32[]{:S(2)}) async-start(), calls=%async_computation.8 | async-start | bytes 3440640 | tf_op jit(solution)/shard_map/all_gather | solution.py:23
  11.9 181.3 %reduce-scatter.25.cloned.1.call-start = ((), (), s32[]{:S(2)}) async-start(), calls=%async_computation.16 | async-start | bytes 3440640
  26.9 50.9 %copy-start.8 = (bf16[1,154,1536]{2,1,0:T(8,128)(2,1)}, bf16[1,154,1536]{2,1,0:T(8,128)(2,1)S(1)}, u32[]{:S(2)}) copy-start(bf16[1,154,1536]{2,1,0:T(8,128)(2,1)S(1)} %all_gather.32) | copy-start | bytes 1419268
  27.1 50.8 %copy-start.67 = (f32[154]{0:T(256)}, f32[154]{0:T(256)S(1)}, u32[]{:S(2)}) copy-start(f32[154]{0:T(256)S(1)} %broadcast_multiply_fusion.15) | copy-start | bytes 1852
  27.4 50.5 %copy-start.65 = (f32[154]{0:T(256)}, f32[154]{0:T(256)S(1)}, u32[]{:S(2)}) copy-start(f32[154]{0:T(256)S(1)} %add_rsqrt_fusion.3) | copy-start | bytes 1852
  68.6 9.2 copy-start.37
  77.8 8.8 copy-start.47
  77.8 8.8 copy-start.79
  77.8 163.3 %copy-start.53 = (f32[1536]{0:T(1024)}, f32[1536]{0:T(1024)S(1)}, u32[]{:S(2)}) copy-start(f32[1536]{0:T(1024)S(1)} %get-tuple-element.76) | copy-start | bytes 18436
  83.9 9.0 copy-start.42
  92.9 24.0 %copy-start.1 = (bf16[896,3,384]{0,2,1:T(8,128)(2,1)}, bf16[896,3,384]{0,2,1:T(8,128)(2,1)S(1)}, u32[]{:S(2)}) copy-start(bf16[896,3,384]{0,2,1:T(8,128)(2,1)S(1)} %add_convert_fusion.2) | copy-start | bytes 6193156
  105.1 11.8 %copy-start.32 = (f32[6,1050]{1,0:T(8,128)}, f32[6,1050]{1,0:T(8,128)S(1)}, u32[]{:S(2)}) copy-start(f32[6,1050]{1,0:T(8,128)S(1)} %get-tuple-element.140) | copy-start | bytes 75604
  116.9 12.1 %copy-start.35 = (f32[6,1050]{1,0:T(8,128)}, f32[6,1050]{1,0:T(8,128)S(1)}, u32[]{:S(2)}) copy-start(f32[6,1050]{1,0:T(8,128)S(1)} %fusion) | copy-start | bytes 75604
  116.9 13.0 %copy-start.17 = (bf16[1,2,1536,384]{3,2,1,0:T(8,128)(2,1)S(1)}, bf16[1,2,1536,384]{3,2,1,0:T(8,128)(2,1)}, u32[]{:S(2)}) copy-start(bf16[1,2,1536,384]{3,2,1,0:T(8,128)(2,1)} %param.22) | copy-start | bytes 7077892
  151.8 71.9 %reduce-scatter.29.cloned.1.call-start = ((), (), s32[]{:S(2)}) async-start(), calls=%async_computation.18 | async-start | bytes 983040
  156.6 46.5 %copy-start.56 = (bf16[1,2,1536]{2,1,0:T(2,128)(2,1)S(1)}, bf16[1,2,1536]{2,1,0:T(2,128)(2,1)}, u32[]{:S(2)}) copy-start(bf16[1,2,1536]{2,1,0:T(2,128)(2,1)} %param.25) | copy-start | bytes 18436
  156.6 47.2 %copy-start.25 = (bf16[1,154,384]{2,1,0:T(8,128)(2,1)S(1)}, bf16[1,154,384]{2,1,0:T(8,128)(2,1)}, u32[]{:S(2)}) copy-start(bf16[1,154,384]{2,1,0:T(8,128)(2,1)} %param.29) | copy-start | bytes 354820
  159.1 57.8 %copy-start.13 = (bf16[1,896,384]{2,1,0:T(8,128)(2,1)S(1)}, bf16[1,896,384]{2,1,0:T(8,128)(2,1)}, u32[]{:S(2)}) copy-start(bf16[1,896,384]{2,1,0:T(8,128)(2,1)} %param.28) | copy-start | bytes 2064388
  159.1 108.5 %all-gather.8.cloned.1.call-start = ((), (), s32[]{:S(2)}) async-start(), calls=%async_computation.9 | async-start | bytes 3440640 | tf_op jit(solution)/shard_map/all_gather | solution.py:23
  159.2 59.3 %copy-start.63 = (f32[384]{0:T(512)}, f32[384]{0:T(512)S(1)}, u32[]{:S(2)}) copy-start(f32[384]{0:T(512)S(1)} %get-tuple-element.93) | copy-start | bytes 4612
  159.2 66.7 %copy-start.59 = (f32[384]{0:T(512)}, f32[384]{0:T(512)S(1)}, u32[]{:S(2)}) copy-start(f32[384]{0:T(512)S(1)} %get-tuple-element.92) | copy-start | bytes 4612
  160.1 58.5 %copy-start.57 = (f32[384]{0:T(512)}, f32[384]{0:T(512)S(1)}, u32[]{:S(2)}) copy-start(f32[384]{0:T(512)S(1)} %get-tuple-element.86) | copy-start | bytes 4612
  160.1 58.5 %copy-start.61 = (f32[384]{0:T(512)}, f32[384]{0:T(512)S(1)}, u32[]{:S(2)}) copy-start(f32[384]{0:T(512)S(1)} %get-tuple-element.84) | copy-start | bytes 4612
  160.1 267.2 %copy-start.45 = (f32[384]{0:T(512)}, f32[384]{0:T(512)S(1)}, u32[]{:S(2)}) copy-start(f32[384]{0:T(512)S(1)} %get-tuple-element.87) | copy-start | bytes 4612
  203.1 107.3 %all-gather.10.cloned.1.call-start = ((), (), s32[]{:S(2)}) async-start(), calls=%async_computation.10 | async-start | bytes 3440640 | tf_op jit(solution)/shard_map/all_gather | solution.py:82
  218.5 201.6 %all-reduce.12.cloned.1.call-start = ((), (), s32[]{:S(2)}) async-start(), calls=%async_computation.22 | async-start | bytes 6488064 | tf_op jit(solution)/shard_map/psum | solution.py:48
  240.8 8.9 copy-start.69
  241.1 8.6 copy-start.72
  241.1 9.4 slice-start
  241.1 9.3 slice-start.1
  331.6 164.3 %all-gather.12.cloned.1.call-start = ((), (), s32[]{:S(2)}) async-start(), calls=%async_computation.11 | async-start | bytes 3440640 | tf_op jit(solution)/shard_map/all_gather | solution.py:82
  431.3 234.4 %reduce-scatter.31.cloned.1.call-start = ((), (), s32[]{:S(2)}) async-start(), calls=%async_computation.19 | async-start | bytes 983040
  449.8 218.2 %reduce-scatter.27.cloned.1.call-start = ((), (), s32[]{:S(2)}) async-start(), calls=%async_computation.17 | async-start | bytes 3440640
  479.1 225.9 %all-reduce.10.cloned.1.call-start = ((), (), s32[]{:S(2)}) async-start(), calls=%async_computation.21 | async-start | bytes 6488064 | tf_op jit(solution)/shard_map/psum | solution.py:48
  479.1 15.6 %copy-start.22 = (bf16[384,1536]{1,0:T(8,128)(2,1)S(1)}, bf16[384,1536]{1,0:T(8,128)(2,1)}, u32[]{:S(2)}) copy-start(bf16[384,1536]{1,0:T(8,128)(2,1)} %copy.73) | copy-start | bytes 3538948
  599.9 147.1 %reduce-scatter.19.cloned.1.call-start = ((), (), s32[]{:S(2)}) async-start(), calls=%async_computation.13 | async-start | bytes 2654208 | tf_op jit(solution)/shard_map/reduce_scatter | solution.py:441
  607.0 222.1 %reduce-scatter.23.cloned.1.call-start = ((), (), s32[]{:S(2)}) async-start(), calls=%async_computation.15 | async-start | bytes 10616832 | tf_op jit(solution)/shard_map/reduce_scatter | solution.py:453
  630.5 298.6 %reduce-scatter.21.cloned.1.call-start = ((), (), s32[]{:S(2)}) async-start(), calls=%async_computation.14 | async-start | bytes 10616832 | tf_op jit(solution)/shard_map/reduce_scatter | solution.py:447
  651.9 355.0 %reduce-scatter.17.cloned.1.call-start = ((), (), s32[]{:S(2)}) async-start(), calls=%async_computation.12 | async-start | bytes 7962624 | tf_op jit(solution)/shard_map/reduce_scatter | solution.py:435
  670.9 36.7 %copy-start.23 = (bf16[1,154,384]{2,1,0:T(8,128)(2,1)S(1)}, bf16[1,154,384]{2,1,0:T(8,128)(2,1)}, u32[]{:S(2)}) copy-start(bf16[1,154,384]{2,1,0:T(8,128)(2,1)} %param.16) | copy-start | bytes 354820
  670.9 36.7 %copy-start.24 = (bf16[1,154,384]{2,1,0:T(8,128)(2,1)S(1)}, bf16[1,154,384]{2,1,0:T(8,128)(2,1)}, u32[]{:S(2)}) copy-start(bf16[1,154,384]{2,1,0:T(8,128)(2,1)} %copy.102) | copy-start | bytes 354820
  670.9 36.7 %copy-start.27 = (bf16[1,154,384]{2,1,0:T(8,128)(2,1)S(1)}, bf16[1,154,384]{2,1,0:T(8,128)(2,1)}, u32[]{:S(2)}) copy-start(bf16[1,154,384]{2,1,0:T(8,128)(2,1)} %param.29) | copy-start | bytes 354820
  670.9 36.7 %copy-start.28 = (f32[1,154,384]{2,1,0:T(8,128)S(1)}, f32[1,154,384]{2,1,0:T(8,128)}, u32[]{:S(2)}) copy-start(f32[1,154,384]{2,1,0:T(8,128)} %get-tuple-element.127) | copy-start | bytes 709636
  670.9 36.7 %copy-start.60 = (f32[384]{0:T(512)S(1)}, f32[384]{0:T(512)}, u32[]{:S(2)}) copy-start(f32[384]{0:T(512)} %copy-done.59) | copy-start | bytes 4612
  671.0 36.7 %copy-start.62 = (f32[384]{0:T(512)S(1)}, f32[384]{0:T(512)}, u32[]{:S(2)}) copy-start(f32[384]{0:T(512)} %copy-done.61) | copy-start | bytes 4612
  715.2 28.7 %copy-start.44 = (bf16[8,192]{1,0:T(8,128)(2,1)S(1)}, bf16[8,192]{1,0:T(8,128)(2,1)}, u32[]{:S(2)}) copy-start(bf16[8,192]{1,0:T(8,128)(2,1)} %param.17) | copy-start | bytes 9220
  (71 other events, 232.5 us)
Sparse Core Ops, SparseCore 0:
  11.7 55.4 all-reduce.7
Sparse Core Ops, SparseCore 1:
  13.6 43.0 all-gather.5
  151.9 41.2 reduce-scatter.24
  196.5 27.1 reduce-scatter.28
  226.0 41.5 all-gather.7
  270.0 40.3 all-gather.9
  331.7 88.5 all-reduce.11
  431.3 40.3 all-gather.11
  474.5 26.7 reduce-scatter.30
  504.1 40.5 reduce-scatter.26
  600.0 88.8 all-reduce.9
  691.6 37.0 reduce-scatter.18
  731.1 97.9 reduce-scatter.22
  831.2 97.8 reduce-scatter.20
  931.4 75.5 reduce-scatter.16
where the time goes:
time: 1030 us; the launch traced here: 1020 us
  waiting for transfers between devices  463 us (45%)
  matrix products  207 us (20%)
  other arithmetic  122 us (12%)
  blocking collectives  111 us (11%)
  local copies, waits for them, and re-layouts  96.9 us (9%)
  between operations  17.7 us (2%)
    reduce_scatter x1, waiting for transfers between devices, body(): lax.psum_scatter(jnp.stack([weight_parts[0][2]], axis=0).astype(jnp.bfloa...  97.1 us
    psum x2, waiting for transfers between devices, norm_backward(): lax.psum(partials[0].astype(jnp.bfloat16), 'tensor').astype(jnp.float32)  88.3 us
    unnamed x229, local copies, waits for them, and re-layouts  80.3 us
    reduce_scatter x1, waiting for transfers between devices, body(): lax.psum_scatter(jnp.stack([weight_parts[0][3]], axis=0).astype(jnp.bfloa...  80.3 us
    unnamed x20, waiting for transfers between devices  78.7 us
    reduce_scatter x1, waiting for transfers between devices, body(): lax.psum_scatter(jnp.stack([weight_parts[0][0]], axis=0).astype(jnp.bfloa...  74.9 us
    all_gather x2, waiting for transfers between devices, gather_grads(): lax.all_gather(branch_grads[0], 'tensor', axis=2, tiled=True)  28.9 us
    psum x1, blocking collectives, body(): lax.psum((jnp.stack([bias_parts[0][0]], axis=0), jnp.stack([bias_parts[0]...  27.3 us
  transfers between devices with their start and end apart: 15, of which 9 were waited for; matrix products, arithmetic and copies ran while one was open for 31% of the time, Pallas kernels for 0%

commit v1 on v0

--- a/solution.py
+++ b/solution.py
@@ -1,9 +1,22 @@
+import functools
+
 import jax
 import jax.numpy as jnp
 from jax import lax
+from jax.experimental import pallas as pl
+from jax.experimental.pallas import tpu as pltpu
 from jax.sharding import PartitionSpec as P
 
 HEAD_DIM = 64
+EPS = 1e-06
+F32 = jnp.float32
+BF16 = jnp.bfloat16
+GELU_C = 0.7978845608028654
+GELU_K = 0.044715
+MIB = 1 << 20
+MESH = pl.DeviceIdType.MESH
+VMEM = pl.BlockSpec(memory_space=pltpu.VMEM)
+ANY = pl.BlockSpec(memory_space=pl.ANY)
 
 
 eps_norm = 1e-06
@@ -137,7 +150,7 @@
     return stacked.reshape(seq_count, tokens, 3, heads_here * HEAD_DIM).astype(jnp.bfloat16)
 
 
-def body(
+def plain_body(
     image_in,
     text_in,
     cond_in,
@@ -494,9 +507,987 @@
     )
 
 
+def nt_dot(a, b):
+    return lax.dot_general(a, b, (((1,), (1,)), ((), ())), preferred_element_type=F32)
+
+
+def nn_dot(a, b):
+    return lax.dot_general(a, b, (((1,), (0,)), ((), ())), preferred_element_type=F32)
+
+
+def tn_dot(a, b):
+    return lax.dot_general(a, b, (((0,), (0,)), ((), ())), preferred_element_type=F32)
+
+
+def exact_nt(a, b):
+    return lax.dot_general(
+        a, b, (((1,), (1,)), ((), ())), preferred_element_type=F32, precision=lax.Precision.HIGHEST
+    )
+
+
+def exact_tn(a, b):
+    return lax.dot_general(
+        a, b, (((0,), (0,)), ((), ())), preferred_element_type=F32, precision=lax.Precision.HIGHEST
+    )
+
+
+def sds(shape, dtype):
+    return jax.ShapeDtypeStruct(shape, dtype)
+
+
+def cost(flops, arrays, outs):
+    moved = sum(a.size * a.dtype.itemsize for a in arrays)
+    moved += sum(o.size * o.dtype.itemsize for o in outs)
+    return pl.CostEstimate(flops=flops, bytes_accessed=moved, transcendentals=0)
+
+
+def eye_rows():
+    return (
+        lax.broadcasted_iota(jnp.int32, (8, 128), 0) == lax.broadcasted_iota(jnp.int32, (8, 128), 1)
+    ).astype(F32)
+
+
+def norm_stats(pieces, width):
+    total = sum(jnp.sum(p, axis=-1, keepdims=True) for p in pieces)
+    mean = total / width
+    centred = [p - mean for p in pieces]
+    var = sum(jnp.sum(c * c, axis=-1, keepdims=True) for c in centred) / width
+    return mean, lax.rsqrt(var + EPS), centred
+
+
+def stat_rows(first, second):
+    lane = lax.broadcasted_iota(jnp.int32, (first.shape[0], 128), 1)
+    both = jnp.where(lane == 0, first, jnp.where(lane == 1, second, 0.0))
+    return exact_nt(eye_rows(), both)
+
+
+def stat_cols(first, second):
+    lane = lax.broadcasted_iota(jnp.int32, (first.shape[0], 128), 1)
+    return jnp.where(lane == 0, first, jnp.where(lane == 1, second, 0.0))
+
+
+class Links:
+    def __init__(self, send, recv):
+        self.send_sem, self.recv_sem = send, recv
+        me = lax.axis_index("tensor")
+        self.peers = [me, me + 1 - 2 * (me % 2), (me + 2) % 4, 3 - me]
+
+    def enter(self, extra=()):
+        barrier = pltpu.get_barrier_semaphore()
+        for peer in self.peers[1:]:
+            pl.semaphore_signal(barrier, inc=1, device_id={"tensor": peer}, device_id_type=MESH)
+        for peer in extra:
+            pl.semaphore_signal(barrier, inc=1, device_id={"dp": peer}, device_id_type=MESH)
+        pl.semaphore_wait(barrier, 3 + len(extra))
+
+    def copy(self, src, dst, kind, c, peer):
+        return pltpu.make_async_remote_copy(
+            src_ref=src,
+            dst_ref=dst,
+            send_sem=self.send_sem.at[kind, c],
+            recv_sem=self.recv_sem.at[kind, c],
+            device_id={"tensor": peer},
+            device_id_type=MESH,
+        )
+
+    def route(self, c):
+        odd = c % 2
+        first = self.peers[1] * (1 - odd) + self.peers[2] * odd
+        second = self.peers[2] * (1 - odd) + self.peers[1] * odd
+        return 1 + odd, 2 - odd, first, second
+
+    def gather_copy(self, i, src, buf, kind, c):
+        near, far, first, second = self.route(c)
+        if i == 0:
+            return self.copy(src, buf.at[c, near], kind, c, first)
+        if i == 1:
+            return self.copy(src, buf.at[c, far], kind + 1, c, second)
+        return self.copy(buf.at[c, near], buf.at[c, 3], kind + 2, c, second)
+
+    def gather_start(self, *args):
+        self.gather_copy(0, *args).start()
+        self.gather_copy(1, *args).start()
+
+    def gather_relay(self, *args):
+        self.gather_copy(0, *args).wait_recv()
+        self.gather_copy(2, *args).start()
+
+    def gather_finish(self, *args):
+        self.gather_copy(1, *args).wait_recv()
+        self.gather_copy(2, *args).wait_recv()
+
+    def gather_sent(self, *args):
+        for i in range(3):
+            self.gather_copy(i, *args).wait_send()
+
+    def scatter_copy(self, i, part, relayed, got, kind, c):
+        near, _, first, second = self.route(c)
+        if i == 0:
+            return self.copy(part.at[c, 3], got.at[c, 0], kind, c, first)
+        if i == 1:
+            return self.copy(part.at[c, near], got.at[c, 1], kind + 1, c, first)
+        return self.copy(relayed.at[c], got.at[c, 2], kind + 2, c, second)
+
+    def scatter_start(self, *args):
+        self.scatter_copy(0, *args).start()
+        self.scatter_copy(1, *args).start()
+
+    def scatter_relay(self, part, relayed, got, kind, c):
+        self.scatter_copy(0, part, relayed, got, kind, c).wait_recv()
+        _, far, _, _ = self.route(c)
+        relayed[c] = (part[c, far].astype(F32) + got[c, 0].astype(F32)).astype(BF16)
+        self.scatter_copy(2, part, relayed, got, kind, c).start()
+
+    def scatter_sent(self, *args):
+        for i in range(3):
+            self.scatter_copy(i, *args).wait_send()
+
+    def scatter_finish(self, part, relayed, got, kind, c):
+        self.scatter_copy(1, part, relayed, got, kind, c).wait_recv()
+        self.scatter_copy(2, part, relayed, got, kind, c).wait_recv()
+        return part[c, 0].astype(F32) + got[c, 1].astype(F32) + got[c, 2].astype(F32)
+
+    def rows_copies(self, src, dst, kind, c):
+        return [
+            self.copy(src.at[c], dst.at[c, k - 1], kind + k - 1, c, self.peers[k]) for k in (1, 2, 3)
+        ]
+
+    def rows_start(self, src, dst, kind, c):
+        for copy in self.rows_copies(src, dst, kind, c):
+            copy.start()
+
+    def rows_finish(self, src, dst, kind, c):
+        for copy in self.rows_copies(src, dst, kind, c):
+            copy.wait_recv()
+        return src[c] + dst[c, 0] + dst[c, 1] + dst[c, 2]
+
+
+def wait_sends(copies):
+    for copy in copies:
+        copy.wait_send()
+
+
+def stages(count, steps):
+    last = max(offset for offset, _ in steps)
+
+    def tick(t, carry):
+        for offset, step in steps:
+            c = t - offset
+
+            @pl.when((c >= 0) & (c < count))
+            def _():
+                step(c)
+
+        return carry
+
+    lax.fori_loop(0, count + last, tick, 0)
+
+
+def front_kernel(dp, valid, refs_in, refs_out, scratch):
+    x_ref, cot_ref, act_ref, modw_ref, modb_ref, wq_ref, bq_ref = refs_in
+    m_ref, qkv_ref, o_ref, lse_ref, g_ref, xp_ref, mod_ref, gsum_ref = refs_out
+    modw, wq, terms, got, k_all, aug, local, send, recv, msend, mrecv = scratch
+    count, rows, feats = x_ref.shape
+    cols = qkv_ref.shape[-1]
+    width = 4 * feats
+    links = Links(send, recv)
+    mine = lax.axis_index("dp")
+    others = [(mine + r) % dp for r in range(1, dp)]
+    load_mod = pltpu.make_async_copy(modw_ref, modw, local.at[0])
+    load_wq = pltpu.make_async_copy(wq_ref, wq, local.at[1])
+    load_mod.start()
+    load_wq.start()
+    links.enter(others)
+    for c in range(count):
+        links.gather_start(x_ref.at[c], xp_ref, 0, c)
+    load_mod.wait()
+    act = act_ref[...]
+    for j in range(12):
+        terms[:, j, :] = nn_dot(act, modw[j])
+    pushes = [
+        pltpu.make_async_remote_copy(
+            src_ref=terms.at[others[r]],
+            dst_ref=got.at[r],
+            send_sem=msend.at[r],
+            recv_sem=mrecv.at[r],
+            device_id={"dp": others[r]},
+            device_id_type=MESH,
+        )
+        for r in range(dp - 1)
+    ]
+    for push in pushes:
+        push.start()
+    for c in range(count):
+        xp_ref[c, 0] = x_ref[c]
+    total = terms[mine] + modb_ref[...]
+    for r, push in enumerate(pushes):
+        push.wait_recv()
+        total = total + got[r]
+    mod_ref[0] = total
+    mod_copies = [
+        links.copy(mod_ref.at[0], mod_ref.at[k], 6, k, links.peers[k]) for k in (1, 2, 3)
+    ]
+    for copy in mod_copies:
+        copy.start()
+    for c in range(count):
+        links.gather_relay(x_ref.at[c], xp_ref, 0, c)
+    for c in range(count):
+        stream = c // (count - 1)
+        g = (total[stream * 6 + 5 : stream * 6 + 6, :] * cot_ref[c].astype(F32)).astype(BF16)
+        g_ref[c, 0] = g
+        gsum_ref[c : c + 1, :] = jnp.sum(g.astype(F32), axis=0, keepdims=True)
+    for c in range(count):
+        links.gather_start(g_ref.at[c, 0], g_ref, 3, c)
+    for copy in mod_copies:
+        copy.wait_recv()
+    load_wq.wait()
+
+    def project(c, carry):
+        stream = c // (count - 1)
+        links.gather_finish(x_ref.at[c], xp_ref, 0, c)
+        _, inv, centred = norm_stats([xp_ref[c, k].astype(F32) for k in range(4)], width)
+        acc = [None] * 3
+        for k in range(4):
+            shift = mod_ref[k, pl.ds(stream * 6, 1), :]
+            scale = mod_ref[k, pl.ds(stream * 6 + 1, 1), :]
+            m = (centred[k] * inv * (1.0 + scale) + shift).astype(BF16)
+            m_ref[c, k] = m
+            for j in range(3):
+                part = nn_dot(m, wq[stream, j, links.peers[k]])
+                acc[j] = part if k == 0 else acc[j] + part
+        for j in range(3):
+            qkv_ref[j, c] = (acc[j] + bq_ref[stream, j : j + 1, :]).astype(BF16)
+        links.gather_relay(g_ref.at[c, 0], g_ref, 3, c)
+        return carry
+
+    lax.fori_loop(0, count, project, 0)
+
+    owner = lax.broadcasted_iota(jnp.int32, (1, 128), 1) // HEAD_DIM
+
+    def heads_pair(p, carry):
+        lanes = pl.ds(pl.multiple_of(p * 128, 128), 128)
+        for c in range(count):
+            size = min(rows, valid - c * rows)
+            sl = slice(c * rows, c * rows + size)
+            k_all[sl, :] = qkv_ref[1, c, :size, lanes]
+            values = qkv_ref[2, c, :size, lanes]
+            for h in range(2):
+                aug[h, sl, :] = jnp.where(owner == h, values, jnp.ones_like(values))
+
+        def chunk(c, inner):
+            q = qkv_ref[0, c, :, lanes] * jnp.asarray(HEAD_DIM**-0.5, BF16)
+            out, lse = [], []
+            for h in range(2):
+                scores = nt_dot(jnp.where(owner == h, q, jnp.zeros_like(q)), k_all[...])
+                top = jnp.max(scores, axis=-1, keepdims=True)
+                acc = nn_dot(jnp.exp(scores - top).astype(BF16), aug[h])
+                other = (1 - h) * HEAD_DIM
+                denom = acc[:, other : other + 1]
+                out.append(acc / denom)
+                lse.append(top + jnp.log(denom))
+            o_ref[c, :, lanes] = jnp.where(owner == 0, out[0], out[1]).astype(BF16)
+            lse_ref[c, :, lanes] = jnp.where(owner == 0, lse[0], lse[1])
+            return inner
+
+        lax.fori_loop(0, count, chunk, 0)
+        return carry
+
+    lax.fori_loop(0, cols // 128, heads_pair, 0)
+    for c in range(count):
+        links.gather_finish(g_ref.at[c, 0], g_ref, 3, c)
+        links.gather_sent(x_ref.at[c], xp_ref, 0, c)
+        links.gather_sent(g_ref.at[c, 0], g_ref, 3, c)
+    wait_sends(mod_copies)
+    wait_sends(pushes)
+
+
+def front_call(dp, valid, x, cot, act, mod_w, mod_b, wq, bq):
+    count, rows, feats = x.shape
+    cols = wq.shape[-1]
+    arrays = [x, cot, act, mod_w, mod_b, wq, bq]
+    outs = [
+        sds((count, 4, rows, feats), BF16),
+        sds((3, count, rows, cols), BF16),
+        sds((count, rows, cols), BF16),
+        sds((count, rows, cols), F32),
+        sds((count, 4, rows, feats), BF16),
+        sds((count, 4, rows, feats), BF16),
+        sds((4, 12, feats), F32),
+        sds((count, feats), F32),
+    ]
+    n_in, n_out = len(arrays), len(outs)
+
+    def kernel(*refs):
+        front_kernel(dp, valid, refs[:n_in], refs[n_in : n_in + n_out], refs[n_in + n_out :])
+
+    return pl.pallas_call(
+        kernel,
+        out_shape=outs,
+        in_specs=[VMEM, VMEM, VMEM, ANY, VMEM, ANY, VMEM],
+        out_specs=[VMEM] * n_out,
+        scratch_shapes=[
+            pltpu.VMEM(mod_w.shape, BF16),
+            pltpu.VMEM(wq.shape, BF16),
+            pltpu.VMEM((dp, 12, feats), F32),
+            pltpu.VMEM((dp - 1, 12, feats), F32),
+            pltpu.VMEM((valid, 128), BF16),
+            pltpu.VMEM((2, valid, 128), BF16),
+            pltpu.SemaphoreType.DMA((2,)),
+            pltpu.SemaphoreType.DMA((7, count)),
+            pltpu.SemaphoreType.DMA((7, count)),
+            pltpu.SemaphoreType.DMA((dp - 1,)),
+            pltpu.SemaphoreType.DMA((dp - 1,)),
+        ],
+        compiler_params=pltpu.CompilerParams(
+            collective_id=1, has_side_effects=True, vmem_limit_bytes=56 * MIB
+        ),
+        cost_estimate=cost(20 * 10**9, arrays, outs),
+        name="front",
+    )(*arrays)
+
+
+HB = 512
+
+
+def middle_kernel(refs_in, refs_out, scratch):
+    o_ref, x_ref, cot_ref, db2_ref, mod_ref, wo_ref, up_ref, down_ref, ub_ref, ob_ref = refs_in
+    x1_out, m2_out, a_out, du_out, b2_out, g1_out, g_ref, do_ref, line_ref, dub_ref = refs_out
+    (wo, up, down, db2, part, relayed, got, xp, branch, acc_m, acc_b, cols_s) = scratch[:12]
+    (x1_s, m2_s, a_s, du_s, b2_s, g1_s, srow, sgot, local, out_sem, send, recv) = scratch[12:]
+    count, _, feats = x_ref.shape
+    width = 4 * feats
+    hidden = up.shape[-1]
+    links = Links(send, recv)
+    loads = [
+        pltpu.make_async_copy(src, dst, local.at[i])
+        for i, (src, dst) in enumerate(
+            [(wo_ref, wo), (up_ref, up), (down_ref, down), (db2_ref, db2)]
+        )
+    ]
+    for load in loads:
+        load.start()
+    links.enter()
+    loads[0].wait()
+
+    def flush(staged, out, kind, c):
+        return pltpu.make_async_copy(staged.at[c % 2], out.at[c], out_sem.at[kind, c % 2])
+
+    def project(c):
+        stream = c // (count - 1)
+        o = o_ref[c]
+        for k in (3, 1, 2, 0):
+            part[c, k] = nt_dot(o, wo[stream, links.peers[k]]).astype(BF16)
+        links.scatter_start(part, relayed, got, 0, c)
+
+    def first_relay(c):
+        links.scatter_relay(part, relayed, got, 0, c)
+
+    def residual(c):
+        stream = c // (count - 1)
+        total = links.scatter_finish(part, relayed, got, 0, c)
+        add = total + ob_ref[pl.ds(stream, 1), :]
+        branch[c] = add
+        moved = x_ref[c].astype(F32) + mod_ref[0, pl.ds(stream * 6 + 2, 1), :] * add
+
+        @pl.when(c >= 2)
+        def _():
+            flush(x1_s, x1_out, 0, c - 2).wait()
+
+        x1_s[c % 2] = moved
+        flush(x1_s, x1_out, 0, c).start()
+        xp[c, 0] = moved.astype(BF16)
+        links.gather_start(xp.at[c, 0], xp, 3, c)
+
+    def second_relay(c):
+        links.gather_relay(xp.at[c, 0], xp, 3, c)
+
+    def feed_forward(c):
+        stream = c // (count - 1)
+        slot = c % 2
+
+        @pl.when(c == 0)
+        def _():
+            for load in loads[1:]:
+                load.wait()
+
+        @pl.when(c >= 2)
+        def _():
+            for kind, (staged, out) in enumerate(
+                [(m2_s, m2_out), (a_s, a_out), (du_s, du_out), (b2_s, b2_out)]
+            ):
+                flush(staged, out, kind + 1, c - 2).wait()
+
+        links.gather_finish(xp.at[c, 0], xp, 3, c)
+        links.scatter_sent(part, relayed, got, 0, c)
+        mean, inv, centred = norm_stats([xp[c, k].astype(F32) for k in range(4)], width)
+        for k in range(4):
+            shift = mod_ref[k, pl.ds(stream * 6 + 3, 1), :]
+            scale = mod_ref[k, pl.ds(stream * 6 + 4, 1), :]
+            m2_s[slot, k] = (centred[k] * inv * (1.0 + scale) + shift).astype(BF16)
+
+        def block(b, carry):
+            cols = pl.ds(pl.multiple_of(b * HB, HB), HB)
+            u = ub_ref[pl.ds(stream, 1), cols]
+            for k in range(4):
+                u = u + nn_dot(m2_s[slot, k], up[stream, links.peers[k], :, cols])
+            da = None
+            for k in range(4):
+                piece = nn_dot(db2[c, k], down[stream, links.peers[k], :, cols])
+                da = piece if da is None else da + piece
+            square = u * u
+            th = jnp.tanh(u * (GELU_C + (GELU_C * GELU_K) * square))
+            up_half = 0.5 + 0.5 * th
+            a = (u * up_half).astype(BF16)
+            slope = up_half * (
+                1.0 + u * (1.0 - th) * (GELU_C + (3.0 * GELU_C * GELU_K) * square)
+            )
+            du = (da * slope).astype(BF16)
+            a_s[slot, :, cols] = a
+            du_s[slot, :, cols] = du
+            dub_ref[pl.ds(c, 1), cols] = jnp.sum(du.astype(F32), axis=0, keepdims=True)
+            for k in range(4):
+                dm = nt_dot(du, up[stream, links.peers[k], :, cols])
+                bb = nt_dot(a, down[stream, links.peers[k], :, cols])
+
+                @pl.when(b == 0)
+                def _():
+                    acc_m[k] = dm
+                    acc_b[k] = bb
+
+                @pl.when(b != 0)
+                def _():
+                    acc_m[k] += dm
+                    acc_b[k] += bb
+
+            return carry
+
+        lax.fori_loop(0, hidden // HB, block, 0)
+        first = second = None
+        for k in range(4):
+            dm = acc_m[k]
+            part[c, k] = dm.astype(BF16)
+            dh = dm * (1.0 + mod_ref[k, pl.ds(stream * 6 + 4, 1), :])
+            one = jnp.sum(dh, axis=-1, keepdims=True)
+            two = jnp.sum(dh * (xp[c, k].astype(F32) - mean), axis=-1, keepdims=True)
+            first = one if first is None else first + one
+            second = two if second is None else second + two
+        srow[c] = stat_rows(first, second * inv)
+        links.scatter_start(part, relayed, got, 6, c)
+        links.rows_start(srow, sgot, 12, c)
+        cols_s[c] = stat_cols(mean, inv)
+        for k in range(4):
+            b2_s[slot, k] = acc_b[k].astype(BF16)
+        for kind, (staged, out) in enumerate(
+            [(m2_s, m2_out), (a_s, a_out), (du_s, du_out), (b2_s, b2_out)]
+        ):
+            flush(staged, out, kind + 1, c).start()
+
+    def third_relay(c):
+        links.scatter_relay(part, relayed, got, 6, c)
+
+    def norm_back(c):
+        stream = c // (count - 1)
+        total = links.scatter_finish(part, relayed, got, 6, c)
+        sums = exact_tn(links.rows_finish(srow, sgot, 12, c), eye_rows())
+        mean, inv = cols_s[c, :, 0:1], cols_s[c, :, 1:2]
+        normed = (xp[c, 0].astype(F32) - mean) * inv
+        grad = total * (1.0 + mod_ref[0, pl.ds(stream * 6 + 4, 1), :])
+        g = cot_ref[c].astype(F32) + inv * (
+            grad - sums[:, 0:1] / width - normed * (sums[:, 1:2] / width)
+        )
+        db = (mod_ref[0, pl.ds(stream * 6 + 2, 1), :] * g).astype(BF16)
+        g_ref[c, 0] = db
+        links.gather_start(g_ref.at[c, 0], g_ref, 9, c)
+
+        @pl.when(c >= 2)
+        def _():
+            flush(g1_s, g1_out, 5, c - 2).wait()
+
+        g1_s[c % 2] = g
+        flush(g1_s, g1_out, 5, c).start()
+        line_ref[c, 0:1, :] = jnp.sum(total, axis=0, keepdims=True)
+        line_ref[c, 1:2, :] = jnp.sum(total * normed, axis=0, keepdims=True)
+        line_ref[c, 2:3, :] = jnp.sum(branch[c] * g, axis=0, keepdims=True)
+        line_ref[c, 3:4, :] = jnp.sum(db.astype(F32), axis=0, keepdims=True)
+
+    def fourth_relay(c):
+        links.gather_relay(g_ref.at[c, 0], g_ref, 9, c)
+
+    def head_grads(c):
+        stream = c // (count - 1)
+        links.gather_finish(g_ref.at[c, 0], g_ref, 9, c)
+        acc = None
+        for k in range(4):
+            piece = nn_dot(g_ref[c, k], wo[stream, links.peers[k]])
+            acc = piece if acc is None else acc + piece
+        do_ref[c] = acc.astype(BF16)
+
+    stages(
+        count,
+        [
+            (7, fourth_relay),
+            (5, third_relay),
+            (3, second_relay),
+            (1, first_relay),
+            (6, norm_back),
+            (2, residual),
+            (0, project),
+            (8, head_grads),
+            (4, feed_forward),
+        ],
+    )
+    for c in range(count):
+        links.gather_sent(xp.at[c, 0], xp, 3, c)
+        links.scatter_sent(part, relayed, got, 6, c)
+        links.gather_sent(g_ref.at[c, 0], g_ref, 9, c)
+        wait_sends(links.rows_copies(srow, sgot, 12, c))
+    for c in (count - 2, count - 1):
+        for kind, (staged, out) in enumerate(
+            [
+                (x1_s, x1_out),
+                (m2_s, m2_out),
+                (a_s, a_out),
+                (du_s, du_out),
+                (b2_s, b2_out),
+                (g1_s, g1_out),
+            ]
+        ):
+            flush(staged, out, kind, c).wait()
+
+
+def middle_call(o, x, cot, db2, mods, wo, up, down, ub, ob):
+    count, rows, feats = x.shape
+    cols, hidden = wo.shape[-1], up.shape[-1]
+    arrays = [o, x, cot, db2, mods, wo, up, down, ub, ob]
+    outs = [
+        sds((count, rows, feats), F32),
+        sds((count, 4, rows, feats), BF16),
+        sds((count, rows, hidden), BF16),
+        sds((count, rows, hidden), BF16),
+        sds((count, 4, rows, feats), BF16),
+        sds((count, rows, feats), F32),
+        sds((count, 4, rows, feats), BF16),
+        sds((count, rows, cols), BF16),
+        sds((count, 4, feats), F32),
+        sds((count, hidden), F32),
+    ]
+    n_in, n_out = len(arrays), len(outs)
+
+    def kernel(*refs):
+        middle_kernel(refs[:n_in], refs[n_in : n_in + n_out], refs[n_in + n_out :])
+
+    return pl.pallas_call(
+        kernel,
+        out_shape=outs,
+        in_specs=[VMEM, VMEM, VMEM, ANY, VMEM, ANY, ANY, ANY, VMEM, VMEM],
+        out_specs=[ANY] * 6 + [VMEM] * 4,
+        scratch_shapes=[
+            pltpu.VMEM(wo.shape, BF16),
+            pltpu.VMEM(up.shape, BF16),
+            pltpu.VMEM(down.shape, BF16),
+            pltpu.VMEM(db2.shape, BF16),
+            pltpu.VMEM((count, 4, rows, feats), BF16),
+            pltpu.VMEM((count, rows, feats), BF16),
+            pltpu.VMEM((count, 3, rows, feats), BF16),
+            pltpu.VMEM((count, 4, rows, feats), BF16),
+            pltpu.VMEM((count, rows, feats), F32),
+            pltpu.VMEM((4, rows, feats), F32),
+            pltpu.VMEM((4, rows, feats), F32),
+            pltpu.VMEM((count, rows, 128), F32),
+            pltpu.VMEM((2, rows, feats), F32),
+            pltpu.VMEM((2, 4, rows, feats), BF16),
+            pltpu.VMEM((2, rows, hidden), BF16),
+            pltpu.VMEM((2, rows, hidden), BF16),
+            pltpu.VMEM((2, 4, rows, feats), BF16),
+            pltpu.VMEM((2, rows, feats), F32),
+            pltpu.VMEM((count, 8, rows), F32),
+            pltpu.VMEM((count, 3, 8, rows), F32),
+            pltpu.SemaphoreType.DMA((4,)),
+            pltpu.SemaphoreType.DMA((6, 2)),
+            pltpu.SemaphoreType.DMA((15, count)),
+            pltpu.SemaphoreType.DMA((15, count)),
+        ],
+        compiler_params=pltpu.CompilerParams(
+            collective_id=2, has_side_effects=True, vmem_limit_bytes=63 * MIB
+        ),
+        cost_estimate=cost(30 * 10**9, arrays, outs),
+        name="middle",
+    )(*arrays)
+
+
+def back_kernel(valid, blocks, refs_in, refs_out, scratch):
+    qkv_ref, o_ref, do_ref, lse_ref, b2_ref, x1_ref, cot_ref, g1_ref, xp_ref, mod_ref = refs_in[:10]
+    wq_ref, db_ref = refs_in[10:]
+    dqkv_ref, x2_ref, grad_ref, line_ref, bias_ref = refs_out
+    wq, q_all, k_all, v_all, do_all, lse_all, od_all, dk_all, dv_all, dqt_all, dq_all = scratch[:11]
+    part, relayed, got, relayed2, got2, cols_s, srow, sgot, local, send, recv = scratch[11:]
+    count, rows, feats = cot_ref.shape
+    cols = o_ref.shape[-1]
+    width = 4 * feats
+    links = Links(send, recv)
+    load = pltpu.make_async_copy(wq_ref, wq, local.at[0])
+    load.start()
+    links.enter()
+    for c in range(count):
+        links.scatter_start(b2_ref, relayed2, got2, 0, c)
+    scale = jnp.asarray(HEAD_DIM**-0.5, BF16)
+    head_row = lax.broadcasted_iota(jnp.int32, (8, 128), 0)
+    lane = lax.broadcasted_iota(jnp.int32, (8, 128), 1)
+    first_lane = (lane == head_row * HEAD_DIM).astype(F32)
+    within = (lane // HEAD_DIM == head_row).astype(F32)
+    owner = lax.broadcasted_iota(jnp.int32, (1, 128), 1) // HEAD_DIM
+    zero = jnp.zeros((), BF16)
+    for c in range(count):
+        size = min(rows, valid - c * rows)
+        if size < rows:
+            for j in range(3):
+                dqkv_ref[j, c] = jnp.zeros((rows, cols), BF16)
+
+    def heads_pair(p, carry):
+        lanes = pl.ds(pl.multiple_of(p * 128, 128), 128)
+        for c in range(count):
+            size = min(rows, valid - c * rows)
+            sl = slice(c * rows, c * rows + size)
+            q_all[sl, :] = qkv_ref[0, c, :size, lanes] * scale
+            k_all[sl, :] = qkv_ref[1, c, :size, lanes]
+            v_all[sl, :] = qkv_ref[2, c, :size, lanes]
+            do = do_ref[c, :size, lanes]
+            do_all[sl, :] = do
+            lse_all[sl, :] = lse_ref[c, :size, lanes]
+            od_all[sl, :] = o_ref[c, :size, lanes].astype(F32) * do.astype(F32)
+        lse_rows = exact_nt(first_lane, lse_all[...])
+        dot_rows = exact_nt(within, od_all[...])
+        dqt = None
+        for h in range(2):
+            mine = owner == h
+            q = jnp.where(mine, q_all[...], zero)
+            do = jnp.where(mine, do_all[...], zero)
+            lse_row, dot_row = lse_rows[h : h + 1, :], dot_rows[h : h + 1, :]
+            for start, size in blocks:
+                sl = slice(start, start + size)
+                keys, values = k_all[sl, :], v_all[sl, :]
+                weights = jnp.exp(nt_dot(keys, q) - lse_row)
+                grads = (weights * (nt_dot(values, do) - dot_row)).astype(BF16)
+                dv = nn_dot(weights.astype(BF16), do)
+                dk = nn_dot(grads, q)
+                if h == 0:
+                    dv_all[sl, :] = dv
+                    dk_all[sl, :] = dk
+                else:
+                    dv_all[sl, :] += dv
+                    dk_all[sl, :] += dk
+                piece = tn_dot(jnp.where(mine, keys, zero) * scale, grads)
+                dqt = piece if dqt is None else dqt + piece
+        dqt_all[:, :valid] = dqt
+        dq_all[...] = dqt_all[...].T
+        for c in range(count):
+            size = min(rows, valid - c * rows)
+            sl = slice(c * rows, c * rows + size)
+            dqkv_ref[0, c, :size, lanes] = dq_all[sl, :].astype(BF16)
+            dqkv_ref[1, c, :size, lanes] = dk_all[sl, :].astype(BF16)
+            dqkv_ref[2, c, :size, lanes] = dv_all[sl, :].astype(BF16)
+
+        @pl.when(p == 0)
+        def _():
+            for c in range(count):
+                links.scatter_relay(b2_ref, relayed2, got2, 0, c)
+
+        return carry
+
+    lax.fori_loop(0, cols // 128, heads_pair, 0)
+    load.wait()
+
+    def input_grads(c):
+        stream = c // (count - 1)
+        mean, inv, centred = norm_stats([xp_ref[c, k].astype(F32) for k in range(4)], width)
+        first = second = None
+        for k in (3, 1, 2, 0):
+            dm = None
+            for j in range(3):
+                piece = nt_dot(dqkv_ref[j, c], wq[stream, j, links.peers[k]])
+                dm = piece if dm is None else dm + piece
+            part[c, k] = dm.astype(BF16)
+            dh = dm * (1.0 + mod_ref[k, pl.ds(stream * 6 + 1, 1), :])
+            one = jnp.sum(dh, axis=-1, keepdims=True)
+            two = jnp.sum(dh * centred[k], axis=-1, keepdims=True)
+            first = one if first is None else first + one
+            second = two if second is None else second + two
+        srow[c] = stat_rows(first, second * inv)
+        links.scatter_start(part, relayed, got, 3, c)
+        links.rows_start(srow, sgot, 6, c)
+        cols_s[c] = stat_cols(mean, inv)
+        for j in range(3):
+            bias_ref[c, j : j + 1, :] = jnp.sum(
+                dqkv_ref[j, c].astype(F32), axis=0, keepdims=True
+            )
+
+    def last_relay(c):
+        links.scatter_relay(part, relayed, got, 3, c)
+
+    def out_stream(c):
+        stream = c // (count - 1)
+        total = links.scatter_finish(b2_ref, relayed2, got2, 0, c)
+        add = total + db_ref[pl.ds(stream, 1), :]
+        x2_ref[c] = x1_ref[c] + mod_ref[0, pl.ds(stream * 6 + 5, 1), :] * add
+        line_ref[c, 2:3, :] = jnp.sum(add * cot_ref[c].astype(F32), axis=0, keepdims=True)
+
+    def norm_back(c):
+        stream = c // (count - 1)
+        total = links.scatter_finish(part, relayed, got, 3, c)
+        sums = exact_tn(links.rows_finish(srow, sgot, 6, c), eye_rows())
+        mean, inv = cols_s[c, :, 0:1], cols_s[c, :, 1:2]
+        normed = (xp_ref[c, 0].astype(F32) - mean) * inv
+        grad = total * (1.0 + mod_ref[0, pl.ds(stream * 6 + 1, 1), :])
+        grad_ref[c] = g1_ref[c] + inv * (
+            grad - sums[:, 0:1] / width - normed * (sums[:, 1:2] / width)
+        )
+        line_ref[c, 0:1, :] = jnp.sum(total, axis=0, keepdims=True)
+        line_ref[c, 1:2, :] = jnp.sum(total * normed, axis=0, keepdims=True)
+
+    stages(count, [(1, last_relay), (0, input_grads), (2, norm_back), (1, out_stream)])
+    for c in range(count):
+        links.scatter_sent(b2_ref, relayed2, got2, 0, c)
+        links.scatter_sent(part, relayed, got, 3, c)
+        wait_sends(links.rows_copies(srow, sgot, 6, c))
+
+
+def back_call(valid, qkv, o, do, lse, b2, x1, cot, g1, xp, mods, wq, down_b):
+    count, rows, feats = cot.shape
+    cols = o.shape[-1]
+    padded = -(-valid // 128) * 128
+    step = -(-valid // 3 // 16) * 16
+    blocks = [(b, min(step, valid - b)) for b in range(0, valid, step)]
+    arrays = [qkv, o, do, lse, b2, x1, cot, g1, xp, mods, wq, down_b]
+    outs = [
+        sds(qkv.shape, BF16),
+        sds((count, rows, feats), F32),
+        sds((count, rows, feats), F32),
+        sds((count, 3, feats), F32),
+        sds((count, 3, cols), F32),
+    ]
+    n_in, n_out = len(arrays), len(outs)
+
+    def kernel(*refs):
+        back_kernel(valid, blocks, refs[:n_in], refs[n_in : n_in + n_out], refs[n_in + n_out :])
+
+    return pl.pallas_call(
+        kernel,
+        out_shape=outs,
+        in_specs=[VMEM] * 10 + [ANY, VMEM],
+        out_specs=[VMEM] * n_out,
+        scratch_shapes=[pltpu.VMEM(wq.shape, BF16)]
+        + [pltpu.VMEM((valid, 128), BF16)] * 4
+        + [pltpu.VMEM((valid, 128), F32)] * 4
+        + [
+            pltpu.VMEM((128, padded), F32),
+            pltpu.VMEM((padded, 128), F32),
+            pltpu.VMEM((count, 4, rows, feats), BF16),
+            pltpu.VMEM((count, rows, feats), BF16),
+            pltpu.VMEM((count, 3, rows, feats), BF16),
+            pltpu.VMEM((count, rows, feats), BF16),
+            pltpu.VMEM((count, 3, rows, feats), BF16),
+            pltpu.VMEM((count, rows, 128), F32),
+            pltpu.VMEM((count, 8, rows), F32),
+            pltpu.VMEM((count, 3, 8, rows), F32),
+            pltpu.SemaphoreType.DMA((1,)),
+            pltpu.SemaphoreType.DMA((9, count)),
+            pltpu.SemaphoreType.DMA((9, count)),
+        ],
+        compiler_params=pltpu.CompilerParams(
+            collective_id=3, has_side_effects=True, vmem_limit_bytes=63 * MIB
+        ),
+        cost_estimate=cost(40 * 10**9, arrays, outs),
+        name="back",
+    )(*arrays)
+
+
+def flat(value):
+    return value.reshape((-1,) + value.shape[-1:])
+
+
+def wgrad_kernel(pairs, split, t_ref, *refs):
+    out_ref = refs[-1]
+    slot = 0
+    at = 0
+    for groups in pairs:
+        left, right = flat(refs[at][:, 0]), refs[at + 1]
+        at += 2
+        for j in range(groups):
+            acc = tn_dot(left, flat(right[j] if groups > 1 else right[...]))
+            size = acc.shape[0] // split
+            for p in range(split):
+                out_ref[p, slot] = acc[p * size : (p + 1) * size].astype(BF16)
+            slot += 1
+
+
+def wgrad_call(base, pairs, into, stream, dp):
+    count, _, rows, feats = pairs[0][0].shape
+    chunks = 1 if stream else count - 1
+    first = (count - 1) if stream else 0
+    cols = pairs[0][1].shape[-1]
+    split = dp // 4
+    groups = [right.shape[0] if right.ndim == 4 else 1 for _, right in pairs]
+    slots = sum(groups)
+    arrays, specs = [], []
+    for (left, right), g in zip(pairs, groups):
+        arrays += [left, right]
+        specs.append(
+            pl.BlockSpec((chunks, 1, rows, feats), lambda k, t: (first // chunks, k, 0, 0))
+        )
+        if g > 1:
+            specs.append(
+                pl.BlockSpec((g, chunks, rows, cols), lambda k, t: (0, first // chunks, 0, 0))
+            )
+        else:
+            specs.append(pl.BlockSpec((chunks, rows, cols), lambda k, t: (first // chunks, 0, 0)))
+    out = sds((dp, 2 * slots, feats // split, cols), BF16)
+    aliases = {}
+    if into is not None:
+        aliases = {1 + len(arrays): 0}
+        arrays.append(into)
+        specs.append(ANY)
+
+    def kernel(*refs):
+        wgrad_kernel(groups, split, *refs)
+
+    return pl.pallas_call(
+        kernel,
+        out_shape=[out],
+        grid_spec=pltpu.PrefetchScalarGridSpec(
+            num_scalar_prefetch=1,
+            grid=(4,),
+            in_specs=specs,
+            out_specs=[
+                pl.BlockSpec(
+                    (split, slots, feats // split, cols), lambda k, t: (t[0] ^ k, stream, 0, 0)
+                )
+            ],
+        ),
+        input_output_aliases=aliases,
+        compiler_params=pltpu.CompilerParams(
+            dimension_semantics=("arbitrary",), vmem_limit_bytes=48 * MIB
+        ),
+        cost_estimate=cost(2 * 4 * feats * slots * cols * chunks * rows, arrays, [out]),
+    )(base, *arrays)[0]
+
+
+def fast_body(
+    dp,
+    image_in,
+    text_in,
+    cond_in,
+    mod_weight,
+    mod_bias,
+    qkv_weight,
+    qkv_bias,
+    out_weight,
+    out_bias,
+    up_weight,
+    up_bias,
+    down_weight,
+    down_bias,
+    image_cot,
+    text_cot,
+):
+    base = lax.axis_index("tensor").astype(jnp.int32).reshape(1)
+    feats = image_in.shape[2]
+    images, texts = image_in.shape[1], text_in.shape[1]
+    rows = images // 4
+    valid = images + texts
+
+    def join(image, text):
+        padded = jnp.pad(text[0], ((0, rows - texts), (0, 0)))
+        return jnp.concatenate([image[0].reshape(4, rows, feats), padded[None]], axis=0)
+
+    def parted(value):
+        image = value[:4].reshape(1, images, feats)
+        return image, value[4:, :texts]
+
+    x, cot = join(image_in, text_in), join(image_cot, text_cot)
+    cond_float = cond_in.astype(F32)
+    cond_act = jax.nn.silu(cond_float).astype(BF16)
+    mod_w = jnp.transpose(mod_weight[0], (0, 2, 1, 3)).reshape(12, -1, feats)
+    mod_b = mod_bias[0].reshape(12, feats).astype(F32)
+    qkv_w = jnp.transpose(qkv_weight[0], (0, 2, 1, 3))
+    qkv_w = qkv_w.reshape(2, 3, 4, feats, qkv_w.shape[-1])
+    out_w = out_weight[0].reshape(2, 4, feats, -1)
+    up_w = up_weight[0].reshape(2, 4, feats, -1)
+    down_w = down_weight[0].reshape(2, 4, feats, -1)
+
+    m, qkv, o, lse, db2, xp, mods, db2_sum = front_call(
+        dp, valid, x, cot, cond_act, mod_w, mod_b, qkv_w, qkv_bias[0].astype(F32)
+    )
+    x1, m2, act, du, b2, g1, db1, do, lines2, du_sum = middle_call(
+        o, x, cot, db2, mods, out_w, up_w, down_w, up_bias[0].astype(F32), out_bias[0].astype(F32)
+    )
+    part = wgrad_call(base, [(m2, du), (db2, act)], None, 0, dp)
+    part = wgrad_call(base, [(m2, du), (db2, act)], part, 1, dp)
+    do, part = lax.optimization_barrier((do, part))
+    ff_sum = lax.psum_scatter(part, "dp", scatter_dimension=0, tiled=True)
+    ff_grad = ff_sum[0].astype(F32)
+    dqkv, x2, grad, lines1, qkv_sum = back_call(
+        valid, qkv, o, do, lse, b2, x1, cot, g1, xp, mods, qkv_w, down_bias[0].astype(F32)
+    )
+    part2 = wgrad_call(base, [(m, dqkv), (db1, o)], None, 0, dp)
+    part2 = wgrad_call(base, [(m, dqkv), (db1, o)], part2, 1, dp)
+    at_sum = lax.psum_scatter(part2, "dp", scatter_dimension=0, tiled=True)
+    at_grad = at_sum[0].astype(F32)
+
+    def by_stream(value):
+        return jnp.stack([jnp.sum(value[:4], axis=0), value[4]])
+
+    late, early = by_stream(lines1), by_stream(lines2)
+    mod_rows = jnp.stack(
+        [late[:, 0], late[:, 1], early[:, 2], early[:, 0], early[:, 1], late[:, 2]], axis=1
+    )
+    mod_grad = mod_rows.reshape(12, feats).astype(BF16)
+    all_mod = lax.all_gather(mod_grad, "dp", axis=0)
+    mod_wgrad = jnp.einsum("sc,sgd->gcd", cond_act, all_mod, preferred_element_type=F32)
+    mod_wgrad = jnp.transpose(mod_wgrad.reshape(1, 2, 6, -1, feats), (0, 1, 3, 2, 4))
+    mod_bgrad = jnp.sum(all_mod.astype(F32), axis=0).reshape(1, 2, 6, feats)
+    act_part = jnp.einsum("sgd,gcd->sc", all_mod, mod_w, preferred_element_type=F32)
+    act_total = act_part + sum(
+        lax.ppermute(act_part, "tensor", [(i, i ^ k) for i in range(4)]) for k in (1, 2, 3)
+    )
+    cond_grad = jax.vjp(jax.nn.silu, cond_float)[1](act_total)[0]
+    biases = lax.psum(
+        (
+            by_stream(qkv_sum)[None],
+            early[None, :, 3],
+            by_stream(du_sum)[None],
+            by_stream(db2_sum)[None],
+        ),
+        "dp",
+    )
+    at_grad = at_grad.reshape((2, 4) + at_grad.shape[1:])
+    ff_grad = ff_grad.reshape((2, 2) + ff_grad.shape[1:])
+    qkv_wgrad = jnp.transpose(at_grad[None, :, :3], (0, 1, 3, 2, 4))
+    image_out, text_out = parted(x2)
+    image_grad, text_grad = parted(grad)
+    return (
+        image_out,
+        text_out,
+        image_grad,
+        text_grad,
+        cond_grad,
+        mod_wgrad,
+        mod_bgrad,
+        qkv_wgrad,
+        biases[0],
+        at_grad[None, :, 3],
+        biases[1],
+        ff_grad[None, :, 0],
+        biases[2],
+        ff_grad[None, :, 1],
+        biases[3],
+    )
+
+
 def solution(mesh):
+    dp, tensor = mesh.shape["dp"], mesh.shape["tensor"]
+    chosen = functools.partial(fast_body, dp) if tensor == 4 else plain_body
     return jax.shard_map(
-        body,
+        chosen,
         mesh=mesh,
         in_specs=(
             P("dp", None, "tensor"),

time: 1030 us -> 674 us (0.65); the launches traced: 1020 us -> 673 us
  Pallas kernels: 0 us -> 351 us
  waiting for transfers between devices: 463 us -> 225 us
  matrix products: 207 us -> 3.02 us
  other arithmetic: 122 us -> 14.4 us
  local copies, waits for them, and re-layouts: 96.9 us -> 18.6 us
  blocking collectives: 111 us -> 42.2 us
    pallas_call x0 -> x7, Pallas kernels: none -> 351 us  [the longest x1 149 us: middle_call(): pl.pallas_call(kernel, out_shape=outs, in_specs=[VMEM, VMEM, VMEM, ANY, V...]
    dot_general x33 -> x2, matrix products: 207 us -> 3.02 us  [the longest x1 2.47 us: fast_body(): jnp.einsum('sc,sgd->gcd', cond_act, all_mod, preferred_element_type=F32)]
    psum x2 -> x0, waiting for transfers between devices: 88.3 us -> none  [norm_backward(): lax.psum(partials[0].astype(jnp.bfloat16), 'tensor').astype(jnp.float32)]
    unnamed x20 -> x2, waiting for transfers between devices: 78.7 us -> 0.71 us
    unnamed x229 -> x27, local copies, waits for them, and re-layouts: 80.3 us -> 7.39 us
    all_gather x6 -> x1, blocking collectives: 74.3 us -> 14.5 us  [fast_body(): all_mod = lax.all_gather(mod_grad, 'dp', axis=0)]
    all_gather x4 -> x0, waiting for transfers between devices: 43.6 us -> none  [the longest x2 28.9 us: gather_grads(): lax.all_gather(branch_grads[0], 'tensor', axis=2, tiled=True)]
    reduce_sum x22 -> x6, other arithmetic: 43.9 us -> 0.84 us  [the longest x5 0.81 us: by_stream(): return jnp.stack([jnp.sum(value[:4], axis=0), value[4]])]
  transfers between devices with their start and end apart: 15 -> 5, of which waited for: 9 -> 2; matrix products, arithmetic and copies ran while one was open for 31% -> 2% of each run, Pallas kernels for 0% -> 0%
where the time goes in v1:
time: 674 us; the launch traced here: 673 us
  Pallas kernels  351 us (52%)
  waiting for transfers between devices  225 us (33%)
  blocking collectives  42.2 us (6%)
  local copies, waits for them, and re-layouts  18.6 us (3%)
  other arithmetic  14.4 us (2%)
  between operations  14.4 us (2%)
    reduce_scatter x1, waiting for transfers between devices, fast_body(): ff_sum = lax.psum_scatter(part, 'dp', scatter_dimension=0, tiled=True)  185 us
    pallas_call x1, Pallas kernels, middle_call(): pl.pallas_call(kernel, out_shape=outs, in_specs=[VMEM, VMEM, VMEM, ANY, V...  149 us
    pallas_call x1, Pallas kernels, back_call(): pl.pallas_call(kernel, out_shape=outs, in_specs=[VMEM] * 10 + [ANY, VMEM]...  83.5 us
    pallas_call x1, Pallas kernels, front_call(): pl.pallas_call(kernel, out_shape=outs, in_specs=[VMEM, VMEM, VMEM, ANY, V...  82.3 us
    reduce_scatter x1, waiting for transfers between devices, fast_body(): at_sum = lax.psum_scatter(part2, 'dp', scatter_dimension=0, tiled=True)  39.9 us
    pallas_call x4, Pallas kernels, wgrad_call(): pl.pallas_call(kernel, out_shape=[out], grid_spec=pltpu.PrefetchScalarGri...  36.7 us
    psum x1, blocking collectives, fast_body(): lax.psum((by_stream(qkv_sum)[None], early[None, :, 3], by_stream(du_sum)[...  27.7 us
    all_gather x1, blocking collectives, fast_body(): all_mod = lax.all_gather(mod_grad, 'dp', axis=0)  14.5 us
  transfers between devices with their start and end apart: 5, of which 2 were waited for; matrix products, arithmetic and copies ran while one was open for 2% of the time, Pallas kernels for 0%

profile of v1, /device:TPU:0, one launch (start us, length us, event | category | flops | bytes accessed | tf_op | source)
XLA Modules:
  0.0 672.7 jit_solution(14652585945065546675)
XLA Ops:
  7.2 0.0 reduce-scatter.3.cloned.1.call-start
  7.2 1.3 bitcast_convert_fusion.3.refs_9_
  8.5 1.3 bitcast_convert_fusion.2.refs_11_
  9.8 1.3 fusion.7.refs_2_
  11.0 1.3 bitcast_convert_fusion.1.refs_6_
  12.3 1.3 bitcast_convert_fusion.refs_8_
  13.6 0.7 copy.53
  14.3 0.6 reshape.88.refs_4_
  14.9 0.9 pad_bitcast_fusion.1
  15.9 0.9 pad_bitcast_fusion
  16.8 2.7 pad_maximum_fusion
  19.5 82.3 %front.1 = (bf16[5,4,224,384]{3,2,1,0:T(8,128)(2,1)}, bf16[3,5,224,384]{3,2,1,0:T(8,128)(2,1)}, bf16[5,224,384]{2,1,0:T(8,128)(2,1)}, f32[5,224,384]{2,1,0:T(8,1...) custom-call(bf16[5,224,384]{2,1,0:T(8,128)(2,1)} %get-tuple-element., ...), custom_call_target="tpu_custom_call" | custom-call | flops 20000000000 | bytes 26162688 | tf_op jit(solution)/shard_map/front/pallas_call | solution.py:823
  101.8 148.5 %middle.1 = (f32[5,224,384]{2,1,0:T(8,128)}, bf16[5,4,224,384]{3,2,1,0:T(8,128)(2,1)}, bf16[5,224,1536]{2,1,0:T(8,128)(2,1)}, bf16[5,224,1536]{2,1,0:T(8,128)(2,...) custom-call(bf16[5,224,384]{2,1,0:T(8,128)(2,1)} %get-tuple-element., ...), custom_call_target="tpu_custom_call" | custom-call | flops 30000001024 | bytes 48909312 | tf_op jit(solution)/shard_map/middle/pallas_call | solution.py:1079
  250.4 2.0 copy-done
  252.4 15.1 %shard_map.262.refs_5_ = bf16[8,4,192,1536]{3,2,1,0:T(8,128)(2,1)} custom-call(s32[1]{0:T(128)} %bitcast.18.refs_0_, bf16[5,4,224,384]{3,2,1,0:T(8,128)(2,1)S(1)} %copy-done, bf16[5,224,1536]{2,1,0:T(8,128)(2,1)} %get-tuple-element.46.refs_2_, bf16[5,4,224,384]{3,2,1,0:T(8,128)(2,1)} %get-tuple-element.42.refs_3_, ...), custom_call_target="tpu_custom_call" | custom-call | flops 8455716864 | bytes 32636928 | tf_op jit(solution)/shard_map/pallas_call | solution.py:1353
  267.5 7.0 %shard_map.263 = bf16[8,4,192,1536]{3,2,1,0:T(8,128)(2,1)} custom-call(s32[1]{0:T(128)} %bitcast.18.refs_0_, bf16[5,4,224,384]{3,2,1,0:T(8,128)(2,1)S(1)} %copy-done, bf16[5,224,1536]{2,1,0:T(8,128)(2,1)} %get-tuple-element.46.refs_2_, bf16[5,4,224,384]{3,2,1,0:T(8,128)(2,1)} %get-tuple-element.42.refs_3_, ...), custom_call_target="tpu_custom_call", output_to_operand_aliasing={{}: (5, {})} | custom-call | flops 2113929216 | bytes 51511296 | tf_op jit(solution)/shard_map/pallas_call | solution.py:1353
  274.4 83.5 %back.1 = (bf16[3,5,224,384]{3,2,1,0:T(8,128)(2,1)}, f32[5,224,384]{2,1,0:T(8,128)}, f32[5,224,384]{2,1,0:T(8,128)}, f32[5,3,384]{2,1,0:T(4,128)}, f32[5,3,384]{2,1,0:T(4,128)}) custom-call(bf16[3,5,224,384]{3,2,1,0:T(8,128)(2,1)} %get-tuple-element.40.refs_0_, bf16[5,224,384]{2,1,0:T(8,128)(2,1)} %get-tuple-element.41.refs_0_.refs_1_.refs_4_, ...), custom_call_target="tpu_custom_call" | custom-call | flops 40000000000 | bytes 30425088 | tf_op jit(solution)/shard_map/back/pallas_call | solution.py:1273
  358.0 1.7 copy-done.1
  359.7 9.4 %shard_map.264.refs_5_ = bf16[8,8,192,384]{3,2,1,0:T(8,128)(2,1)} custom-call(s32[1]{0:T(128)} %bitcast.18.refs_0_, bf16[5,4,224,384]{3,2,1,0:T(8,128)(2,1)} %get-tuple-element.58.refs_1_, bf16[3,5,224,384]{3,2,1,0:T(8,128)(2,1)S(1)} %copy-done.1, bf16[5,4,224,384]{3,2,1,0:T(8,128)(2,1)} %get-tuple-element.60.refs_3_, bf16[5,224,384]{2,1,0:T(8,128)(2,1)S(1)} %copy-done.2), custom_call_target="tpu_custom_call" | custom-call | flops 4227858432 | bytes 19759104 | tf_op jit(solution)/shard_map/pallas_call | solution.py:1353
  369.0 5.3 shard_map.265
  374.4 0.0 reduce-scatter.3.cloned.1.call-update
  374.4 0.0 copy-start.3
  374.4 0.0 reduce-scatter.5.cloned.1.call-start
  374.5 0.7 reduce-scatter.5.cloned.1.call-update
  375.2 0.9 slice.82
  376.1 0.8 slice_reduce_fusion.3
  377.0 14.5 %all_gather.4 = bf16[8,12,384]{2,1,0:T(8,128)(2,1)S(1)} all-gather(bf16[1,12,384]{2,1,0:T(8,128)(2,1)S(1)} %convert_element_type.74), channel_id=1, replica_groups=mesh['dp'=8,'tensor'=4] {'dp'}, dimensions={0}, use_global_device_ids=true | all-gather | bytes 82944 | tf_op jit(solution)/shard_map/all_gather | solution.py:1444
  391.5 0.5 convolution_bitcast_fusion
  392.0 0.8 collective-permute-start.2
  392.8 2.2 collective-permute-start.1
  395.0 0.5 collective-permute-start
  395.6 1.2 slice.77
  396.7 1.2 slice.79
  398.2 2.5 fusion
  400.6 27.7 %all-reduce.2 = (f32[1,2,3,384]{3,2,1,0:T(4,128)S(1)}, f32[1,2,384]{2,0,1:T(1,128)S(1)}, f32[1,2,1536]{2,1,0:T(2,128)}, f32[1,2,384]{2,1,0:T(2,128)}) all-reduce(f32[1,2,3,384]{3,2,1,0:T(4,128)S(1)} %maximum_bitcast_fusion, f32[1,2,384]{2,0,1:T(1,128)S(1)} %fusion.12, ...), channel_id=1, replica_groups=mesh['dp'=8,'tensor'=4] {'dp'}, use_global_device_ids=true, to_apply=%region_5.6 | all-reduce | flops 6912 | bytes 55296 | tf_op jit(solution)/shard_map/psum | solution.py:1453
  428.4 0.6 copy.63
  429.0 0.6 copy.64
  429.6 0.6 copy.62
  430.2 0.9 copy.60
  431.1 0.9 copy.61
  432.1 0.6 fusion.9
  432.7 39.9 %reduce-scatter.3.cloned.1.call-done = bf16[1,8,192,384]{3,2,1,0:T(8,128)(2,1)} async-done(((bf16[8,8,192,384]{3,2,1,0:T(8,128)(2,1)}), bf16[1,8,192,384]{3,2,1,0:T(8,128)(2,1)}) %reduce-scatter.3.cloned.1.call-update) | async-done | bytes 1179664 | tf_op jit(solution)/shard_map/reduce_scatter | solution.py:1433
  472.6 1.4 convert.21
  474.0 0.9 slice_bitcast_fusion.3
  474.9 1.3 slice_bitcast_fusion.2
  476.2 184.8 %reduce-scatter.5.cloned.1.call-done = bf16[1,4,192,1536]{3,2,1,0:T(8,128)(2,1)} async-done(((bf16[8,4,192,1536]{3,2,1,0:T(8,128)(2,1)}), bf16[1,4,192,1536]{3,2,1,0:T(8,128)(2,1)}) %reduce-scatter.5.cloned.1.call-update) | async-done | bytes 2359312 | tf_op jit(solution)/shard_map/reduce_scatter | solution.py:1426
  661.0 2.3 convert.22
  663.3 2.5 slice_bitcast_fusion
  (48 shorter events, 0.3 us)
Async XLA Ops:
  7.2 465.4 %reduce-scatter.3.cloned.1.call-start = ((), (), s32[]{:S(2)}) async-start(), calls=%async_computation.2 | async-start | bytes 10616832 | tf_op jit(solution)/shard_map/reduce_scatter | solution.py:1433
  250.4 2.0 copy-start
  274.4 83.5 %copy-start.2 = (bf16[5,224,384]{2,1,0:T(8,128)(2,1)S(1)}, bf16[5,224,384]{2,1,0:T(8,128)(2,1)}, u32[]{:S(2)}) copy-start(bf16[5,224,384]{2,1,0:T(8,128)(2,1)} %get-tuple-element.41.refs_0_.refs_1_.refs_4_) | copy-start | bytes 2580484
  358.0 1.7 copy-start.1
  374.4 0.8 copy-start.8
  374.4 17.1 %copy-start.3 = (bf16[1,2,192,6,384]{4,2,3,1,0:T(8,128)(2,1)S(1)}, bf16[1,2,192,6,384]{4,2,3,1,0:T(8,128)(2,1)}, u32[]{:S(2)}) copy-start(bf16[1,2,192,6,384]{4,2,3,1,0:T(8,128)(2,1)} %param.18) | copy-start | bytes 5308420
  374.4 21.1 %copy-start.5 = (f32[5,224,384]{2,1,0:T(8,128)S(1)}, f32[5,224,384]{2,1,0:T(8,128)}, u32[]{:S(2)}) copy-start(f32[5,224,384]{2,1,0:T(8,128)} %get-tuple-element.54) | copy-start | bytes 5160964
  374.4 286.6 %reduce-scatter.5.cloned.1.call-start = ((), (), s32[]{:S(2)}) async-start(), calls=%async_computation.3 | async-start | bytes 21233664 | tf_op jit(solution)/shard_map/reduce_scatter | solution.py:1426
  391.5 5.3 copy-start.4
  392.0 40.0 %collective-permute-start.2 = (f32[8,192]{1,0:T(8,128)S(1)}, f32[8,192]{1,0:T(8,128)S(1)}, u32[]{:S(2)}, u32[]{:S(2)}) collective-permute-start(f32[8,192]{1,0:T(8,128)S(1)} %convolution_bitcast_fusion), channel_id=1, source_target_pairs={{0,3},{1,2},{2,1},{3,0},{4,7},{5,6},{6,5},{7,4},{8,11},{9,10},{10,... | collective-permute-start | bytes 18440 | tf_op jit(solution)/shard_map/ppermute | solution.py:1450
  392.8 39.3 %collective-permute-start.1 = (f32[8,192]{1,0:T(8,128)S(1)}, f32[8,192]{1,0:T(8,128)S(1)}, u32[]{:S(2)}, u32[]{:S(2)}) collective-permute-start(f32[8,192]{1,0:T(8,128)S(1)} %convolution_bitcast_fusion), channel_id=1, source_target_pairs={{0,2},{1,3},{2,0},{3,1},{4,6},{5,7},{6,4},{7,5},{8,10},{9,11},{10,... | collective-permute-start | bytes 18440 | tf_op jit(solution)/shard_map/ppermute | solution.py:1450
  395.0 37.1 %collective-permute-start = (f32[8,192]{1,0:T(8,128)S(1)}, f32[8,192]{1,0:T(8,128)S(1)}, u32[]{:S(2)}, u32[]{:S(2)}) collective-permute-start(f32[8,192]{1,0:T(8,128)S(1)} %convolution_bitcast_fusion), channel_id=1, source_target_pairs={{0,1},{1,0},{2,3},{3,2},{4,5},{5,4},{6,7},{7,6},{8,9},{9,8},{10,11... | collective-permute-start | bytes 18440 | tf_op jit(solution)/shard_map/ppermute | solution.py:1450
  395.5 2.4 copy-start.10
  395.5 2.4 copy-start.9
  395.5 2.5 copy-start.7
  396.7 1.4 copy-start.6
Sparse Core Ops, SparseCore 0:
  374.5 98.0 reduce-scatter.2
  474.9 186.0 reduce-scatter.4

commit v2 on v1

--- a/solution.py
+++ b/solution.py
@@ -662,6 +662,81 @@
         return src[c] + dst[c, 0] + dst[c, 1] + dst[c, 2]
 
 
+class Column:
+    def __init__(self, chips, send, recv):
+        index = lax.axis_index("dp")
+        self.chips, self.z, self.core = chips, index // 2, index % 2
+        self.send_sem, self.recv_sem = send, recv
+        self.others = [((self.z + r) % chips) * 2 + self.core for r in range(1, chips)]
+
+    def copy(self, src, dst, kind, i, chip):
+        return pltpu.make_async_remote_copy(
+            src_ref=src,
+            dst_ref=dst,
+            send_sem=self.send_sem.at[kind, i],
+            recv_sem=self.recv_sem.at[kind, i],
+            device_id={"dp": chip * 2 + self.core},
+            device_id_type=MESH,
+        )
+
+    def hop(self, buf, kind, dist, way, behind):
+        step = 1 - 2 * way
+        origin = self.z - step * (dist + behind)
+        block = buf.at[origin]
+        return self.copy(block, block, kind, 2 * dist + way, self.z + step * (1 - behind))
+
+    def sends(self, dist, way):
+        if way == 0:
+            return (self.z >= dist) & (self.z < self.chips - 1)
+        return (self.z < self.chips - dist) & (self.z > 0)
+
+    def receives(self, dist, way):
+        return self.z > dist if way == 0 else self.z < self.chips - 1 - dist
+
+    def spread(self, buf, kind, dist):
+        for way in (0, 1):
+            if dist:
+
+                @pl.when(self.receives(dist - 1, way))
+                def _():
+                    self.hop(buf, kind, dist - 1, way, 1).wait_recv()
+
+            if dist < self.chips - 1:
+
+                @pl.when(self.sends(dist, way))
+                def _():
+                    self.hop(buf, kind, dist, way, 0).start()
+
+    def spread_sent(self, buf, kind):
+        for dist in range(self.chips - 1):
+            for way in (0, 1):
+
+                @pl.when(self.sends(dist, way))
+                def _():
+                    self.hop(buf, kind, dist, way, 0).wait_send()
+
+    def block_of(self, chip):
+        me = lax.axis_index("tensor")
+        return (chip % 2 + me % 2) % 2 + 2 * ((chip // 2 + me // 2) % 2)
+
+    def deal_copy(self, blocks, buf, kind, r, taken):
+        chip = (self.z + r) % self.chips
+        src = blocks.at[self.block_of(chip), pl.ds(0, taken), :]
+        return self.copy(src, buf.at[self.z], kind, r - 1, chip)
+
+    def deal(self, blocks, buf, kind, taken):
+        for r in range(1, self.chips):
+            self.deal_copy(blocks, buf, kind, r, taken).start()
+
+    def deal_own(self, blocks, buf, sem, taken):
+        src = blocks.at[self.block_of(self.z), pl.ds(0, taken), :]
+        return pltpu.make_async_copy(src, buf.at[self.z], sem)
+
+    def deal_wait(self, blocks, buf, kind, taken):
+        for r in range(1, self.chips):
+            self.deal_copy(blocks, buf, kind, r, taken).wait()
+
+
 def wait_sends(copies):
     for copy in copies:
         copy.wait_send()
@@ -685,12 +760,15 @@
 
 def front_kernel(dp, valid, refs_in, refs_out, scratch):
     x_ref, cot_ref, act_ref, modw_ref, modb_ref, wq_ref, bq_ref = refs_in
-    m_ref, qkv_ref, o_ref, lse_ref, g_ref, xp_ref, mod_ref, gsum_ref = refs_out
-    modw, wq, terms, got, k_all, aug, local, send, recv, msend, mrecv = scratch
+    m_ref, qkv_ref, o_ref, lse_ref, g_ref, xp_ref, mod_ref, gsum_ref, zm_ref = refs_out
+    modw, wq, terms, got, k_all, aug, local, send, recv, msend, mrecv, zsend, zrecv = scratch
     count, rows, feats = x_ref.shape
     cols = qkv_ref.shape[-1]
     width = 4 * feats
     links = Links(send, recv)
+    column = Column(dp // 2, zsend, zrecv)
+    taken = zm_ref.shape[1]
+    text = count - 1
     mine = lax.axis_index("dp")
     others = [(mine + r) % dp for r in range(1, dp)]
     load_mod = pltpu.make_async_copy(modw_ref, modw, local.at[0])
@@ -698,7 +776,7 @@
     load_mod.start()
     load_wq.start()
     links.enter(others)
-    for c in range(count):
+    for c in (text, *range(text)):
         links.gather_start(x_ref.at[c], xp_ref, 0, c)
     load_mod.wait()
     act = act_ref[...]
@@ -729,20 +807,21 @@
     ]
     for copy in mod_copies:
         copy.start()
-    for c in range(count):
+    for c in (text, *range(text)):
         links.gather_relay(x_ref.at[c], xp_ref, 0, c)
     for c in range(count):
         stream = c // (count - 1)
         g = (total[stream * 6 + 5 : stream * 6 + 6, :] * cot_ref[c].astype(F32)).astype(BF16)
         g_ref[c, 0] = g
         gsum_ref[c : c + 1, :] = jnp.sum(g.astype(F32), axis=0, keepdims=True)
-    for c in range(count):
+    for c in (text, *range(text)):
         links.gather_start(g_ref.at[c, 0], g_ref, 3, c)
     for copy in mod_copies:
         copy.wait_recv()
     load_wq.wait()
 
-    def project(c, carry):
+    def project(s, carry):
+        c = (s + text) % count
         stream = c // (count - 1)
         links.gather_finish(x_ref.at[c], xp_ref, 0, c)
         _, inv, centred = norm_stats([xp_ref[c, k].astype(F32) for k in range(4)], width)
@@ -758,6 +837,12 @@
         for j in range(3):
             qkv_ref[j, c] = (acc[j] + bq_ref[stream, j : j + 1, :]).astype(BF16)
         links.gather_relay(g_ref.at[c, 0], g_ref, 3, c)
+
+        @pl.when(s == 0)
+        def _():
+            column.deal(m_ref.at[text], zm_ref, 0, taken)
+            column.deal_own(m_ref.at[text], zm_ref, local.at[2], taken).start()
+
         return carry
 
     lax.fori_loop(0, count, project, 0)
@@ -799,9 +884,11 @@
         links.gather_sent(g_ref.at[c, 0], g_ref, 3, c)
     wait_sends(mod_copies)
     wait_sends(pushes)
-
-
-def front_call(dp, valid, x, cot, act, mod_w, mod_b, wq, bq):
+    column.deal_own(m_ref.at[text], zm_ref, local.at[2], taken).wait()
+    column.deal_wait(m_ref.at[text], zm_ref, 0, taken)
+
+
+def front_call(dp, valid, taken, x, cot, act, mod_w, mod_b, wq, bq):
     count, rows, feats = x.shape
     cols = wq.shape[-1]
     arrays = [x, cot, act, mod_w, mod_b, wq, bq]
@@ -814,6 +901,7 @@
         sds((count, 4, rows, feats), BF16),
         sds((4, 12, feats), F32),
         sds((count, feats), F32),
+        sds((dp // 2, taken, feats), BF16),
     ]
     n_in, n_out = len(arrays), len(outs)
 
@@ -824,7 +912,7 @@
         kernel,
         out_shape=outs,
         in_specs=[VMEM, VMEM, VMEM, ANY, VMEM, ANY, VMEM],
-        out_specs=[VMEM] * n_out,
+        out_specs=[VMEM] * (n_out - 1) + [ANY],
         scratch_shapes=[
             pltpu.VMEM(mod_w.shape, BF16),
             pltpu.VMEM(wq.shape, BF16),
@@ -832,11 +920,13 @@
             pltpu.VMEM((dp - 1, 12, feats), F32),
             pltpu.VMEM((valid, 128), BF16),
             pltpu.VMEM((2, valid, 128), BF16),
-            pltpu.SemaphoreType.DMA((2,)),
+            pltpu.SemaphoreType.DMA((3,)),
             pltpu.SemaphoreType.DMA((7, count)),
             pltpu.SemaphoreType.DMA((7, count)),
             pltpu.SemaphoreType.DMA((dp - 1,)),
             pltpu.SemaphoreType.DMA((dp - 1,)),
+            pltpu.SemaphoreType.DMA((1, dp // 2 - 1)),
+            pltpu.SemaphoreType.DMA((1, dp // 2 - 1)),
         ],
         compiler_params=pltpu.CompilerParams(
             collective_id=1, has_side_effects=True, vmem_limit_bytes=56 * MIB
@@ -849,15 +939,24 @@
 HB = 512
 
 
-def middle_kernel(refs_in, refs_out, scratch):
+def middle_kernel(chips, refs_in, refs_out, scratch):
     o_ref, x_ref, cot_ref, db2_ref, mod_ref, wo_ref, up_ref, down_ref, ub_ref, ob_ref = refs_in
-    x1_out, m2_out, a_out, du_out, b2_out, g1_out, g_ref, do_ref, line_ref, dub_ref = refs_out
+    x1_out, m2_out, a_out, du_out, b2_out, g1_out = refs_out[:6]
+    g_ref, do_ref, line_ref, dub_ref, zr_ref, zl_ref, zo_ref = refs_out[6:]
     (wo, up, down, db2, part, relayed, got, xp, branch, acc_m, acc_b, cols_s) = scratch[:12]
-    (x1_s, m2_s, a_s, du_s, b2_s, g1_s, srow, sgot, local, out_sem, send, recv) = scratch[12:]
+    (x1_s, m2_s, a_s, du_s, b2_s, g1_s, srow, sgot, local, out_sem, send, recv) = scratch[12:24]
+    zsend, zrecv, zlocal = scratch[24:]
     count, _, feats = x_ref.shape
     width = 4 * feats
     hidden = up.shape[-1]
     links = Links(send, recv)
+    column = Column(chips, zsend, zrecv)
+    text = count - 1
+    taken = zo_ref.shape[1]
+
+    def at(s):
+        return (s + text) % count
+
     loads = [
         pltpu.make_async_copy(src, dst, local.at[i])
         for i, (src, dst) in enumerate(
@@ -866,56 +965,113 @@
     ]
     for load in loads:
         load.start()
-    links.enter()
+    links.enter(column.others)
     loads[0].wait()
 
-    def flush(staged, out, kind, c):
-        return pltpu.make_async_copy(staged.at[c % 2], out.at[c], out_sem.at[kind, c % 2])
-
-    def project(c):
+    def flush(staged, out, kind, s):
+        return pltpu.make_async_copy(staged.at[s % 2], out.at[at(s)], out_sem.at[kind, s % 2])
+
+    first_rows = pl.ds(0, taken)
+
+    def own_rights():
+        return [
+            pltpu.make_async_copy(
+                du_s.at[0, first_rows, :], zr_ref.at[column.z, 0], zlocal.at[0]
+            ),
+            pltpu.make_async_copy(a_s.at[0, first_rows, :], zr_ref.at[column.z, 1], zlocal.at[1]),
+            column.deal_own(m2_s.at[0], zl_ref.at[0], zlocal.at[2], taken),
+        ]
+
+    def own_early():
+        return [
+            pltpu.make_async_copy(o_ref.at[text, first_rows, :], zo_ref.at[column.z], zlocal.at[3]),
+            column.deal_own(db2.at[text], zl_ref.at[1], zlocal.at[4], taken),
+        ]
+
+    def column_early(s):
+        @pl.when(s == 0)
+        def _():
+            loads[3].wait()
+            for copy in own_early():
+                copy.start()
+            column.deal(db2.at[text], zl_ref.at[1], 3, taken)
+            for copy in own_early():
+                copy.wait()
+            column.spread(zo_ref, 1, 0)
+
+    def column_start(s):
+        @pl.when(s == 0)
+        def _():
+            for copy in own_rights():
+                copy.wait()
+            flush(m2_s, m2_out, 1, 0).wait()
+            column.spread(zr_ref, 0, 0)
+            column.deal(m2_out.at[text], zl_ref.at[0], 2, taken)
+            column.spread(zo_ref, 1, 1)
+
+    def column_relay(dist):
+        def step(s):
+            @pl.when(s == 0)
+            def _():
+                column.spread(zr_ref, 0, dist)
+                if dist == 1:
+                    column.spread(zo_ref, 1, 2)
+
+        return step
+
+    def project(s):
+        c = at(s)
         stream = c // (count - 1)
         o = o_ref[c]
         for k in (3, 1, 2, 0):
             part[c, k] = nt_dot(o, wo[stream, links.peers[k]]).astype(BF16)
         links.scatter_start(part, relayed, got, 0, c)
 
-    def first_relay(c):
+    def first_relay(s):
+        c = at(s)
         links.scatter_relay(part, relayed, got, 0, c)
 
-    def residual(c):
+    def residual(s):
+        c = at(s)
         stream = c // (count - 1)
         total = links.scatter_finish(part, relayed, got, 0, c)
         add = total + ob_ref[pl.ds(stream, 1), :]
         branch[c] = add
         moved = x_ref[c].astype(F32) + mod_ref[0, pl.ds(stream * 6 + 2, 1), :] * add
 
-        @pl.when(c >= 2)
+        @pl.when(s >= 2)
         def _():
-            flush(x1_s, x1_out, 0, c - 2).wait()
-
-        x1_s[c % 2] = moved
-        flush(x1_s, x1_out, 0, c).start()
+            flush(x1_s, x1_out, 0, s - 2).wait()
+
+        x1_s[s % 2] = moved
+        flush(x1_s, x1_out, 0, s).start()
         xp[c, 0] = moved.astype(BF16)
         links.gather_start(xp.at[c, 0], xp, 3, c)
 
-    def second_relay(c):
+    def second_relay(s):
+        c = at(s)
         links.gather_relay(xp.at[c, 0], xp, 3, c)
 
-    def feed_forward(c):
+    def feed_forward(s):
+        c = at(s)
         stream = c // (count - 1)
-        slot = c % 2
-
-        @pl.when(c == 0)
+        slot = s % 2
+
+        @pl.when(s == 0)
         def _():
-            for load in loads[1:]:
+            for load in loads[1:3]:
                 load.wait()
 
-        @pl.when(c >= 2)
+        @pl.when(s >= 2)
         def _():
             for kind, (staged, out) in enumerate(
-                [(m2_s, m2_out), (a_s, a_out), (du_s, du_out), (b2_s, b2_out)]
+                [(a_s, a_out), (du_s, du_out), (b2_s, b2_out)]
             ):
-                flush(staged, out, kind + 1, c - 2).wait()
+                flush(staged, out, kind + 2, s - 2).wait()
+
+        @pl.when(s >= 3)
+        def _():
+            flush(m2_s, m2_out, 1, s - 2).wait()
 
         links.gather_finish(xp.at[c, 0], xp, 3, c)
         links.scatter_sent(part, relayed, got, 0, c)
@@ -980,12 +1136,19 @@
         for kind, (staged, out) in enumerate(
             [(m2_s, m2_out), (a_s, a_out), (du_s, du_out), (b2_s, b2_out)]
         ):
-            flush(staged, out, kind + 1, c).start()
-
-    def third_relay(c):
+            flush(staged, out, kind + 1, s).start()
+
+        @pl.when(s == 0)
+        def _():
+            for copy in own_rights():
+                copy.start()
+
+    def third_relay(s):
+        c = at(s)
         links.scatter_relay(part, relayed, got, 6, c)
 
-    def norm_back(c):
+    def norm_back(s):
+        c = at(s)
         stream = c // (count - 1)
         total = links.scatter_finish(part, relayed, got, 6, c)
         sums = exact_tn(links.rows_finish(srow, sgot, 12, c), eye_rows())
@@ -999,21 +1162,23 @@
         g_ref[c, 0] = db
         links.gather_start(g_ref.at[c, 0], g_ref, 9, c)
 
-        @pl.when(c >= 2)
+        @pl.when(s >= 2)
         def _():
-            flush(g1_s, g1_out, 5, c - 2).wait()
-
-        g1_s[c % 2] = g
-        flush(g1_s, g1_out, 5, c).start()
+            flush(g1_s, g1_out, 5, s - 2).wait()
+
+        g1_s[s % 2] = g
+        flush(g1_s, g1_out, 5, s).start()
         line_ref[c, 0:1, :] = jnp.sum(total, axis=0, keepdims=True)
         line_ref[c, 1:2, :] = jnp.sum(total * normed, axis=0, keepdims=True)
         line_ref[c, 2:3, :] = jnp.sum(branch[c] * g, axis=0, keepdims=True)
         line_ref[c, 3:4, :] = jnp.sum(db.astype(F32), axis=0, keepdims=True)
 
-    def fourth_relay(c):
+    def fourth_relay(s):
+        c = at(s)
         links.gather_relay(g_ref.at[c, 0], g_ref, 9, c)
 
-    def head_grads(c):
+    def head_grads(s):
+        c = at(s)
         stream = c // (count - 1)
         links.gather_finish(g_ref.at[c, 0], g_ref, 9, c)
         acc = None
@@ -1032,10 +1197,20 @@
             (6, norm_back),
             (2, residual),
             (0, project),
+            (1, column_early),
+            (5, column_start),
+            (7, column_relay(1)),
+            (9, column_relay(2)),
             (8, head_grads),
             (4, feed_forward),
         ],
     )
+    column.spread(zr_ref, 0, chips - 1)
+    column.spread(zo_ref, 1, chips - 1)
+    column.deal_wait(m2_out.at[text], zl_ref.at[0], 2, taken)
+    column.deal_wait(db2.at[text], zl_ref.at[1], 3, taken)
+    column.spread_sent(zr_ref, 0)
+    column.spread_sent(zo_ref, 1)
     for c in range(count):
         links.gather_sent(xp.at[c, 0], xp, 3, c)
         links.scatter_sent(part, relayed, got, 6, c)
@@ -1055,7 +1230,7 @@
             flush(staged, out, kind, c).wait()
 
 
-def middle_call(o, x, cot, db2, mods, wo, up, down, ub, ob):
+def middle_call(dp, taken, o, x, cot, db2, mods, wo, up, down, ub, ob):
     count, rows, feats = x.shape
     cols, hidden = wo.shape[-1], up.shape[-1]
     arrays = [o, x, cot, db2, mods, wo, up, down, ub, ob]
@@ -1070,17 +1245,20 @@
         sds((count, rows, cols), BF16),
         sds((count, 4, feats), F32),
         sds((count, hidden), F32),
+        sds((dp // 2, 2, taken, hidden), BF16),
+        sds((2, dp // 2, taken, feats), BF16),
+        sds((dp // 2, taken, cols), BF16),
     ]
     n_in, n_out = len(arrays), len(outs)
 
     def kernel(*refs):
-        middle_kernel(refs[:n_in], refs[n_in : n_in + n_out], refs[n_in + n_out :])
+        middle_kernel(dp // 2, refs[:n_in], refs[n_in : n_in + n_out], refs[n_in + n_out :])
 
     return pl.pallas_call(
         kernel,
         out_shape=outs,
         in_specs=[VMEM, VMEM, VMEM, ANY, VMEM, ANY, ANY, ANY, VMEM, VMEM],
-        out_specs=[ANY] * 6 + [VMEM] * 4,
+        out_specs=[ANY] * 6 + [VMEM] * 4 + [ANY] * 3,
         scratch_shapes=[
             pltpu.VMEM(wo.shape, BF16),
             pltpu.VMEM(up.shape, BF16),
@@ -1106,6 +1284,9 @@
             pltpu.SemaphoreType.DMA((6, 2)),
             pltpu.SemaphoreType.DMA((15, count)),
             pltpu.SemaphoreType.DMA((15, count)),
+            pltpu.SemaphoreType.DMA((4, dp - 2)),
+            pltpu.SemaphoreType.DMA((4, dp - 2)),
+            pltpu.SemaphoreType.DMA((5,)),
         ],
         compiler_params=pltpu.CompilerParams(
             collective_id=2, has_side_effects=True, vmem_limit_bytes=63 * MIB
@@ -1115,21 +1296,38 @@
     )(*arrays)
 
 
-def back_kernel(valid, blocks, refs_in, refs_out, scratch):
+def back_kernel(chips, valid, blocks, refs_in, refs_out, scratch):
     qkv_ref, o_ref, do_ref, lse_ref, b2_ref, x1_ref, cot_ref, g1_ref, xp_ref, mod_ref = refs_in[:10]
-    wq_ref, db_ref = refs_in[10:]
-    dqkv_ref, x2_ref, grad_ref, line_ref, bias_ref = refs_out
+    wq_ref, db_ref, db1_ref = refs_in[10:]
+    dqkv_ref, x2_ref, grad_ref, line_ref, bias_ref, zq_ref, zd_ref = refs_out
     wq, q_all, k_all, v_all, do_all, lse_all, od_all, dk_all, dv_all, dqt_all, dq_all = scratch[:11]
-    part, relayed, got, relayed2, got2, cols_s, srow, sgot, local, send, recv = scratch[11:]
+    part, relayed, got, relayed2, got2, cols_s, srow, sgot, local, send, recv = scratch[11:22]
+    zsend, zrecv = scratch[22:]
     count, rows, feats = cot_ref.shape
     cols = o_ref.shape[-1]
     width = 4 * feats
     links = Links(send, recv)
+    column = Column(chips, zsend, zrecv)
+    text = count - 1
+    taken = zd_ref.shape[1]
     load = pltpu.make_async_copy(wq_ref, wq, local.at[0])
     load.start()
-    links.enter()
+    links.enter(column.others)
     for c in range(count):
         links.scatter_start(b2_ref, relayed2, got2, 0, c)
+    own_db = pltpu.make_async_copy(
+        db1_ref.at[text, column.block_of(column.z), pl.ds(0, taken), :],
+        zd_ref.at[column.z],
+        local.at[1],
+    )
+    own_db.start()
+    column.deal(db1_ref.at[text], zd_ref, 1, taken)
+    own_q = [
+        pltpu.make_async_copy(
+            dqkv_ref.at[j, text, pl.ds(0, taken), :], zq_ref.at[column.z, j], local.at[2 + j]
+        )
+        for j in range(3)
+    ]
     scale = jnp.asarray(HEAD_DIM**-0.5, BF16)
     head_row = lax.broadcasted_iota(jnp.int32, (8, 128), 0)
     lane = lax.broadcasted_iota(jnp.int32, (8, 128), 1)
@@ -1195,7 +1393,20 @@
         return carry
 
     lax.fori_loop(0, cols // 128, heads_pair, 0)
+    for copy in own_q:
+        copy.start()
     load.wait()
+
+    def column_step(dist):
+        def step(c):
+            @pl.when(c == 0)
+            def _():
+                if dist == 0:
+                    for copy in own_q:
+                        copy.wait()
+                column.spread(zq_ref, 0, dist)
+
+        return step
 
     def input_grads(c):
         stream = c // (count - 1)
@@ -1244,37 +1455,54 @@
         line_ref[c, 0:1, :] = jnp.sum(total, axis=0, keepdims=True)
         line_ref[c, 1:2, :] = jnp.sum(total * normed, axis=0, keepdims=True)
 
-    stages(count, [(1, last_relay), (0, input_grads), (2, norm_back), (1, out_stream)])
+    stages(
+        count,
+        [
+            (1, last_relay),
+            (0, column_step(0)),
+            (2, column_step(1)),
+            (4, column_step(2)),
+            (0, input_grads),
+            (2, norm_back),
+            (1, out_stream),
+        ],
+    )
+    column.spread(zq_ref, 0, chips - 1)
+    column.spread_sent(zq_ref, 0)
+    own_db.wait()
+    column.deal_wait(db1_ref.at[text], zd_ref, 1, taken)
     for c in range(count):
         links.scatter_sent(b2_ref, relayed2, got2, 0, c)
         links.scatter_sent(part, relayed, got, 3, c)
         wait_sends(links.rows_copies(srow, sgot, 6, c))
 
 
-def back_call(valid, qkv, o, do, lse, b2, x1, cot, g1, xp, mods, wq, down_b):
+def back_call(dp, valid, taken, qkv, o, do, lse, b2, x1, cot, g1, xp, mods, wq, down_b, db1):
     count, rows, feats = cot.shape
     cols = o.shape[-1]
     padded = -(-valid // 128) * 128
     step = -(-valid // 3 // 16) * 16
     blocks = [(b, min(step, valid - b)) for b in range(0, valid, step)]
-    arrays = [qkv, o, do, lse, b2, x1, cot, g1, xp, mods, wq, down_b]
+    arrays = [qkv, o, do, lse, b2, x1, cot, g1, xp, mods, wq, down_b, db1]
     outs = [
         sds(qkv.shape, BF16),
         sds((count, rows, feats), F32),
         sds((count, rows, feats), F32),
         sds((count, 3, feats), F32),
         sds((count, 3, cols), F32),
+        sds((dp // 2, 3, taken, cols), BF16),
+        sds((dp // 2, taken, feats), BF16),
     ]
     n_in, n_out = len(arrays), len(outs)
 
     def kernel(*refs):
-        back_kernel(valid, blocks, refs[:n_in], refs[n_in : n_in + n_out], refs[n_in + n_out :])
+        back_kernel(dp // 2, valid, blocks, refs[:n_in], refs[n_in : n_in + n_out], refs[n_in + n_out :])
 
     return pl.pallas_call(
         kernel,
         out_shape=outs,
-        in_specs=[VMEM] * 10 + [ANY, VMEM],
-        out_specs=[VMEM] * n_out,
+        in_specs=[VMEM] * 10 + [ANY, VMEM, ANY],
+        out_specs=[VMEM] * (n_out - 2) + [ANY] * 2,
         scratch_shapes=[pltpu.VMEM(wq.shape, BF16)]
         + [pltpu.VMEM((valid, 128), BF16)] * 4
         + [pltpu.VMEM((valid, 128), F32)] * 4
@@ -1289,9 +1517,11 @@
             pltpu.VMEM((count, rows, 128), F32),
             pltpu.VMEM((count, 8, rows), F32),
             pltpu.VMEM((count, 3, 8, rows), F32),
-            pltpu.SemaphoreType.DMA((1,)),
+            pltpu.SemaphoreType.DMA((5,)),
             pltpu.SemaphoreType.DMA((9, count)),
             pltpu.SemaphoreType.DMA((9, count)),
+            pltpu.SemaphoreType.DMA((2, dp - 2)),
+            pltpu.SemaphoreType.DMA((2, dp - 2)),
         ],
         compiler_params=pltpu.CompilerParams(
             collective_id=3, has_side_effects=True, vmem_limit_bytes=63 * MIB
@@ -1320,10 +1550,9 @@
             slot += 1
 
 
-def wgrad_call(base, pairs, into, stream, dp):
+def wgrad_call(base, pairs, dp):
     count, _, rows, feats = pairs[0][0].shape
-    chunks = 1 if stream else count - 1
-    first = (count - 1) if stream else 0
+    chunks = count - 1
     cols = pairs[0][1].shape[-1]
     split = dp // 4
     groups = [right.shape[0] if right.ndim == 4 else 1 for _, right in pairs]
@@ -1331,21 +1560,12 @@
     arrays, specs = [], []
     for (left, right), g in zip(pairs, groups):
         arrays += [left, right]
-        specs.append(
-            pl.BlockSpec((chunks, 1, rows, feats), lambda k, t: (first // chunks, k, 0, 0))
-        )
+        specs.append(pl.BlockSpec((chunks, 1, rows, feats), lambda k, t: (0, k, 0, 0)))
         if g > 1:
-            specs.append(
-                pl.BlockSpec((g, chunks, rows, cols), lambda k, t: (0, first // chunks, 0, 0))
-            )
+            specs.append(pl.BlockSpec((g, chunks, rows, cols), lambda k, t: (0, 0, 0, 0)))
         else:
-            specs.append(pl.BlockSpec((chunks, rows, cols), lambda k, t: (first // chunks, 0, 0)))
-    out = sds((dp, 2 * slots, feats // split, cols), BF16)
-    aliases = {}
-    if into is not None:
-        aliases = {1 + len(arrays): 0}
-        arrays.append(into)
-        specs.append(ANY)
+            specs.append(pl.BlockSpec((chunks, rows, cols), lambda k, t: (0, 0, 0)))
+    out = sds((dp, slots, feats // split, cols), BF16)
 
     def kernel(*refs):
         wgrad_kernel(groups, split, *refs)
@@ -1359,16 +1579,136 @@
             in_specs=specs,
             out_specs=[
                 pl.BlockSpec(
-                    (split, slots, feats // split, cols), lambda k, t: (t[0] ^ k, stream, 0, 0)
+                    (split, slots, feats // split, cols), lambda k, t: (t[0] ^ k, 0, 0, 0)
                 )
             ],
         ),
-        input_output_aliases=aliases,
         compiler_params=pltpu.CompilerParams(
             dimension_semantics=("arbitrary",), vmem_limit_bytes=48 * MIB
         ),
         cost_estimate=cost(2 * 4 * feats * slots * cols * chunks * rows, arrays, [out]),
     )(base, *arrays)[0]
+
+
+def text_kernel(refs_in, refs_out, scratch):
+    zm_ref, zl_ref, zd_ref, zq_ref, zr_ref, zo_ref = refs_in
+    at_ref, ff_ref = refs_out
+    send_a, got_a, send_f, got_f, keep_a, keep_f, send, recv = scratch
+    index = lax.axis_index("dp")
+    core = index % 2
+    partner = index + 1 - 2 * core
+    barrier = pltpu.get_barrier_semaphore()
+    pl.semaphore_signal(barrier, inc=1, device_id={"dp": partner}, device_id_type=MESH)
+    pl.semaphore_wait(barrier, 1)
+    half = at_ref.shape[1]
+
+    def move(src, dst, i):
+        return pltpu.make_async_remote_copy(
+            src_ref=src.at[i],
+            dst_ref=dst.at[i],
+            send_sem=send.at[i if src is send_a else 4 + i],
+            recv_sem=recv.at[i if src is send_a else 4 + i],
+            device_id={"dp": partner},
+            device_id_type=MESH,
+        )
+
+    work = [
+        (zl_ref.at[0], zr_ref.at[:, 0], keep_f, send_f, got_f, ff_ref, 0),
+        (zl_ref.at[1], zr_ref.at[:, 1], keep_f, send_f, got_f, ff_ref, 1),
+        (zm_ref, zq_ref.at[:, 0], keep_a, send_a, got_a, at_ref, 0),
+        (zm_ref, zq_ref.at[:, 1], keep_a, send_a, got_a, at_ref, 1),
+        (zm_ref, zq_ref.at[:, 2], keep_a, send_a, got_a, at_ref, 2),
+        (zd_ref, zo_ref, keep_a, send_a, got_a, at_ref, 3),
+    ]
+    for left, right, keep, out, got, _, i in work:
+        keep[i] = tn_dot(flat(left[...]), flat(right[...]))
+        out[i] = keep[i, pl.ds((1 - core) * half, half), :].astype(BF16)
+        move(out, got, i).start()
+    for left, right, keep, out, got, final, i in work:
+        move(out, got, i).wait_recv()
+        final[i] = keep[i, pl.ds(core * half, half), :] + got[i].astype(F32)
+    for left, right, keep, out, got, final, i in work:
+        move(out, got, i).wait_send()
+
+
+def text_call(zm, zl, zd, zq, zr, zo):
+    feats, cols, hidden = zm.shape[-1], zq.shape[-1], zr.shape[-1]
+    half = feats // 2
+    arrays = [zm, zl, zd, zq, zr, zo]
+    outs = [sds((4, half, cols), F32), sds((2, half, hidden), F32)]
+
+    def kernel(*refs):
+        text_kernel(refs[:6], refs[6:8], refs[8:])
+
+    return pl.pallas_call(
+        kernel,
+        out_shape=outs,
+        in_specs=[VMEM] * 6,
+        out_specs=[VMEM] * 2,
+        scratch_shapes=[
+            pltpu.VMEM((4, half, cols), BF16),
+            pltpu.VMEM((4, half, cols), BF16),
+            pltpu.VMEM((2, half, hidden), BF16),
+            pltpu.VMEM((2, half, hidden), BF16),
+            pltpu.VMEM((4, feats, cols), F32),
+            pltpu.VMEM((2, feats, hidden), F32),
+            pltpu.SemaphoreType.DMA((6,)),
+            pltpu.SemaphoreType.DMA((6,)),
+        ],
+        compiler_params=pltpu.CompilerParams(
+            collective_id=4, has_side_effects=True, vmem_limit_bytes=40 * MIB
+        ),
+        cost_estimate=cost(6 * 10**9, arrays, outs),
+        name="dw_text",
+    )(*arrays)
+
+
+def rows_kernel(dp, row_ref, all_ref, sum_ref, send, recv):
+    mine = lax.axis_index("dp")
+    others = [(mine + r) % dp for r in range(1, dp)]
+    barrier = pltpu.get_barrier_semaphore()
+    for peer in others:
+        pl.semaphore_signal(barrier, inc=1, device_id={"dp": peer}, device_id_type=MESH)
+    pl.semaphore_wait(barrier, dp - 1)
+    copies = [
+        pltpu.make_async_remote_copy(
+            src_ref=row_ref,
+            dst_ref=all_ref.at[mine],
+            send_sem=send.at[r],
+            recv_sem=recv.at[r],
+            device_id={"dp": peer},
+            device_id_type=MESH,
+        )
+        for r, peer in enumerate(others)
+    ]
+    for copy in copies:
+        copy.start()
+    all_ref[mine] = row_ref[...]
+    for copy in copies:
+        copy.wait()
+    total = all_ref[0]
+    for s in range(1, dp):
+        total = total + all_ref[s]
+    sum_ref[...] = total
+
+
+def rows_call(dp, rows):
+    outs = [sds((dp,) + rows.shape, F32), sds(rows.shape, F32)]
+    return pl.pallas_call(
+        functools.partial(rows_kernel, dp),
+        out_shape=outs,
+        in_specs=[VMEM],
+        out_specs=[VMEM] * 2,
+        scratch_shapes=[
+            pltpu.SemaphoreType.DMA((dp - 1,)),
+            pltpu.SemaphoreType.DMA((dp - 1,)),
+        ],
+        compiler_params=pltpu.CompilerParams(
+            collective_id=5, has_side_effects=True, vmem_limit_bytes=16 * MIB
+        ),
+        cost_estimate=cost(10**6, [rows], outs),
+        name="rows",
+    )(rows)
 
 
 def fast_body(
@@ -1414,24 +1754,24 @@
     up_w = up_weight[0].reshape(2, 4, feats, -1)
     down_w = down_weight[0].reshape(2, 4, feats, -1)
 
-    m, qkv, o, lse, db2, xp, mods, db2_sum = front_call(
-        dp, valid, x, cot, cond_act, mod_w, mod_b, qkv_w, qkv_bias[0].astype(F32)
-    )
-    x1, m2, act, du, b2, g1, db1, do, lines2, du_sum = middle_call(
-        o, x, cot, db2, mods, out_w, up_w, down_w, up_bias[0].astype(F32), out_bias[0].astype(F32)
-    )
-    part = wgrad_call(base, [(m2, du), (db2, act)], None, 0, dp)
-    part = wgrad_call(base, [(m2, du), (db2, act)], part, 1, dp)
+    taken = -(-texts // 16) * 16
+    m, qkv, o, lse, db2, xp, mods, db2_sum, zm = front_call(
+        dp, valid, taken, x, cot, cond_act, mod_w, mod_b, qkv_w, qkv_bias[0].astype(F32)
+    )
+    up_b, out_b, down_b = (b[0].astype(F32) for b in (up_bias, out_bias, down_bias))
+    x1, m2, act, du, b2, g1, db1, do, lines2, du_sum, zr, zl, zo = middle_call(
+        dp, taken, o, x, cot, db2, mods, out_w, up_w, down_w, up_b, out_b
+    )
+    part = wgrad_call(base, [(m2, du), (db2, act)], dp)
     do, part = lax.optimization_barrier((do, part))
     ff_sum = lax.psum_scatter(part, "dp", scatter_dimension=0, tiled=True)
-    ff_grad = ff_sum[0].astype(F32)
-    dqkv, x2, grad, lines1, qkv_sum = back_call(
-        valid, qkv, o, do, lse, b2, x1, cot, g1, xp, mods, qkv_w, down_bias[0].astype(F32)
-    )
-    part2 = wgrad_call(base, [(m, dqkv), (db1, o)], None, 0, dp)
-    part2 = wgrad_call(base, [(m, dqkv), (db1, o)], part2, 1, dp)
+    dqkv, x2, grad, lines1, qkv_sum, zq, zd = back_call(
+        dp, valid, taken, qkv, o, do, lse, b2, x1, cot, g1, xp, mods, qkv_w, down_b, db1
+    )
+    part2 = wgrad_call(base, [(m, dqkv), (db1, o)], dp)
+    part2, zq = lax.optimization_barrier((part2, zq))
     at_sum = lax.psum_scatter(part2, "dp", scatter_dimension=0, tiled=True)
-    at_grad = at_sum[0].astype(F32)
+    at_text, ff_text = text_call(zm, zl, zd, zq, zr, zo)
 
     def by_stream(value):
         return jnp.stack([jnp.sum(value[:4], axis=0), value[4]])
@@ -1440,28 +1780,37 @@
     mod_rows = jnp.stack(
         [late[:, 0], late[:, 1], early[:, 2], early[:, 0], early[:, 1], late[:, 2]], axis=1
     )
-    mod_grad = mod_rows.reshape(12, feats).astype(BF16)
-    all_mod = lax.all_gather(mod_grad, "dp", axis=0)
+    mod_rows = mod_rows.reshape(12, feats).astype(BF16).astype(F32)
+    every = [
+        mod_rows,
+        by_stream(qkv_sum).reshape(6, feats),
+        early[:, 3],
+        by_stream(du_sum).reshape(8, feats),
+        by_stream(db2_sum),
+        jnp.zeros((2, feats), F32),
+    ]
+    all_rows, row_sums = rows_call(dp, jnp.concatenate(every, axis=0))
+    all_mod = all_rows[:, :12].astype(BF16)
     mod_wgrad = jnp.einsum("sc,sgd->gcd", cond_act, all_mod, preferred_element_type=F32)
     mod_wgrad = jnp.transpose(mod_wgrad.reshape(1, 2, 6, -1, feats), (0, 1, 3, 2, 4))
-    mod_bgrad = jnp.sum(all_mod.astype(F32), axis=0).reshape(1, 2, 6, feats)
     act_part = jnp.einsum("sgd,gcd->sc", all_mod, mod_w, preferred_element_type=F32)
     act_total = act_part + sum(
         lax.ppermute(act_part, "tensor", [(i, i ^ k) for i in range(4)]) for k in (1, 2, 3)
     )
     cond_grad = jax.vjp(jax.nn.silu, cond_float)[1](act_total)[0]
-    biases = lax.psum(
-        (
-            by_stream(qkv_sum)[None],
-            early[None, :, 3],
-            by_stream(du_sum)[None],
-            by_stream(db2_sum)[None],
-        ),
-        "dp",
-    )
-    at_grad = at_grad.reshape((2, 4) + at_grad.shape[1:])
-    ff_grad = ff_grad.reshape((2, 2) + ff_grad.shape[1:])
-    qkv_wgrad = jnp.transpose(at_grad[None, :, :3], (0, 1, 3, 2, 4))
+    mod_bgrad = row_sums[:12].reshape(1, 2, 6, feats)
+    biases = (
+        row_sums[12:18].reshape(1, 2, 3, feats),
+        row_sums[18:20][None],
+        row_sums[20:28].reshape(1, 2, 4 * feats),
+        row_sums[28:30][None],
+    )
+    at_image, ff_image = at_sum[0].astype(F32), ff_sum[0].astype(F32)
+    qkv_wgrad = jnp.transpose(jnp.stack([at_image[:3], at_text[:3]])[None], (0, 1, 3, 2, 4))
+
+    def streams(image, text):
+        return jnp.stack([image, text])[None]
+
     image_out, text_out = parted(x2)
     image_grad, text_grad = parted(grad)
     return (
@@ -1474,18 +1823,19 @@
         mod_bgrad,
         qkv_wgrad,
         biases[0],
-        at_grad[None, :, 3],
+        streams(at_image[3], at_text[3]),
         biases[1],
-        ff_grad[None, :, 0],
+        streams(ff_image[0], ff_text[0]),
         biases[2],
-        ff_grad[None, :, 1],
+        streams(ff_image[1], ff_text[1]),
         biases[3],
     )
 
 
 def solution(mesh):
     dp, tensor = mesh.shape["dp"], mesh.shape["tensor"]
-    chosen = functools.partial(fast_body, dp) if tensor == 4 else plain_body
+    square = dp == 8 and tensor == 4
+    chosen = functools.partial(fast_body, dp) if square else plain_body
     return jax.shard_map(
         chosen,
         mesh=mesh,

time: 674 us -> 542 us (0.80)
  waiting for transfers between devices: 225 us -> 101 us
  blocking collectives: 42.2 us -> 0 us
  Pallas kernels: 351 us -> 367 us
  local copies, waits for them, and re-layouts: 18.6 us -> 29.7 us
    reduce_scatter x1, waiting for transfers between devices: 185 us -> 97.9 us  [fast_body(): ff_sum = lax.psum_scatter(part, 'dp', scatter_dimension=0, tiled=True)]
    reduce_scatter x1, waiting for transfers between devices: 39.9 us -> 2.66 us  [fast_body(): at_sum = lax.psum_scatter(part2, 'dp', scatter_dimension=0, tiled=True)]
    psum x1 -> x0, blocking collectives: 27.7 us -> none  [fast_body(): lax.psum((by_stream(qkv_sum)[None], early[None, :, 3], by_stream(du_sum)[...]
    pallas_call x1 -> x3, Pallas kernels: 83.5 us -> 107 us  [the longest x1 84.5 us: back_call(): pl.pallas_call(kernel, out_shape=outs, in_specs=[VMEM] * 10 + [ANY, VMEM,...]
    all_gather x1 -> x0, blocking collectives: 14.5 us -> none  [fast_body(): all_mod = lax.all_gather(mod_grad, 'dp', axis=0)]
    pallas_call x4 -> x2, Pallas kernels: 36.7 us -> 24.5 us  [wgrad_call(): pl.pallas_call(kernel, out_shape=[out], grid_spec=pltpu.PrefetchScalarGri...]
  transfers between devices with their start and end apart: 5 -> 5, of which waited for: 2 -> 2; matrix products, arithmetic and copies ran while one was open for 2% -> 5% of each run, Pallas kernels for 0% -> 4%
where the time goes in v2:
time: 542 us; the launch traced here: 541 us
  Pallas kernels  367 us (68%)
  waiting for transfers between devices  101 us (19%)
  local copies, waits for them, and re-layouts  29.7 us (5%)
  other arithmetic  19.8 us (4%)
  between operations  14.5 us (3%)
    pallas_call x1, Pallas kernels, middle_call(): pl.pallas_call(kernel, out_shape=outs, in_specs=[VMEM, VMEM, VMEM, ANY, V...  151 us
    reduce_scatter x1, waiting for transfers between devices, fast_body(): ff_sum = lax.psum_scatter(part, 'dp', scatter_dimension=0, tiled=True)  97.9 us
    pallas_call x1, Pallas kernels, back_call(): pl.pallas_call(kernel, out_shape=outs, in_specs=[VMEM] * 10 + [ANY, VMEM,...  84.5 us
    pallas_call x1, Pallas kernels, front_call(): pl.pallas_call(kernel, out_shape=outs, in_specs=[VMEM, VMEM, VMEM, ANY, V...  84.4 us
    pallas_call x2, Pallas kernels, wgrad_call(): pl.pallas_call(kernel, out_shape=[out], grid_spec=pltpu.PrefetchScalarGri...  24.5 us
    pallas_call x1, Pallas kernels, rows_call(): pl.pallas_call(functools.partial(rows_kernel, dp), out_shape=outs, in_spe...  16.5 us
    unnamed x36, local copies, waits for them, and re-layouts  12.8 us
  transfers between devices with their start and end apart: 5, of which 2 were waited for; matrix products, arithmetic and copies ran while one was open for 5% of the time, Pallas kernels for 4%

profile of v2, /device:TPU:0, one launch (start us, length us, event | category | flops | bytes accessed | tf_op | source)
XLA Modules:
  0.0 540.7 jit_solution(3181017516084154045)
XLA Ops:
  7.2 1.3 bitcast_convert_fusion.3.refs_9_
  8.5 1.3 bitcast_convert_fusion.2.refs_11_
  9.8 1.3 fusion.7.refs_2_
  11.0 1.3 bitcast_convert_fusion.1.refs_6_
  12.3 1.3 bitcast_convert_fusion.refs_8_
  13.6 0.7 copy.40
  14.9 0.9 pad_bitcast_fusion.1
  15.9 0.9 pad_bitcast_fusion
  16.8 2.7 pad_maximum_fusion
  19.5 84.4 %front.1 = (bf16[5,4,224,384]{3,2,1,0:T(8,128)(2,1)}, bf16[3,5,224,384]{3,2,1,0:T(8,128)(2,1)}, bf16[5,224,384]{2,1,0:T(8,128)(2,1)}, f32[5,224,384]{2,1,0:T(8,1...) custom-call(bf16[5,224,384]{2,1,0:T(8,128)(2,1)} %get-tuple-element., ...), custom_call_target="tpu_custom_call" | custom-call | flops 20000000000 | bytes 26654208 | tf_op jit(solution)/shard_map/front/pallas_call | solution.py:911
  103.8 150.7 %middle.1 = (f32[5,224,384]{2,1,0:T(8,128)}, bf16[5,4,224,384]{3,2,1,0:T(8,128)(2,1)}, bf16[5,224,1536]{2,1,0:T(8,128)(2,1)}, bf16[5,224,1536]{2,1,0:T(8,128)(2,...) custom-call(bf16[5,224,384]{2,1,0:T(8,128)(2,1)} %get-tuple-element., ...), custom_call_target="tpu_custom_call" | custom-call | flops 30000001024 | bytes 54316032 | tf_op jit(solution)/shard_map/middle/pallas_call | solution.py:1257
  254.6 2.0 copy-done.2
  256.6 15.1 %shard_map.262 = bf16[8,2,192,1536]{3,2,1,0:T(8,128)(2,1)} custom-call(s32[1]{0:T(128)} %bitcast.18.refs_0_, bf16[5,4,224,384]{3,2,1,0:T(8,128)(2,1)S(1)} %copy-done.2, bf16[5,224,1536]{2,1,0:T(8,128)(2,1)} %get-tuple-element.58.refs_2_, bf16[5,4,224,384]{3,2,1,0:T(8,128)(2,1)} %get-tuple-element.54.refs_3_, bf16[5,224,1536]{2,1,0:T(8,128)(2,1)} %get-tuple-element.59.refs_4_), custom_call_target="tpu_custom_call" | custom-call | flops 8455716864 | bytes 23199744 | tf_op jit(solution)/shard_map/pallas_call | solution.py:1573
  271.7 84.5 %back.1 = (bf16[3,5,224,384]{3,2,1,0:T(8,128)(2,1)}, f32[5,224,384]{2,1,0:T(8,128)}, f32[5,224,384]{2,1,0:T(8,128)}, f32[5,3,384]{2,1,0:T(4,128)}, f32[5,3,384]{...) custom-call(bf16[3,5,224,384]{3,2,1,0:T(8,128)(2,1)} %get-tuple-element.52.refs_0_, ...), custom_call_target="tpu_custom_call" | custom-call | flops 40000000000 | bytes 35831808 | tf_op jit(solution)/shard_map/back/pallas_call | solution.py:1501
  356.2 1.7 copy-done
  358.0 9.3 %shard_map.263 = bf16[8,4,192,384]{3,2,1,0:T(8,128)(2,1)} custom-call(s32[1]{0:T(128)} %bitcast.18.refs_0_, bf16[5,4,224,384]{3,2,1,0:T(8,128)(2,1)} %get-tuple-element.76.refs_1_, bf16[3,5,224,384]{3,2,1,0:T(8,128)(2,1)S(1)} %copy-done, bf16[5,4,224,384]{3,2,1,0:T(8,128)(2,1)} %get-tuple-element.66.refs_12_.refs_3_, bf16[5,224,384]{2,1,0:T(8,128)(2,1)S(1)} %copy-done.1), custom_call_target="tpu_custom_call" | custom-call | flops 4227858432 | bytes 15040512 | tf_op jit(solution)/shard_map/pallas_call | solution.py:1573
  369.4 1.3 slice.136
  370.6 0.7 slice_reduce_fusion.4
  372.1 0.7 slice.131
  372.8 0.8 slice_reduce_fusion.1
  373.6 0.7 maximum_convert_fusion.1
  374.4 0.9 concatenate.11.row_ref
  375.3 16.5 %rows.1 = (f32[8,32,384]{2,1,0:T(8,128)S(1)}, f32[32,384]{1,0:T(8,128)S(1)}) custom-call(f32[32,384]{1,0:T(8,128)S(1)} %concatenate.11.row_ref), custom_call_target="tpu_custom_call" | custom-call | flops 1000000 | bytes 491520 | tf_op jit(solution)/shard_map/rows/pallas_call | solution.py:1697
  391.9 2.6 convolution_bitcast_fusion
  395.0 2.0 collective-permute-start.1
  397.0 1.0 collective-permute-start
  398.0 2.2 copy-done.3
  400.2 1.0 copy-done.8
  401.3 6.2 %dw_text.1 = (f32[4,192,384]{2,1,0:T(8,128)S(1)}, f32[2,192,1536]{2,1,0:T(8,128)S(1)}) custom-call(bf16[4,160,384]{2,1,0:T(8,128)(2,1)S(1)} %copy-done.6, bf16[2,4,160,384]{3,2,1,0:T(8,128)(2,1)S(1)} %copy-done.5, bf16[4,160,384]{2,1,0:T(8,128)(2,1)S(1)} %copy-done.8, bf16[4,3,160,384]{3,2,1,0:T(8,128)(2,1)S(1)} %copy-done.4, ...), custom_call_target="tpu_custom_call" | custom-call | flops 6000000000 | bytes 11403264 | tf_op jit(solution)/shard_map/dw_text/pallas_call | solution.py:1643
  408.2 2.5 fusion
  411.4 0.7 copy-done.11
  412.1 1.2 slice.118
  413.3 1.2 slice.120
  415.7 0.9 copy.47
  416.7 0.9 copy.48
  417.6 1.3 reshape.94
  418.9 1.3 reshape.92
  420.3 1.4 copy.49
  422.2 1.3 copy.50
  423.5 1.4 fusion.9
  424.9 2.7 reduce-scatter.3.cloned.1.call-done
  427.6 1.1 slice.162
  428.9 0.9 maximum_bitcast_fusion.3
  429.8 1.4 maximum_bitcast_fusion.2
  431.1 97.9 %reduce-scatter.5.cloned.1.call-done = bf16[1,2,192,1536]{3,2,1,0:T(8,128)(2,1)} async-done(((bf16[8,2,192,1536]{3,2,1,0:T(8,128)(2,1)}), bf16[1,2,192,1536]{3,2,1,0:T(8,128)(2,1)}) %reduce-scatter.5.cloned.1.call-update) | async-done | bytes 1179664 | tf_op jit(solution)/shard_map/reduce_scatter | solution.py:1767
  529.0 1.5 convert_element_type.66
  530.7 1.6 maximum_bitcast_fusion.1
  532.3 1.6 maximum_bitcast_fusion
  (76 shorter events, 7.4 us)
Async XLA Ops:
  7.2 420.4 %reduce-scatter.3.cloned.1.call-start = ((), (), s32[]{:S(2)}) async-start(), calls=%async_computation.2 | async-start | bytes 5308416 | tf_op jit(solution)/shard_map/reduce_scatter | solution.py:1773
  254.6 2.0 copy-start.2
  271.7 84.5 %copy-start.1 = (bf16[5,224,384]{2,1,0:T(8,128)(2,1)S(1)}, bf16[5,224,384]{2,1,0:T(8,128)(2,1)}, u32[]{:S(2)}) copy-start(bf16[5,224,384]{2,1,0:T(8,128)(2,1)} %get-tuple-element.53.refs_0_.refs_1_.refs_4_) | copy-start | bytes 2580484
  356.2 1.7 copy-start
  367.3 0.8 copy-start.13
  367.3 4.6 copy-start.15
  367.3 4.7 copy-start.12
  367.4 161.6 %reduce-scatter.5.cloned.1.call-start = ((), (), s32[]{:S(2)}) async-start(), calls=%async_computation.3 | async-start | bytes 10616832 | tf_op jit(solution)/shard_map/reduce_scatter | solution.py:1767
  367.6 30.4 %copy-start.6 = (bf16[4,160,384]{2,1,0:T(8,128)(2,1)S(1)}, bf16[4,160,384]{2,1,0:T(8,128)(2,1)}, u32[]{:S(2)}) copy-start(bf16[4,160,384]{2,1,0:T(8,128)(2,1)} %get-tuple-element.80.refs_0_) | copy-start | bytes 1474564
  367.6 30.4 %copy-start.7 = (bf16[4,160,384]{2,1,0:T(8,128)(2,1)S(1)}, bf16[4,160,384]{2,1,0:T(8,128)(2,1)}, u32[]{:S(2)}) copy-start(bf16[4,160,384]{2,1,0:T(8,128)(2,1)} %get-tuple-element.85.refs_5_) | copy-start | bytes 1474564
  368.1 29.9 %copy-start.4 = (bf16[4,3,160,384]{3,2,1,0:T(8,128)(2,1)S(1)}, bf16[4,3,160,384]{3,2,1,0:T(8,128)(2,1)}, u32[]{:S(2)}) copy-start(bf16[4,3,160,384]{3,2,1,0:T(8,128)(2,1)} %get-tuple-element.83.refs_3_) | copy-start | bytes 4423684
  368.1 29.9 %copy-start.5 = (bf16[2,4,160,384]{3,2,1,0:T(8,128)(2,1)S(1)}, bf16[2,4,160,384]{3,2,1,0:T(8,128)(2,1)}, u32[]{:S(2)}) copy-start(bf16[2,4,160,384]{3,2,1,0:T(8,128)(2,1)} %get-tuple-element.81.refs_1_) | copy-start | bytes 2949124
  394.5 29.0 %collective-permute-start.2 = (f32[8,192]{1,0:T(8,128)}, f32[8,192]{1,0:T(8,128)}, u32[]{:S(2)}, u32[]{:S(2)}) collective-permute-start(f32[8,192]{1,0:T(8,128)} %convolution_bitcast_fusion), channel_id=1, source_target_pairs={{0,3},{1,2},{2,1},{3,0},{4,7},{5,6},{6,5},{7,4},{8,11},{9,10},{10,... | collective-permute-start | bytes 18440 | tf_op jit(solution)/shard_map/ppermute | solution.py:1798
  395.0 28.5 %collective-permute-start.1 = (f32[8,192]{1,0:T(8,128)}, f32[8,192]{1,0:T(8,128)}, u32[]{:S(2)}, u32[]{:S(2)}) collective-permute-start(f32[8,192]{1,0:T(8,128)} %convolution_bitcast_fusion), channel_id=1, source_target_pairs={{0,2},{1,3},{2,0},{3,1},{4,6},{5,7},{6,4},{7,5},{8,10},{9,11},{10,... | collective-permute-start | bytes 18440 | tf_op jit(solution)/shard_map/ppermute | solution.py:1798
  397.0 26.6 %collective-permute-start = (f32[8,192]{1,0:T(8,128)}, f32[8,192]{1,0:T(8,128)}, u32[]{:S(2)}, u32[]{:S(2)}) collective-permute-start(f32[8,192]{1,0:T(8,128)} %convolution_bitcast_fusion), channel_id=1, source_target_pairs={{0,1},{1,0},{2,3},{3,2},{4,5},{5,4},{6,7},{7,6},{8,9},{9,8},{10,11... | collective-permute-start | bytes 18440 | tf_op jit(solution)/shard_map/ppermute | solution.py:1798
  398.0 2.2 copy-start.3
  400.2 1.0 copy-start.8
  407.5 0.7 copy-start.14
  410.6 1.5 copy-start.11
  410.8 2.5 copy-start.10
  427.6 1.2 copy-start.9
Sparse Core Ops, SparseCore 0:
  367.4 60.0 reduce-scatter.2
  429.9 99.0 reduce-scatter.4

commit v3 on v2

--- a/solution.py
+++ b/solution.py
@@ -567,8 +567,9 @@
 
 
 class Links:
-    def __init__(self, send, recv):
+    def __init__(self, send, recv, text, rows, taken):
         self.send_sem, self.recv_sem = send, recv
+        self.text, self.rows, self.taken = text, rows, taken
         me = lax.axis_index("tensor")
         self.peers = [me, me + 1 - 2 * (me % 2), (me + 2) % 4, 3 - me]
 
@@ -596,55 +597,77 @@
         second = self.peers[2] * (1 - odd) + self.peers[1] * odd
         return 1 + odd, 2 - odd, first, second
 
-    def gather_copy(self, i, src, buf, kind, c):
+    def act(self, action, copy, i, *args):
+        c = args[-1]
+        if isinstance(c, int):
+            getattr(copy(i, self.taken if c == self.text else self.rows, *args), action)()
+            return
+
+        @pl.when(c == self.text)
+        def _():
+            getattr(copy(i, self.taken, *args), action)()
+
+        @pl.when(c != self.text)
+        def _():
+            getattr(copy(i, self.rows, *args), action)()
+
+    def clear(self, *views):
+        for view in views:
+            view[self.taken :, :] = jnp.zeros((self.rows - self.taken, view.shape[-1]), BF16)
+
+    def gather_copy(self, i, rows, src, buf, kind, c):
         near, far, first, second = self.route(c)
+        some = pl.ds(0, rows)
         if i == 0:
-            return self.copy(src, buf.at[c, near], kind, c, first)
+            return self.copy(src.at[some, :], buf.at[c, near, some, :], kind, c, first)
         if i == 1:
-            return self.copy(src, buf.at[c, far], kind + 1, c, second)
-        return self.copy(buf.at[c, near], buf.at[c, 3], kind + 2, c, second)
+            return self.copy(src.at[some, :], buf.at[c, far, some, :], kind + 1, c, second)
+        return self.copy(buf.at[c, near, some, :], buf.at[c, 3, some, :], kind + 2, c, second)
 
     def gather_start(self, *args):
-        self.gather_copy(0, *args).start()
-        self.gather_copy(1, *args).start()
+        self.act("start", self.gather_copy, 0, *args)
+        self.act("start", self.gather_copy, 1, *args)
 
     def gather_relay(self, *args):
-        self.gather_copy(0, *args).wait_recv()
-        self.gather_copy(2, *args).start()
+        self.act("wait_recv", self.gather_copy, 0, *args)
+        self.act("start", self.gather_copy, 2, *args)
 
     def gather_finish(self, *args):
-        self.gather_copy(1, *args).wait_recv()
-        self.gather_copy(2, *args).wait_recv()
+        self.act("wait_recv", self.gather_copy, 1, *args)
+        self.act("wait_recv", self.gather_copy, 2, *args)
 
     def gather_sent(self, *args):
         for i in range(3):
-            self.gather_copy(i, *args).wait_send()
-
-    def scatter_copy(self, i, part, relayed, got, kind, c):
+            self.act("wait_send", self.gather_copy, i, *args)
+
+    def scatter_copy(self, i, rows, part, relayed, got, kind, c):
         near, _, first, second = self.route(c)
+        some = pl.ds(0, rows)
         if i == 0:
-            return self.copy(part.at[c, 3], got.at[c, 0], kind, c, first)
+            return self.copy(part.at[c, 3, some, :], got.at[c, 0, some, :], kind, c, first)
         if i == 1:
-            return self.copy(part.at[c, near], got.at[c, 1], kind + 1, c, first)
-        return self.copy(relayed.at[c], got.at[c, 2], kind + 2, c, second)
+            return self.copy(part.at[c, near, some, :], got.at[c, 1, some, :], kind + 1, c, first)
+        return self.copy(relayed.at[c, some, :], got.at[c, 2, some, :], kind + 2, c, second)
 
     def scatter_start(self, *args):
-        self.scatter_copy(0, *args).start()
-        self.scatter_copy(1, *args).start()
+        self.act("start", self.scatter_copy, 0, *args)
+        self.act("start", self.scatter_copy, 1, *args)
 
     def scatter_relay(self, part, relayed, got, kind, c):
-        self.scatter_copy(0, part, relayed, got, kind, c).wait_recv()
+        args = (part, relayed, got, kind, c)
+        self.act("wait_recv", self.scatter_copy, 0, *args)
         _, far, _, _ = self.route(c)
         relayed[c] = (part[c, far].astype(F32) + got[c, 0].astype(F32)).astype(BF16)
-        self.scatter_copy(2, part, relayed, got, kind, c).start()
+        self.act("start", self.scatter_copy, 2, *args)
 
     def scatter_sent(self, *args):
         for i in range(3):
-            self.scatter_copy(i, *args).wait_send()
+            self.act("wait_send", self.scatter_copy, i, *args)
 
     def scatter_finish(self, part, relayed, got, kind, c):
-        self.scatter_copy(1, part, relayed, got, kind, c).wait_recv()
-        self.scatter_copy(2, part, relayed, got, kind, c).wait_recv()
+        args = (part, relayed, got, kind, c)
+        self.act("wait_recv", self.scatter_copy, 1, *args)
+        self.act("wait_recv", self.scatter_copy, 2, *args)
         return part[c, 0].astype(F32) + got[c, 1].astype(F32) + got[c, 2].astype(F32)
 
     def rows_copies(self, src, dst, kind, c):
@@ -765,16 +788,17 @@
     count, rows, feats = x_ref.shape
     cols = qkv_ref.shape[-1]
     width = 4 * feats
-    links = Links(send, recv)
-    column = Column(dp // 2, zsend, zrecv)
     taken = zm_ref.shape[1]
     text = count - 1
+    links = Links(send, recv, text, rows, taken)
+    column = Column(dp // 2, zsend, zrecv)
     mine = lax.axis_index("dp")
     others = [(mine + r) % dp for r in range(1, dp)]
     load_mod = pltpu.make_async_copy(modw_ref, modw, local.at[0])
     load_wq = pltpu.make_async_copy(wq_ref, wq, local.at[1])
     load_mod.start()
     load_wq.start()
+    links.clear(*[ref.at[text, k] for ref in (xp_ref, g_ref) for k in (1, 2, 3)])
     links.enter(others)
     for c in (text, *range(text)):
         links.gather_start(x_ref.at[c], xp_ref, 0, c)
@@ -797,7 +821,7 @@
         push.start()
     for c in range(count):
         xp_ref[c, 0] = x_ref[c]
-    total = terms[mine] + modb_ref[...]
+    total = terms[mine] + modb_ref[...].astype(F32)
     for r, push in enumerate(pushes):
         push.wait_recv()
         total = total + got[r]
@@ -835,7 +859,7 @@
                 part = nn_dot(m, wq[stream, j, links.peers[k]])
                 acc[j] = part if k == 0 else acc[j] + part
         for j in range(3):
-            qkv_ref[j, c] = (acc[j] + bq_ref[stream, j : j + 1, :]).astype(BF16)
+            qkv_ref[j, c] = (acc[j] + bq_ref[stream, j : j + 1, :].astype(F32)).astype(BF16)
         links.gather_relay(g_ref.at[c, 0], g_ref, 3, c)
 
         @pl.when(s == 0)
@@ -946,13 +970,13 @@
     (wo, up, down, db2, part, relayed, got, xp, branch, acc_m, acc_b, cols_s) = scratch[:12]
     (x1_s, m2_s, a_s, du_s, b2_s, g1_s, srow, sgot, local, out_sem, send, recv) = scratch[12:24]
     zsend, zrecv, zlocal = scratch[24:]
-    count, _, feats = x_ref.shape
+    count, rows, feats = x_ref.shape
     width = 4 * feats
     hidden = up.shape[-1]
-    links = Links(send, recv)
-    column = Column(chips, zsend, zrecv)
     text = count - 1
     taken = zo_ref.shape[1]
+    links = Links(send, recv, text, rows, taken)
+    column = Column(chips, zsend, zrecv)
 
     def at(s):
         return (s + text) % count
@@ -965,6 +989,8 @@
     ]
     for load in loads:
         load.start()
+    links.clear(*[ref.at[text, k] for ref in (xp, g_ref) for k in (1, 2, 3)])
+    links.clear(*[got.at[text, k] for k in (0, 1, 2)])
     links.enter(column.others)
     loads[0].wait()
 
@@ -987,6 +1013,9 @@
             pltpu.make_async_copy(o_ref.at[text, first_rows, :], zo_ref.at[column.z], zlocal.at[3]),
             column.deal_own(db2.at[text], zl_ref.at[1], zlocal.at[4], taken),
         ]
+
+    def own_last():
+        return column.deal_own(g_ref.at[text], zl_ref.at[2], zlocal.at[5], taken)
 
     def column_early(s):
         @pl.when(s == 0)
@@ -1035,7 +1064,8 @@
         c = at(s)
         stream = c // (count - 1)
         total = links.scatter_finish(part, relayed, got, 0, c)
-        add = total + ob_ref[pl.ds(stream, 1), :]
+        bias = jnp.where(c == text, ob_ref[1:2, :], ob_ref[0:1, :]).astype(F32)
+        add = total + bias
         branch[c] = add
         moved = x_ref[c].astype(F32) + mod_ref[0, pl.ds(stream * 6 + 2, 1), :] * add
 
@@ -1083,7 +1113,7 @@
 
         def block(b, carry):
             cols = pl.ds(pl.multiple_of(b * HB, HB), HB)
-            u = ub_ref[pl.ds(stream, 1), cols]
+            u = jnp.where(c == text, ub_ref[1:2, cols], ub_ref[0:1, cols]).astype(F32)
             for k in range(4):
                 u = u + nn_dot(m2_s[slot, k], up[stream, links.peers[k], :, cols])
             da = None
@@ -1187,6 +1217,11 @@
             acc = piece if acc is None else acc + piece
         do_ref[c] = acc.astype(BF16)
 
+        @pl.when(s == 0)
+        def _():
+            column.deal(g_ref.at[text], zl_ref.at[2], 4, taken)
+            own_last().start()
+
     stages(
         count,
         [
@@ -1209,6 +1244,8 @@
     column.spread(zo_ref, 1, chips - 1)
     column.deal_wait(m2_out.at[text], zl_ref.at[0], 2, taken)
     column.deal_wait(db2.at[text], zl_ref.at[1], 3, taken)
+    column.deal_wait(g_ref.at[text], zl_ref.at[2], 4, taken)
+    own_last().wait()
     column.spread_sent(zr_ref, 0)
     column.spread_sent(zo_ref, 1)
     for c in range(count):
@@ -1246,7 +1283,7 @@
         sds((count, 4, feats), F32),
         sds((count, hidden), F32),
         sds((dp // 2, 2, taken, hidden), BF16),
-        sds((2, dp // 2, taken, feats), BF16),
+        sds((3, dp // 2, taken, feats), BF16),
         sds((dp // 2, taken, cols), BF16),
     ]
     n_in, n_out = len(arrays), len(outs)
@@ -1284,9 +1321,9 @@
             pltpu.SemaphoreType.DMA((6, 2)),
             pltpu.SemaphoreType.DMA((15, count)),
             pltpu.SemaphoreType.DMA((15, count)),
-            pltpu.SemaphoreType.DMA((4, dp - 2)),
-            pltpu.SemaphoreType.DMA((4, dp - 2)),
-            pltpu.SemaphoreType.DMA((5,)),
+            pltpu.SemaphoreType.DMA((5, dp - 2)),
+            pltpu.SemaphoreType.DMA((5, dp - 2)),
+            pltpu.SemaphoreType.DMA((6,)),
         ],
         compiler_params=pltpu.CompilerParams(
             collective_id=2, has_side_effects=True, vmem_limit_bytes=63 * MIB
@@ -1296,38 +1333,19 @@
     )(*arrays)
 
 
-def back_kernel(chips, valid, blocks, refs_in, refs_out, scratch):
-    qkv_ref, o_ref, do_ref, lse_ref, b2_ref, x1_ref, cot_ref, g1_ref, xp_ref, mod_ref = refs_in[:10]
-    wq_ref, db_ref, db1_ref = refs_in[10:]
-    dqkv_ref, x2_ref, grad_ref, line_ref, bias_ref, zq_ref, zd_ref = refs_out
-    wq, q_all, k_all, v_all, do_all, lse_all, od_all, dk_all, dv_all, dqt_all, dq_all = scratch[:11]
-    part, relayed, got, relayed2, got2, cols_s, srow, sgot, local, send, recv = scratch[11:22]
-    zsend, zrecv = scratch[22:]
-    count, rows, feats = cot_ref.shape
+def back_kernel(valid, taken, blocks, refs_in, refs_out, scratch):
+    qkv_ref, o_ref, do_ref, lse_ref, b2_ref, x1_ref, cot_ref, mod_ref, db_ref = refs_in
+    dqkv_ref, x2_ref, gate_ref = refs_out
+    q_all, k_all, v_all, do_all, lse_all, od_all, dk_all, dv_all, dqt_all, dq_all = scratch[:10]
+    relayed2, got2, send, recv = scratch[10:]
+    count, rows, _ = cot_ref.shape
     cols = o_ref.shape[-1]
-    width = 4 * feats
-    links = Links(send, recv)
-    column = Column(chips, zsend, zrecv)
     text = count - 1
-    taken = zd_ref.shape[1]
-    load = pltpu.make_async_copy(wq_ref, wq, local.at[0])
-    load.start()
-    links.enter(column.others)
+    links = Links(send, recv, text, rows, taken)
+    links.clear(*[got2.at[text, k] for k in (0, 1, 2)])
+    links.enter()
     for c in range(count):
         links.scatter_start(b2_ref, relayed2, got2, 0, c)
-    own_db = pltpu.make_async_copy(
-        db1_ref.at[text, column.block_of(column.z), pl.ds(0, taken), :],
-        zd_ref.at[column.z],
-        local.at[1],
-    )
-    own_db.start()
-    column.deal(db1_ref.at[text], zd_ref, 1, taken)
-    own_q = [
-        pltpu.make_async_copy(
-            dqkv_ref.at[j, text, pl.ds(0, taken), :], zq_ref.at[column.z, j], local.at[2 + j]
-        )
-        for j in range(3)
-    ]
     scale = jnp.asarray(HEAD_DIM**-0.5, BF16)
     head_row = lax.broadcasted_iota(jnp.int32, (8, 128), 0)
     lane = lax.broadcasted_iota(jnp.int32, (8, 128), 1)
@@ -1385,25 +1403,99 @@
             dqkv_ref[1, c, :size, lanes] = dk_all[sl, :].astype(BF16)
             dqkv_ref[2, c, :size, lanes] = dv_all[sl, :].astype(BF16)
 
-        @pl.when(p == 0)
+        @pl.when(p == pairs - 2)
         def _():
             for c in range(count):
                 links.scatter_relay(b2_ref, relayed2, got2, 0, c)
 
         return carry
 
-    lax.fori_loop(0, cols // 128, heads_pair, 0)
+    pairs = cols // 128
+    lax.fori_loop(0, pairs, heads_pair, 0)
+    for c in range(count):
+        stream = c // (count - 1)
+        total = links.scatter_finish(b2_ref, relayed2, got2, 0, c)
+        bias = jnp.where(c == text, db_ref[1:2, :], db_ref[0:1, :]).astype(F32)
+        add = total + bias
+        x2_ref[c] = x1_ref[c] + mod_ref[0, pl.ds(stream * 6 + 5, 1), :] * add
+        gate_ref[c : c + 1, :] = jnp.sum(add * cot_ref[c].astype(F32), axis=0, keepdims=True)
+
+    for c in range(count):
+        links.scatter_sent(b2_ref, relayed2, got2, 0, c)
+
+
+def back_call(valid, taken, qkv, o, do, lse, b2, x1, cot, mods, down_b):
+    count, rows, feats = cot.shape
+    padded = -(-valid // 128) * 128
+    step = -(-valid // 3 // 16) * 16
+    blocks = [(b, min(step, valid - b)) for b in range(0, valid, step)]
+    arrays = [qkv, o, do, lse, b2, x1, cot, mods, down_b]
+    outs = [
+        sds(qkv.shape, BF16),
+        sds((count, rows, feats), F32),
+        sds((count, feats), F32),
+    ]
+    n_in, n_out = len(arrays), len(outs)
+
+    def kernel(*refs):
+        back_kernel(
+            valid, taken, blocks, refs[:n_in], refs[n_in : n_in + n_out], refs[n_in + n_out :]
+        )
+
+    return pl.pallas_call(
+        kernel,
+        out_shape=outs,
+        in_specs=[VMEM] * n_in,
+        out_specs=[VMEM] * n_out,
+        scratch_shapes=[pltpu.VMEM((valid, 128), BF16)] * 4
+        + [pltpu.VMEM((valid, 128), F32)] * 4
+        + [
+            pltpu.VMEM((128, padded), F32),
+            pltpu.VMEM((padded, 128), F32),
+            pltpu.VMEM((count, rows, feats), BF16),
+            pltpu.VMEM((count, 3, rows, feats), BF16),
+            pltpu.SemaphoreType.DMA((3, count)),
+            pltpu.SemaphoreType.DMA((3, count)),
+        ],
+        compiler_params=pltpu.CompilerParams(
+            collective_id=3, has_side_effects=True, vmem_limit_bytes=56 * MIB
+        ),
+        cost_estimate=cost(30 * 10**9, arrays, outs),
+        name="back",
+    )(*arrays)
+
+
+def last_kernel(chips, refs_in, refs_out, scratch):
+    dqkv_ref, g1_ref, xp_ref, mod_ref, wq_ref = refs_in
+    grad_ref, line_ref, bias_ref, zq_ref = refs_out
+    wq, part, relayed, got, cols_s, srow, sgot, local, send, recv, zsend, zrecv = scratch
+    count, rows, feats = g1_ref.shape
+    width = 4 * feats
+    text = count - 1
+    taken = zq_ref.shape[2]
+    links = Links(send, recv, text, rows, taken)
+    column = Column(chips, zsend, zrecv)
+    load = pltpu.make_async_copy(wq_ref, wq, local.at[0])
+    load.start()
+    own_q = [
+        pltpu.make_async_copy(
+            dqkv_ref.at[j, text, pl.ds(0, taken), :], zq_ref.at[column.z, j], local.at[1 + j]
+        )
+        for j in range(3)
+    ]
     for copy in own_q:
         copy.start()
+    links.clear(*[got.at[text, k] for k in (0, 1, 2)])
+    links.enter(column.others)
+    for copy in own_q:
+        copy.wait()
+    column.spread(zq_ref, 0, 0)
     load.wait()
 
     def column_step(dist):
         def step(c):
             @pl.when(c == 0)
             def _():
-                if dist == 0:
-                    for copy in own_q:
-                        copy.wait()
                 column.spread(zq_ref, 0, dist)
 
         return step
@@ -1435,13 +1527,6 @@
     def last_relay(c):
         links.scatter_relay(part, relayed, got, 3, c)
 
-    def out_stream(c):
-        stream = c // (count - 1)
-        total = links.scatter_finish(b2_ref, relayed2, got2, 0, c)
-        add = total + db_ref[pl.ds(stream, 1), :]
-        x2_ref[c] = x1_ref[c] + mod_ref[0, pl.ds(stream * 6 + 5, 1), :] * add
-        line_ref[c, 2:3, :] = jnp.sum(add * cot_ref[c].astype(F32), axis=0, keepdims=True)
-
     def norm_back(c):
         stream = c // (count - 1)
         total = links.scatter_finish(part, relayed, got, 3, c)
@@ -1459,75 +1544,58 @@
         count,
         [
             (1, last_relay),
-            (0, column_step(0)),
             (2, column_step(1)),
             (4, column_step(2)),
             (0, input_grads),
             (2, norm_back),
-            (1, out_stream),
         ],
     )
+    for c in range(count):
+        links.scatter_sent(part, relayed, got, 3, c)
+        wait_sends(links.rows_copies(srow, sgot, 6, c))
     column.spread(zq_ref, 0, chips - 1)
     column.spread_sent(zq_ref, 0)
-    own_db.wait()
-    column.deal_wait(db1_ref.at[text], zd_ref, 1, taken)
-    for c in range(count):
-        links.scatter_sent(b2_ref, relayed2, got2, 0, c)
-        links.scatter_sent(part, relayed, got, 3, c)
-        wait_sends(links.rows_copies(srow, sgot, 6, c))
-
-
-def back_call(dp, valid, taken, qkv, o, do, lse, b2, x1, cot, g1, xp, mods, wq, down_b, db1):
-    count, rows, feats = cot.shape
-    cols = o.shape[-1]
-    padded = -(-valid // 128) * 128
-    step = -(-valid // 3 // 16) * 16
-    blocks = [(b, min(step, valid - b)) for b in range(0, valid, step)]
-    arrays = [qkv, o, do, lse, b2, x1, cot, g1, xp, mods, wq, down_b, db1]
+
+
+def last_call(dp, taken, dqkv, g1, xp, mods, wq):
+    count, rows, feats = g1.shape
+    cols = dqkv.shape[-1]
+    arrays = [dqkv, g1, xp, mods, wq]
     outs = [
-        sds(qkv.shape, BF16),
         sds((count, rows, feats), F32),
-        sds((count, rows, feats), F32),
-        sds((count, 3, feats), F32),
+        sds((count, 2, feats), F32),
         sds((count, 3, cols), F32),
         sds((dp // 2, 3, taken, cols), BF16),
-        sds((dp // 2, taken, feats), BF16),
     ]
     n_in, n_out = len(arrays), len(outs)
 
     def kernel(*refs):
-        back_kernel(dp // 2, valid, blocks, refs[:n_in], refs[n_in : n_in + n_out], refs[n_in + n_out :])
+        last_kernel(dp // 2, refs[:n_in], refs[n_in : n_in + n_out], refs[n_in + n_out :])
 
     return pl.pallas_call(
         kernel,
         out_shape=outs,
-        in_specs=[VMEM] * 10 + [ANY, VMEM, ANY],
-        out_specs=[VMEM] * (n_out - 2) + [ANY] * 2,
-        scratch_shapes=[pltpu.VMEM(wq.shape, BF16)]
-        + [pltpu.VMEM((valid, 128), BF16)] * 4
-        + [pltpu.VMEM((valid, 128), F32)] * 4
-        + [
-            pltpu.VMEM((128, padded), F32),
-            pltpu.VMEM((padded, 128), F32),
+        in_specs=[VMEM] * 4 + [ANY],
+        out_specs=[VMEM] * 3 + [ANY],
+        scratch_shapes=[
+            pltpu.VMEM(wq.shape, BF16),
             pltpu.VMEM((count, 4, rows, feats), BF16),
-            pltpu.VMEM((count, rows, feats), BF16),
-            pltpu.VMEM((count, 3, rows, feats), BF16),
             pltpu.VMEM((count, rows, feats), BF16),
             pltpu.VMEM((count, 3, rows, feats), BF16),
             pltpu.VMEM((count, rows, 128), F32),
             pltpu.VMEM((count, 8, rows), F32),
             pltpu.VMEM((count, 3, 8, rows), F32),
-            pltpu.SemaphoreType.DMA((5,)),
+            pltpu.SemaphoreType.DMA((4,)),
             pltpu.SemaphoreType.DMA((9, count)),
             pltpu.SemaphoreType.DMA((9, count)),
-            pltpu.SemaphoreType.DMA((2, dp - 2)),
-            pltpu.SemaphoreType.DMA((2, dp - 2)),
+            pltpu.SemaphoreType.DMA((1, dp - 2)),
+            pltpu.SemaphoreType.DMA((1, dp - 2)),
         ],
         compiler_params=pltpu.CompilerParams(
-            collective_id=3, has_side_effects=True, vmem_limit_bytes=63 * MIB
+            collective_id=6, has_side_effects=True, vmem_limit_bytes=48 * MIB
         ),
-        cost_estimate=cost(40 * 10**9, arrays, outs),
-        name="back",
+        cost_estimate=cost(15 * 10**9, arrays, outs),
+        name="last",
     )(*arrays)
 
 
@@ -1591,7 +1659,7 @@
 
 
 def text_kernel(refs_in, refs_out, scratch):
-    zm_ref, zl_ref, zd_ref, zq_ref, zr_ref, zo_ref = refs_in
+    zm_ref, zl_ref, zq_ref, zr_ref, zo_ref = refs_in
     at_ref, ff_ref = refs_out
     send_a, got_a, send_f, got_f, keep_a, keep_f, send, recv = scratch
     index = lax.axis_index("dp")
@@ -1618,7 +1686,7 @@
         (zm_ref, zq_ref.at[:, 0], keep_a, send_a, got_a, at_ref, 0),
         (zm_ref, zq_ref.at[:, 1], keep_a, send_a, got_a, at_ref, 1),
         (zm_ref, zq_ref.at[:, 2], keep_a, send_a, got_a, at_ref, 2),
-        (zd_ref, zo_ref, keep_a, send_a, got_a, at_ref, 3),
+        (zl_ref.at[2], zo_ref, keep_a, send_a, got_a, at_ref, 3),
     ]
     for left, right, keep, out, got, _, i in work:
         keep[i] = tn_dot(flat(left[...]), flat(right[...]))
@@ -1631,19 +1699,19 @@
         move(out, got, i).wait_send()
 
 
-def text_call(zm, zl, zd, zq, zr, zo):
+def text_call(zm, zl, zq, zr, zo):
     feats, cols, hidden = zm.shape[-1], zq.shape[-1], zr.shape[-1]
     half = feats // 2
-    arrays = [zm, zl, zd, zq, zr, zo]
+    arrays = [zm, zl, zq, zr, zo]
     outs = [sds((4, half, cols), F32), sds((2, half, hidden), F32)]
 
     def kernel(*refs):
-        text_kernel(refs[:6], refs[6:8], refs[8:])
+        text_kernel(refs[:5], refs[5:7], refs[7:])
 
     return pl.pallas_call(
         kernel,
         out_shape=outs,
-        in_specs=[VMEM] * 6,
+        in_specs=[VMEM] * 5,
         out_specs=[VMEM] * 2,
         scratch_shapes=[
             pltpu.VMEM((4, half, cols), BF16),
@@ -1747,7 +1815,7 @@
     cond_float = cond_in.astype(F32)
     cond_act = jax.nn.silu(cond_float).astype(BF16)
     mod_w = jnp.transpose(mod_weight[0], (0, 2, 1, 3)).reshape(12, -1, feats)
-    mod_b = mod_bias[0].reshape(12, feats).astype(F32)
+    mod_b = mod_bias[0].reshape(12, feats)
     qkv_w = jnp.transpose(qkv_weight[0], (0, 2, 1, 3))
     qkv_w = qkv_w.reshape(2, 3, 4, feats, qkv_w.shape[-1])
     out_w = out_weight[0].reshape(2, 4, feats, -1)
@@ -1756,29 +1824,29 @@
 
     taken = -(-texts // 16) * 16
     m, qkv, o, lse, db2, xp, mods, db2_sum, zm = front_call(
-        dp, valid, taken, x, cot, cond_act, mod_w, mod_b, qkv_w, qkv_bias[0].astype(F32)
-    )
-    up_b, out_b, down_b = (b[0].astype(F32) for b in (up_bias, out_bias, down_bias))
+        dp, valid, taken, x, cot, cond_act, mod_w, mod_b, qkv_w, qkv_bias[0]
+    )
     x1, m2, act, du, b2, g1, db1, do, lines2, du_sum, zr, zl, zo = middle_call(
-        dp, taken, o, x, cot, db2, mods, out_w, up_w, down_w, up_b, out_b
+        dp, taken, o, x, cot, db2, mods, out_w, up_w, down_w, up_bias[0], out_bias[0]
     )
     part = wgrad_call(base, [(m2, du), (db2, act)], dp)
     do, part = lax.optimization_barrier((do, part))
     ff_sum = lax.psum_scatter(part, "dp", scatter_dimension=0, tiled=True)
-    dqkv, x2, grad, lines1, qkv_sum, zq, zd = back_call(
-        dp, valid, taken, qkv, o, do, lse, b2, x1, cot, g1, xp, mods, qkv_w, down_b, db1
+    dqkv, x2, gate2 = back_call(
+        valid, taken, qkv, o, do, lse, b2, x1, cot, mods, down_bias[0]
     )
     part2 = wgrad_call(base, [(m, dqkv), (db1, o)], dp)
-    part2, zq = lax.optimization_barrier((part2, zq))
+    part2, dqkv = lax.optimization_barrier((part2, dqkv))
     at_sum = lax.psum_scatter(part2, "dp", scatter_dimension=0, tiled=True)
-    at_text, ff_text = text_call(zm, zl, zd, zq, zr, zo)
+    grad, lines1, qkv_sum, zq = last_call(dp, taken, dqkv, g1, xp, mods, qkv_w)
+    at_text, ff_text = text_call(zm, zl, zq, zr, zo)
 
     def by_stream(value):
         return jnp.stack([jnp.sum(value[:4], axis=0), value[4]])
 
     late, early = by_stream(lines1), by_stream(lines2)
     mod_rows = jnp.stack(
-        [late[:, 0], late[:, 1], early[:, 2], early[:, 0], early[:, 1], late[:, 2]], axis=1
+        [late[:, 0], late[:, 1], early[:, 2], early[:, 0], early[:, 1], by_stream(gate2)], axis=1
     )
     mod_rows = mod_rows.reshape(12, feats).astype(BF16).astype(F32)
     every = [

time: 542 us -> 495 us (0.913)
  waiting for transfers between devices: 101 us -> 75.9 us
  Pallas kernels: 367 us -> 358 us
  other arithmetic: 19.8 us -> 11.7 us
    reduce_scatter x1, waiting for transfers between devices: 97.9 us -> 75.2 us  [fast_body(): ff_sum = lax.psum_scatter(part, 'dp', scatter_dimension=0, tiled=True)]
    pallas_call x1, Pallas kernels: 151 us -> 142 us  [middle_call(): pl.pallas_call(kernel, out_shape=outs, in_specs=[VMEM, VMEM, VMEM, ANY, V...]
    pallas_call x2 -> x3, Pallas kernels: 90.7 us -> 97.4 us  [the longest x1 57.1 us: last_call(): pl.pallas_call(kernel, out_shape=outs, in_specs=[VMEM] * 4 + [ANY], out_s...]
    unnamed x36 -> x47, local copies, waits for them, and re-layouts: 12.8 us -> 16.3 us
  transfers between devices with their start and end apart: 5 -> 5, of which waited for: 2 -> 1; matrix products, arithmetic and copies ran while one was open for 5% -> 4% of each run, Pallas kernels for 4% -> 15%
where the time goes in v3:
time: 495 us; the launch traced here: 494 us
  Pallas kernels  358 us (72%)
  waiting for transfers between devices  75.9 us (15%)
  local copies, waits for them, and re-layouts  26.2 us (5%)
  between operations  14.5 us (3%)
  other arithmetic  11.7 us (2%)
    pallas_call x1, Pallas kernels, middle_call(): pl.pallas_call(kernel, out_shape=outs, in_specs=[VMEM, VMEM, VMEM, ANY, V...  142 us
    pallas_call x1, Pallas kernels, front_call(): pl.pallas_call(kernel, out_shape=outs, in_specs=[VMEM, VMEM, VMEM, ANY, V...  81.3 us
    reduce_scatter x1, waiting for transfers between devices, fast_body(): ff_sum = lax.psum_scatter(part, 'dp', scatter_dimension=0, tiled=True)  75.2 us
    pallas_call x1, Pallas kernels, last_call(): pl.pallas_call(kernel, out_shape=outs, in_specs=[VMEM] * 4 + [ANY], out_s...  57.1 us
    pallas_call x1, Pallas kernels, back_call(): pl.pallas_call(kernel, out_shape=outs, in_specs=[VMEM] * n_in, out_specs=...  33.9 us
    pallas_call x2, Pallas kernels, wgrad_call(): pl.pallas_call(kernel, out_shape=[out], grid_spec=pltpu.PrefetchScalarGri...  24.4 us
    unnamed x47, local copies, waits for them, and re-layouts  16.3 us
    pallas_call x1, Pallas kernels, rows_call(): pl.pallas_call(functools.partial(rows_kernel, dp), out_shape=outs, in_spe...  12.8 us
  transfers between devices with their start and end apart: 5, of which 1 were waited for; matrix products, arithmetic and copies ran while one was open for 4% of the time, Pallas kernels for 15%

profile of v3, /device:TPU:0, one launch (start us, length us, event | category | flops | bytes accessed | tf_op | source)
XLA Modules:
  0.0 494.3 jit_solution(8931922223309354278)
XLA Ops:
  7.2 1.3 fusion.7.refs_2_
  8.5 1.3 copy.70
  9.8 0.7 copy.52
  10.5 0.6 reshape_squeeze.20.refs_4_
  11.1 0.9 pad_bitcast_fusion.1
  12.0 0.9 pad_bitcast_fusion
  13.0 2.7 pad_maximum_fusion
  15.7 81.3 %front.1 = (bf16[5,4,224,384]{3,2,1,0:T(8,128)(2,1)}, bf16[3,5,224,384]{3,2,1,0:T(8,128)(2,1)}, bf16[5,224,384]{2,1,0:T(8,128)(2,1)}, f32[5,224,384]{2,1,0:T(8,1...) custom-call(bf16[5,224,384]{2,1,0:T(8,128)(2,1)} %get-tuple-element., ...), custom_call_target="tpu_custom_call" | custom-call | flops 20000000000 | bytes 26640384 | tf_op jit(solution)/shard_map/front/pallas_call | solution.py:935
  96.9 141.9 %middle.1 = (f32[5,224,384]{2,1,0:T(8,128)}, bf16[5,4,224,384]{3,2,1,0:T(8,128)(2,1)}, bf16[5,224,1536]{2,1,0:T(8,128)(2,1)}, bf16[5,224,1536]{2,1,0:T(8,128)(2,...) custom-call(bf16[5,224,384]{2,1,0:T(8,128)(2,1)} %get-tuple-element., ...), custom_call_target="tpu_custom_call" | custom-call | flops 30000001024 | bytes 54799872 | tf_op jit(solution)/shard_map/middle/pallas_call | solution.py:1294
  238.9 2.0 copy-done.2
  240.9 15.1 %shard_map.262 = bf16[8,2,192,1536]{3,2,1,0:T(8,128)(2,1)} custom-call(s32[1]{0:T(128)} %bitcast.18.refs_0_, bf16[5,4,224,384]{3,2,1,0:T(8,128)(2,1)S(1)} %copy-done.2, bf16[5,224,1536]{2,1,0:T(8,128)(2,1)} %get-tuple-element.58.refs_2_, bf16[5,4,224,384]{3,2,1,0:T(8,128)(2,1)} %get-tuple-element.54.refs_3_, bf16[5,224,1536]{2,1,0:T(8,128)(2,1)} %get-tuple-element.59.refs_4_), custom_call_target="tpu_custom_call" | custom-call | flops 8455716864 | bytes 23199744 | tf_op jit(solution)/shard_map/pallas_call | solution.py:1641
  256.0 33.9 %back.1 = (bf16[3,5,224,384]{3,2,1,0:T(8,128)(2,1)}, f32[5,224,384]{2,1,0:T(8,128)}, f32[5,384]{1,0:T(8,128)}) custom-call(bf16[3,5,224,384]{3,2,1,0:T(8,128)(2,1)} %get-tuple-element.52.refs_0_, bf16[5,224,384]{2,1,0:T(8,128)(2,1)} %get-tuple-element.53.refs_0_.refs_1_.refs_4_, bf16[5,224,384]{2,1,0:T(8,128)(2,1)} %get-tuple-element.60.refs_2_, ...), custom_call_target="tpu_custom_call" | custom-call | flops 30000001024 | bytes 16425984 | tf_op jit(solution)/shard_map/back/pallas_call | solution.py:1445
  290.0 1.7 copy-done
  291.7 9.3 %shard_map.263 = bf16[8,4,192,384]{3,2,1,0:T(8,128)(2,1)} custom-call(s32[1]{0:T(128)} %bitcast.18.refs_0_, bf16[5,4,224,384]{3,2,1,0:T(8,128)(2,1)} %get-tuple-element.65.refs_1_, bf16[3,5,224,384]{3,2,1,0:T(8,128)(2,1)S(1)} %copy-done, bf16[5,4,224,384]{3,2,1,0:T(8,128)(2,1)} %get-tuple-element.67.refs_3_, bf16[5,224,384]{2,1,0:T(8,128)(2,1)S(1)} %copy-done.1), custom_call_target="tpu_custom_call" | custom-call | flops 4227858432 | bytes 15040512 | tf_op jit(solution)/shard_map/pallas_call | solution.py:1641
  301.1 0.7 reduce-scatter.5.cloned.1.call-update
  302.2 0.4 copy-done.9
  302.6 0.9 copy-done.10
  303.5 57.1 %last.1 = (f32[5,224,384]{2,1,0:T(8,128)S(1)}, f32[5,2,384]{2,1,0:T(2,128)S(1)}, f32[5,3,384]{2,1,0:T(4,128)S(1)}, bf16[4,3,160,384]{3,2,1,0:T(8,128)(2,1)S(1)}) custom-call(bf16[3,5,224,384]{3,2,1,0:T(8,128)(2,1)} %get-tuple-element.68.refs_2_.refs_0_, f32[5,224,384]{2,1,0:T(8,128)S(1)} %copy-done.9, bf16[5,4,224,384]{3,2,1,0:T(8,128)(2,1)} %get-tuple-element.70.refs_2_, ...), custom_call_target="tpu_custom_call" | custom-call | flops 15000000512 | bytes 18126336 | tf_op jit(solution)/shard_map/last/pallas_call | solution.py:1575
  360.6 1.1 copy-done.5
  362.2 12.8 %rows.1 = (f32[8,32,384]{2,1,0:T(8,128)S(1)}, f32[32,384]{1,0:T(8,128)S(1)}) custom-call(f32[32,384]{1,0:T(8,128)S(1)} %concatenate.11.row_ref), custom_call_target="tpu_custom_call" | custom-call | flops 1000000 | bytes 491520 | tf_op jit(solution)/shard_map/rows/pallas_call | solution.py:1765
  375.0 2.0 convolution_bitcast_fusion
  377.0 1.9 collective-permute-start.2
  378.9 0.5 collective-permute-start.1
  379.5 1.1 collective-permute-start
  380.6 2.1 copy-done.3
  382.7 1.4 copy-done.6
  384.0 6.3 %dw_text.1 = (f32[4,192,384]{2,1,0:T(8,128)S(1)}, f32[2,192,1536]{2,1,0:T(8,128)S(1)}) custom-call(bf16[4,160,384]{2,1,0:T(8,128)(2,1)S(1)} %copy-done.7, bf16[3,4,160,384]{3,2,1,0:T(8,128)(2,1)S(1)} %copy-done.4, bf16[4,3,160,384]{3,2,1,0:T(8,128)(2,1)S(1)} %copy-done.6, bf16[4,2,160,1536]{3,2,1,0:T(8,128)(2,1)S(1)} %copy-done.3, ...), custom_call_target="tpu_custom_call" | custom-call | flops 6000000000 | bytes 11403264 | tf_op jit(solution)/shard_map/dw_text/pallas_call | solution.py:1711
  390.4 1.0 slice_bitcast_fusion.2
  391.4 2.5 fusion
  393.8 1.2 fusion.14
  395.0 0.6 slice_bitcast_fusion.4
  395.6 1.2 slice.121
  396.8 1.2 slice.119
  398.0 0.9 copy.61
  399.0 0.9 copy.60
  399.9 0.6 reshape.84
  400.5 0.6 copy.62
  401.1 0.6 copy.63
  401.8 0.6 fusion.9
  402.4 1.1 slice.163
  403.7 0.9 maximum_bitcast_fusion.3
  404.6 0.4 copy-done.13
  405.0 1.3 maximum_bitcast_fusion.2
  406.3 75.2 %reduce-scatter.5.cloned.1.call-done = bf16[1,2,192,1536]{3,2,1,0:T(8,128)(2,1)} async-done(((bf16[8,2,192,1536]{3,2,1,0:T(8,128)(2,1)}), bf16[1,2,192,1536]{3,2,1,0:T(8,128)(2,1)}) %reduce-scatter.5.cloned.1.call-update) | async-done | bytes 1179664 | tf_op jit(solution)/shard_map/reduce_scatter | solution.py:1834
  481.5 1.5 convert_element_type.31
  483.3 1.1 copy-done.11
  484.4 1.6 maximum_bitcast_fusion.1
  485.9 1.6 maximum_bitcast_fusion
  (83 shorter events, 1.1 us)
Async XLA Ops:
  7.2 395.2 %reduce-scatter.3.cloned.1.call-start = ((), (), s32[]{:S(2)}) async-start(), calls=%async_computation.2 | async-start | bytes 5308416 | tf_op jit(solution)/shard_map/reduce_scatter | solution.py:1840
  238.9 2.0 copy-start.2
  256.0 34.0 %copy-start.1 = (bf16[5,224,384]{2,1,0:T(8,128)(2,1)S(1)}, bf16[5,224,384]{2,1,0:T(8,128)(2,1)}, u32[]{:S(2)}) copy-start(bf16[5,224,384]{2,1,0:T(8,128)(2,1)} %get-tuple-element.53.refs_0_.refs_1_.refs_4_) | copy-start | bytes 2580484
  289.9 1.7 copy-start
  301.0 0.8 copy-start.15
  301.0 0.9 copy-start.19
  301.0 1.0 copy-start.17
  301.1 1.1 copy-start.18
  301.1 1.5 copy-start.9
  301.1 180.5 %reduce-scatter.5.cloned.1.call-start = ((), (), s32[]{:S(2)}) async-start(), calls=%async_computation.3 | async-start | bytes 10616832 | tf_op jit(solution)/shard_map/reduce_scatter | solution.py:1834
  302.6 0.9 copy-start.10
  360.6 1.1 copy-start.5
  361.7 18.8 %copy-start.4 = (bf16[3,4,160,384]{3,2,1,0:T(8,128)(2,1)S(1)}, bf16[3,4,160,384]{3,2,1,0:T(8,128)(2,1)}, u32[]{:S(2)}) copy-start(bf16[3,4,160,384]{3,2,1,0:T(8,128)(2,1)} %get-tuple-element.82.refs_1_) | copy-start | bytes 4423684
  362.1 18.4 %copy-start.7 = (bf16[4,160,384]{2,1,0:T(8,128)(2,1)S(1)}, bf16[4,160,384]{2,1,0:T(8,128)(2,1)}, u32[]{:S(2)}) copy-start(bf16[4,160,384]{2,1,0:T(8,128)(2,1)} %get-tuple-element.81.refs_0_) | copy-start | bytes 1474564
  362.1 18.4 %copy-start.8 = (bf16[4,160,384]{2,1,0:T(8,128)(2,1)S(1)}, bf16[4,160,384]{2,1,0:T(8,128)(2,1)}, u32[]{:S(2)}) copy-start(bf16[4,160,384]{2,1,0:T(8,128)(2,1)} %get-tuple-element.85.refs_4_) | copy-start | bytes 1474564
  377.0 24.7 %collective-permute-start.2 = (f32[8,192]{1,0:T(8,128)S(1)}, f32[8,192]{1,0:T(8,128)S(1)}, u32[]{:S(2)}, u32[]{:S(2)}) collective-permute-start(f32[8,192]{1,0:T(8,128)S(1)} %convolution_bitcast_fusion), channel_id=1, source_target_pairs={{0,3},{1,2},{2,1},{3,0},{4,7},{5,6},{6,5},{7,4},{8,11},{9,10},{10,... | collective-permute-start | bytes 18440 | tf_op jit(solution)/shard_map/ppermute | solution.py:1866
  378.9 22.8 %collective-permute-start.1 = (f32[8,192]{1,0:T(8,128)S(1)}, f32[8,192]{1,0:T(8,128)S(1)}, u32[]{:S(2)}, u32[]{:S(2)}) collective-permute-start(f32[8,192]{1,0:T(8,128)S(1)} %convolution_bitcast_fusion), channel_id=1, source_target_pairs={{0,2},{1,3},{2,0},{3,1},{4,6},{5,7},{6,4},{7,5},{8,10},{9,11},{10,... | collective-permute-start | bytes 18440 | tf_op jit(solution)/shard_map/ppermute | solution.py:1866
  379.5 22.3 %collective-permute-start = (f32[8,192]{1,0:T(8,128)S(1)}, f32[8,192]{1,0:T(8,128)S(1)}, u32[]{:S(2)}, u32[]{:S(2)}) collective-permute-start(f32[8,192]{1,0:T(8,128)S(1)} %convolution_bitcast_fusion), channel_id=1, source_target_pairs={{0,1},{1,0},{2,3},{3,2},{4,5},{5,4},{6,7},{7,6},{8,9},{9,8},{10,11... | collective-permute-start | bytes 18440 | tf_op jit(solution)/shard_map/ppermute | solution.py:1866
  380.5 2.1 copy-start.3
  382.7 1.4 copy-start.6
  390.4 1.0 copy-start.16
  395.0 1.8 copy-start.14
  402.4 1.2 copy-start.12
  403.6 1.4 copy-start.13
  483.1 1.3 copy-start.11
Sparse Core Ops, SparseCore 0:
  301.1 76.7 reduce-scatter.2
  380.2 101.2 reduce-scatter.4
